TPU v7x, 32 devices: a whole 2x2x4 slice. The times are simulated.
32 devices in a mesh: model: 4 (over z), data: 8 (over y, x, core).
Axes of the slice: x: 2, y: 2, z: 4, core: 2. Of those that a mesh axis runs over, the one named last changes fastest.
Arguments:
- x_in: bfloat16 [8, 2048, 1024], P('data')
- cot_out: bfloat16 [8, 2048, 1024], P('data')
- step_emb: bfloat16 [2, 1024], replicated
- w_q: bfloat16 [1024, 1024], P(None, 'model')
- w_k: bfloat16 [1024, 1024], P(None, 'model')
- w_v: bfloat16 [1024, 1024], P(None, 'model')
- w_o: bfloat16 [1024, 1024], P('model')
- w_1: bfloat16 [1024, 4096], P(None, 'model')
- w_2: bfloat16 [4096, 1024], P('model')
Outputs:
- output 1: float32 [1024, 1024], P(None, 'model')
- output 2: float32 [1024, 1024], P(None, 'model')
- output 3: float32 [1024, 1024], P(None, 'model')
- output 4: float32 [1024, 1024], P('model')
- output 5: float32 [1024, 4096], P(None, 'model')
- output 6: float32 [4096, 1024], P('model')
- output 7: bfloat16 [8, 2048, 1024], P('data')
All inputs are finite; a program needn't handle non-finite values.
Results may differ from a plain program's by a relative error of at most 0.0150261.
Values are sent between devices in bfloat16 or wider.
A program may use at most 1 GiB of HBM per device.

v0:
```python
import functools
import math

import jax
import jax.numpy as jnp
from jax import lax
from jax.experimental import pallas as pl
from jax.experimental.pallas import tpu as pltpu
from jax.sharding import PartitionSpec as P


HEAD_DIM = 64
EPS_NORM = 1e-6
SCALE = HEAD_DIM ** -0.5
EXP2_SCALE = SCALE * math.log2(math.e)
PAIR = 2 * HEAD_DIM
FWD_ROWS = 512
BWD_ROWS = 256
KEYS = 256
INTERPRET = False
AXES = ('model', 'data')
BF16 = jnp.bfloat16
F32 = jnp.float32
MESH = pl.DeviceIdType.MESH


def rms_norm(values):
    return values * lax.rsqrt(jnp.mean(values * values, axis=-1, keepdims=True) + EPS_NORM)


def dot_nt(a, b):
    return lax.dot_general(a, b, (((1,), (1,)), ((), ())), preferred_element_type=F32)


def dot_nn(a, b):
    return lax.dot_general(a, b, (((1,), (0,)), ((), ())), preferred_element_type=F32)


def dot_tn(a, b):
    return lax.dot_general(a, b, (((0,), (0,)), ((), ())), preferred_element_type=F32)


def attn_fwd_kernel(q_ref, k_ref, v_ref, o_ref, lse_ref, vt_ref, *e_refs):
    @pl.when(pl.program_id(0) == 0)
    def _():
        vt_ref[...] = v_ref[...].T

    outs, sums = attend_rows(q_ref[...], k_ref, vt_ref, e_refs)
    o_ref[...] = jnp.concatenate(outs, axis=0).T.astype(BF16)
    for head in range(2):
        lse_ref[head:head + 1, :] = sums[head]


def attn_fwd(qkv, pair):
    seq = qkv.shape[0]
    rows = min(FWD_ROWS, seq)
    return pl.pallas_call(
        attn_fwd_kernel,
        grid=(seq // rows,),
        in_specs=[
            pl.BlockSpec((rows, PAIR), lambda i: (i, pair)),
            pl.BlockSpec((seq, PAIR), lambda i: (0, 2 + pair)),
            pl.BlockSpec((seq, PAIR), lambda i: (0, 4 + pair)),
        ],
        out_specs=[
            pl.BlockSpec((rows, PAIR), lambda i: (i, 0)),
            pl.BlockSpec((2, rows), lambda i: (0, i)),
        ],
        out_shape=[jax.ShapeDtypeStruct((seq, PAIR), BF16), jax.ShapeDtypeStruct((2, seq), F32)],
        scratch_shapes=[pltpu.VMEM((PAIR, seq), BF16)] + [pltpu.VMEM((seq, rows), F32)] * 2,
        compiler_params=pltpu.CompilerParams(vmem_limit_bytes=60 << 20),
        cost_estimate=pl.CostEstimate(
            flops=16 * seq * seq * PAIR, bytes_accessed=8 * seq * PAIR, transcendentals=seq * seq * 2),
        interpret=INTERPRET,
        name="attn_fwd",
    )(qkv, qkv, qkv)


def attn_bwd_kernel(q_ref, k_ref, v_ref, do_ref, lse_ref, out_ref, kt_ref, dk_acc, dv_acc, p_cat, ds_cat):
    step = pl.program_id(0)

    @pl.when(step == 0)
    def _():
        kt_ref[...] = k_ref[...].T
        dk_acc[...] = jnp.zeros_like(dk_acc)
        dv_acc[...] = jnp.zeros_like(dv_acc)

    block = q_ref.shape[0]
    out_ref[pl.ds(pl.multiple_of(step * block, block), block), :PAIR] = backward_rows(
        q_ref[...], do_ref[...], lse_ref[...], k_ref, v_ref, kt_ref, p_cat, ds_cat, dk_acc, dv_acc)

    @pl.when(step == pl.num_programs(0) - 1)
    def _():
        out_ref[:, PAIR:2 * PAIR] = (dk_acc[...] * SCALE).astype(BF16)
        out_ref[:, 2 * PAIR:] = dv_acc[...].astype(BF16)


def attn_bwd(qkv, d_context, lse, pair):
    seq = qkv.shape[0]
    full = lambda column: pl.BlockSpec((seq, PAIR), lambda i: (0, column))
    rows = lambda column: pl.BlockSpec((BWD_ROWS, PAIR), lambda i: (i, column))
    return pl.pallas_call(
        attn_bwd_kernel,
        grid=(seq // BWD_ROWS,),
        in_specs=[rows(pair), full(2 + pair), full(4 + pair), rows(0), pl.BlockSpec((2, BWD_ROWS), lambda i: (0, i))],
        out_specs=pl.BlockSpec((seq, 3 * PAIR), lambda i: (0, 0)),
        out_shape=jax.ShapeDtypeStruct((seq, 3 * PAIR), BF16),
        scratch_shapes=[
            pltpu.VMEM((PAIR, seq), BF16),
            pltpu.VMEM((seq, PAIR), F32),
            pltpu.VMEM((seq, PAIR), F32),
            pltpu.VMEM((seq, 2 * BWD_ROWS), BF16),
            pltpu.VMEM((seq, 2 * BWD_ROWS), BF16),
        ],
        compiler_params=pltpu.CompilerParams(vmem_limit_bytes=60 << 20),
        cost_estimate=pl.CostEstimate(
            flops=40 * seq * seq * PAIR, bytes_accessed=14 * seq * PAIR, transcendentals=seq * seq * 2),
        interpret=INTERPRET,
        name="attn_bwd",
    )(qkv, qkv, qkv, d_context, lse)


def attend_rows(q, k_ref, v_t, e_refs):
    count = k_ref.shape[0] // KEYS
    lane = lax.broadcasted_iota(jnp.int32, q.shape, 1)
    q_heads = [jnp.where(lane // HEAD_DIM == head, q, jnp.zeros_like(q)) for head in range(2)]
    tops, run, total, outs, sums = [[], []], [None, None], [None, None], [], []
    for j in range(count):
        keys = slice(j * KEYS, (j + 1) * KEYS)
        for head in range(2):
            scores = dot_nt(k_ref[keys, :], q_heads[head])
            top = jnp.max(scores, axis=0, keepdims=True) * EXP2_SCALE
            if j:
                top = jnp.maximum(top, run[head])
            weights = jnp.exp2(scores * EXP2_SCALE - top)
            part = jnp.sum(weights, axis=0, keepdims=True)
            total[head] = total[head] * jnp.exp2(run[head] - top) + part if j else part
            run[head] = top
            tops[head].append(top)
            e_refs[head][keys, :] = weights
    for head in range(2):
        inverse = 1.0 / total[head]
        out = None
        for j in range(count):
            keys = slice(j * KEYS, (j + 1) * KEYS)
            factor = inverse * jnp.exp2(tops[head][j] - run[head])
            probs = (e_refs[head][keys, :] * factor).astype(BF16)
            part = dot_nn(v_t[head * HEAD_DIM:(head + 1) * HEAD_DIM, keys], probs)
            out = out + part if j else part
        sums.append(run[head] + jnp.log2(total[head]))
        outs.append(out)
    return outs, sums


class Place:
    def __init__(self):
        self.z = lax.axis_index('model')
        d = lax.axis_index('data')
        self.y, self.x, self.c = d // 4, d // 2 % 2, d % 2
        z = self.z
        self.z_by = {1: z + 1 - 2 * (z % 2), 2: (z + 2) % 4, 3: 3 - z}
        x, y, c = self.x, self.y, self.c
        self.xa, self.ya = x + (1 - c) * (1 - 2 * x), y + c * (1 - 2 * y)
        self.xb, self.yb = x + c * (1 - 2 * x), y + (1 - c) * (1 - 2 * y)
        self.role = z % 2 * 2 + c
        self.owner = c == z // 2

    def piece(self, y, x, c=None):
        return y * 4 + x * 2 + (self.c if c is None else c)

    def device(self, z=None, y=None, x=None, c=None):
        z, y, x, c = (own if given is None else given for given, own in zip((z, y, x, c), (self.z, self.y, self.x, self.c)))
        return {'model': z, 'data': y * 4 + x * 2 + c}

    def peers(self):
        column = [self.device(z=z, c=c) for z in (self.z, *self.z_by.values()) for c in (self.c, 1 - self.c)][1:]
        return column + [self.device(x=1 - self.x), self.device(y=1 - self.y)]

    def meet(self):
        barrier = pltpu.get_barrier_semaphore()
        peers = self.peers()
        for peer in peers:
            pl.semaphore_signal(barrier, inc=1, device_id=peer, device_id_type=MESH)
        pl.semaphore_wait(barrier, len(peers))


class Copies:
    def __init__(self, send_sem, recv_sem):
        self.send_sem, self.recv_sem, self.used, self.sent = send_sem, recv_sem, 0, []

    def make(self, src, dst, device):
        n, self.used = self.used, self.used + 1
        copy = pltpu.make_async_remote_copy(
            src_ref=src, dst_ref=dst, send_sem=self.send_sem.at[n], recv_sem=self.recv_sem.at[n],
            device_id=device, device_id_type=MESH)
        self.sent.append(copy)
        return copy

    def start(self, src, dst, device):
        copy = self.make(src, dst, device)
        copy.start()
        return copy


def first_kernel(x_ref, cot_ref, emb_ref, wq_ref, wk_ref, wv_ref, wo_ref, w1_ref, w2_ref,
                 c1_ref, lse_ref, xs_ref, cot_loc_ref, full_o, full_1, full_2, full_qkv,
                 qkv_s, vt_s, e_a, e_b, c_buf, lse_s, cot_s, local_sem, send_sem, recv_sem, c_send, c_recv, one_send, one_recv):
    seq, d_model = x_ref.shape
    blk = seq // 4
    head_cols = wq_ref.shape[1]
    here = Place()
    z, core, role, owner = here.z, here.c, here.role, here.owner
    here.meet()
    copies = Copies(send_sem, recv_sem)

    def span(index, count):
        return pl.ds(pl.multiple_of(index * count, count), count)

    ff_cols, out_rows, piece = w1_ref.shape[1], wo_ref.shape[0] // 8, d_model // 8
    hidden = w2_ref.shape[0] // 8

    def block_qkv(zz, e):
        return full_qkv.at[span(e, piece), span(zz, 3 * head_cols)]

    units = {
        'o': lambda zz, e: full_o.at[zz, span(e, out_rows), :],
        '1': lambda zz, e: full_1.at[span(e, piece), span(zz, ff_cols)],
        '2': lambda zz, e: full_2.at[zz, span(e, hidden), :],
        'qkv': block_qkv,
    }

    def own_parts(name, e):
        if name == 'o':
            return [(wo_ref.at[span(e, out_rows), :], units[name](z, e))]
        if name == '1':
            return [(w1_ref.at[span(e, piece), :], units[name](z, e))]
        if name == '2':
            return [(w2_ref.at[span(e, hidden), :], units[name](z, e))]
        return [(ref.at[span(e, piece), :],
                 full_qkv.at[span(e, piece), pl.ds(pl.multiple_of((z * 3 + t) * head_cols, head_cols), head_cols)])
                for t, ref in enumerate((wq_ref, wk_ref, wv_ref))]

    mine = here.piece(here.y, here.x)
    by_a = here.piece(here.ya, here.xa)
    by_b = here.piece(here.yb, here.xb)
    by_ab = here.piece(1 - here.y, 1 - here.x)
    to_a, to_b = here.device(y=here.ya, x=here.xa), here.device(y=here.yb, x=here.xb)
    partner = here.device(c=1 - core)
    stage_z, stage_a, stage_b1, stage_b2, stage_c = {}, {}, {}, {}, {}
    names = ('o', '1', '2', 'qkv')

    for name in names:
        stage_z[name] = {k: [copies.start(src, dst, here.device(z=here.z_by[k])) for src, dst in own_parts(name, mine)]
                         for k in (1, 2, 3)}

    def forward_z(name):
        stage_a[name], stage_b1[name] = [], []
        for k in (1, 2, 3):
            for copy in stage_z[name][k]:
                copy.wait_recv()
            block = units[name](here.z_by[k], mine)
            stage_a[name].append(copies.start(block, block, to_a))
            stage_b1[name].append(copies.start(block, block, to_b))

    def forward_a(name):
        stage_b2[name] = []
        for k in (1, 2, 3):
            stage_a[name][k - 1].wait_recv()
            block = units[name](here.z_by[k], by_a)
            stage_b2[name].append(copies.start(block, block, to_b))

    def forward_b(name):
        stage_c[name] = []
        for k in (1, 2, 3):
            stage_b1[name][k - 1].wait_recv()
            stage_b2[name][k - 1].wait_recv()
            for e in (mine, by_a, by_b, by_ab):
                block = units[name](here.z_by[k], e)
                stage_c[name].append(copies.start(block, block, partner))

    locals_ = []

    def copy_local(src, dst):
        copy = pltpu.make_async_copy(src, dst, local_sem.at[len(locals_)])
        locals_.append(copy)
        copy.start()

    copy_local(w1_ref, full_1.at[:, span(z, ff_cols)])
    copy_local(w2_ref, full_2.at[z])
    copy_local(wo_ref, full_o.at[z])
    for t, ref in enumerate((wq_ref, wk_ref, wv_ref)):
        copy_local(ref, full_qkv.at[:, pl.ds(pl.multiple_of((z * 3 + t) * head_cols, head_cols), head_cols)])
    other_role = z % 2 * 2 + 1 - core
    give_x = pltpu.make_async_remote_copy(
        src_ref=x_ref, dst_ref=xs_ref, send_sem=one_send.at[0], recv_sem=one_recv.at[0], device_id=partner, device_id_type=MESH)
    give_cot = pltpu.make_async_remote_copy(
        src_ref=cot_ref.at[span(other_role, blk), :], dst_ref=cot_loc_ref, send_sem=one_send.at[1], recv_sem=one_recv.at[1],
        device_id=partner, device_id_type=MESH)
    keep_x = pltpu.make_async_copy(x_ref, xs_ref, local_sem.at[6])
    take_cot = pltpu.make_async_copy(cot_ref.at[span(role, blk), :], cot_s, local_sem.at[7])
    keep_cot = pltpu.make_async_copy(cot_s, cot_loc_ref, local_sem.at[8])

    @pl.when(owner)
    def _():
        give_x.start()
        give_cot.start()
        keep_x.start()
        take_cot.start()

    def project(i, _):
        rows = span(i, blk)
        values = x_ref[rows, :].astype(F32) + emb_ref[...]
        unit = (values * lax.rsqrt(jnp.mean(values * values, axis=-1, keepdims=True) + EPS_NORM)).astype(BF16)
        for t, ref in enumerate((wq_ref, wk_ref, wv_ref)):
            qkv_s[rows, t * head_cols:(t + 1) * head_cols] = dot_nn(unit, ref[...]).astype(BF16)
        return 0

    lax.fori_loop(0, 4, project, 0)

    def context_copy(j, i):
        src = c_buf.at[j, span(i, blk), :]
        dst = c1_ref.at[:, pl.ds(pl.multiple_of((z * 2 + j) * PAIR, PAIR), PAIR)]
        target_z, target_c = 2 * core + i // 2, i % 2
        remote = pltpu.make_async_remote_copy(
            src_ref=src, dst_ref=dst, send_sem=c_send.at[j * 4 + i], recv_sem=c_recv.at[j * 4 + z],
            device_id=here.device(z=target_z, c=target_c), device_id_type=MESH)
        local = pltpu.make_async_copy(src, dst, c_recv.at[j * 4 + z])
        return remote, local, jnp.logical_and(target_z == z, target_c == core)

    def send_context(j, i):
        remote, local, to_self = context_copy(j, i)
        pl.when(to_self)(local.start)
        pl.when(jnp.logical_not(to_self))(remote.start)

    moves = {(0, 1): [(forward_z, 'o')], (0, 2): [(forward_a, 'o')], (0, 3): [(forward_b, 'o')],
             (1, 2): [(forward_z, '1')], (1, 3): [(forward_a, '1')]}
    for j in range(2):
        vt_s[...] = qkv_s[:, (4 + j) * PAIR:(5 + j) * PAIR].T
        k_view = qkv_s.at[:, (2 + j) * PAIR:(3 + j) * PAIR]
        for i in range(4):
            if i or j:
                send_context(j if i else 0, i - 1 if i else 3)
            for step, name in moves.get((j, i), ()):
                step(name)
            rows = slice(i * blk, (i + 1) * blk)
            outs, sums = attend_rows(qkv_s[rows, j * PAIR:(j + 1) * PAIR], k_view, vt_s, (e_a, e_b))
            c_buf[j, rows, :] = jnp.concatenate(outs, axis=0).T.astype(BF16)
            for head in range(2):
                lse_s[2 * j + head:2 * j + head + 1, rows] = sums[head]

    @pl.when(owner)
    def _():
        take_cot.wait()
        keep_cot.start()

    forward_z('2')
    send_context(1, 3)
    give_lse = pltpu.make_async_remote_copy(
        src_ref=lse_s, dst_ref=lse_ref, send_sem=one_send.at[2], recv_sem=one_recv.at[2],
        device_id=here.device(z=2 * core + z // 2, c=z % 2), device_id_type=MESH)
    keep_lse = pltpu.make_async_copy(lse_s, lse_ref, local_sem.at[9])
    lse_stays = jnp.logical_and(2 * core + z // 2 == z, z % 2 == core)
    pl.when(lse_stays)(keep_lse.start)
    pl.when(jnp.logical_not(lse_stays))(give_lse.start)
    forward_b('1')
    forward_a('2')
    forward_z('qkv')
    forward_b('2')
    forward_a('qkv')
    forward_b('qkv')

    for j in range(2):
        for zz in range(4):
            pltpu.make_async_copy(c_buf.at[j, :blk, :], c1_ref.at[:, :PAIR], c_recv.at[j * 4 + zz]).wait()
        for i in range(4):
            remote, _, to_self = context_copy(j, i)
            pl.when(jnp.logical_not(to_self))(remote.wait_send)
    pl.when(lse_stays)(keep_lse.wait)

    @pl.when(jnp.logical_not(lse_stays))
    def _():
        give_lse.wait_send()
        give_lse.wait_recv()

    @pl.when(owner)
    def _():
        give_x.wait_send()
        give_cot.wait_send()
        keep_x.wait()
        keep_cot.wait()

    @pl.when(jnp.logical_not(owner))
    def _():
        give_x.wait_recv()
        give_cot.wait_recv()

    for copy in locals_:
        copy.wait()
    for name in names:
        for copy in stage_c[name]:
            copy.wait_recv()
    for copy in copies.sent:
        copy.wait_send()


def first_call(x, cot, emb, w_q, w_k, w_v, w_o, w_1, w_2):
    seq, d_model = x.shape
    head_cols, ff_cols, blk = w_q.shape[1], w_1.shape[1], seq // 4
    anywhere = pl.BlockSpec(memory_space=pl.ANY)
    in_vmem = pl.BlockSpec(memory_space=pltpu.VMEM)
    copies = 18 + 12 + 24 + 48
    return pl.pallas_call(
        first_kernel,
        in_specs=[in_vmem, anywhere] + [in_vmem] * 7,
        out_specs=[anywhere] * 8,
        out_shape=[
            jax.ShapeDtypeStruct((blk, d_model), BF16),
            jax.ShapeDtypeStruct((4, seq), F32),
            jax.ShapeDtypeStruct((seq, d_model), BF16),
            jax.ShapeDtypeStruct((blk, d_model), BF16),
            jax.ShapeDtypeStruct((4, *w_o.shape), BF16),
            jax.ShapeDtypeStruct((d_model, 4 * ff_cols), BF16),
            jax.ShapeDtypeStruct((4, *w_2.shape), BF16),
            jax.ShapeDtypeStruct((d_model, 12 * head_cols), BF16),
        ],
        scratch_shapes=[
            pltpu.VMEM((seq, 3 * head_cols), BF16),
            pltpu.VMEM((PAIR, seq), BF16),
            pltpu.VMEM((seq, blk), F32),
            pltpu.VMEM((seq, blk), F32),
            pltpu.VMEM((2, seq, PAIR), BF16),
            pltpu.VMEM((4, seq), F32),
            pltpu.VMEM((blk, d_model), BF16),
            pltpu.SemaphoreType.DMA((10,)),
            pltpu.SemaphoreType.DMA((copies,)),
            pltpu.SemaphoreType.DMA((copies,)),
            pltpu.SemaphoreType.DMA((8,)),
            pltpu.SemaphoreType.DMA((8,)),
            pltpu.SemaphoreType.DMA((3,)),
            pltpu.SemaphoreType.DMA((3,)),
        ],
        compiler_params=pltpu.CompilerParams(vmem_limit_bytes=60 << 20, collective_id=0, has_side_effects=True),
        cost_estimate=pl.CostEstimate(
            flops=64 * seq * seq * PAIR, bytes_accessed=64 * seq * d_model, transcendentals=seq * seq * 4),
        name="first",
    )(x, cot, emb, w_q, w_k, w_v, w_o, w_1, w_2)


def grad_kernel(by_left, _, *refs):
    lefts, rights, (away_ref, mid_ref, keep_ref, left_t, right_s) = refs[:16], refs[16:20], refs[20:]
    count, piece = lefts[0].shape
    step = pl.program_id(0)

    @pl.when(step == 0 if not by_left else step >= 0)
    def _():
        for i in range(16):
            left_t[i % 4 * piece:(i % 4 + 1) * piece, i // 4 * count:(i // 4 + 1) * count] = lefts[i][...].T

    @pl.when(step == 0 if by_left else step >= 0)
    def _():
        for i in range(4):
            right_s[i * count:(i + 1) * count, :] = rights[i][...]

    total = dot_nn(left_t[...], right_s[...])
    away_ref[0] = total[:2 * piece]
    mid_ref[0] = total[2 * piece:3 * piece]
    keep_ref[0] = total[3 * piece:]


def grad_products(order, lefts, rights, by_left=False):
    count = rights[0].shape[0]
    tile = rights[0].shape[1] // (1 if by_left else 4)
    piece = lefts[0].shape[1] // (32 if by_left else 8)
    if by_left:
        left_spec = lambda n: pl.BlockSpec((count, piece), lambda i, order: (0, i * 8 + order[n]))
        right_spec = pl.BlockSpec((count, tile), lambda i, order: (0, 0))
    else:
        left_spec = lambda n: pl.BlockSpec((count, piece), lambda i, order: (0, order[n]))
        right_spec = pl.BlockSpec((count, tile), lambda i, order: (0, i))
    return pl.pallas_call(
        functools.partial(grad_kernel, by_left),
        grid_spec=pltpu.PrefetchScalarGridSpec(
            num_scalar_prefetch=1,
            grid=(4,),
            in_specs=[left_spec(n) for _ in range(4) for n in range(4)] + [right_spec] * 4,
            out_specs=[pl.BlockSpec((1, n * piece, tile), lambda i, order: (i, 0, 0)) for n in (2, 1, 1)],
            scratch_shapes=[pltpu.VMEM((4 * piece, 4 * count), BF16), pltpu.VMEM((4 * count, tile), BF16)],
        ),
        out_shape=[jax.ShapeDtypeStruct((4, n * piece, tile), F32) for n in (2, 1, 1)],
        compiler_params=pltpu.CompilerParams(vmem_limit_bytes=60 << 20),
        cost_estimate=pl.CostEstimate(
            flops=128 * count * piece * tile, bytes_accessed=8 * count * (4 * piece + 4 * tile) + 64 * piece * tile,
            transcendentals=0),
        interpret=INTERPRET,
        name="grad",
    )(order, *[left for left in lefts for _ in range(4)], *rights)


def backward_rows(q, d_out, lse, k_ref, v_ref, k_t, p_cat, ds_cat, dk_acc, dv_acc):
    block = q.shape[0]
    lane = lax.broadcasted_iota(jnp.int32, q.shape, 1)
    q_heads, do_heads, dqs = [], [], []
    for head in range(2):
        mine = lane // HEAD_DIM == head
        q_head = jnp.where(mine, q, jnp.zeros_like(q))
        do_head = jnp.where(mine, d_out, jnp.zeros_like(d_out))
        scores = dot_nt(k_ref[...], q_head)
        probs = jnp.exp2(scores * EXP2_SCALE - lse[head:head + 1, :])
        d_probs = dot_nt(v_ref[...], do_head).astype(BF16).astype(F32)
        inner = jnp.sum(probs * d_probs, axis=0, keepdims=True)
        cols = slice(head * block, (head + 1) * block)
        p_cat[:, cols] = probs.astype(BF16)
        ds_cat[:, cols] = (probs * (d_probs - inner)).astype(BF16)
        dqs.append(dot_nn(k_t[head * HEAD_DIM:(head + 1) * HEAD_DIM, :], ds_cat[:, cols]))
        q_heads.append(q_head)
        do_heads.append(do_head)
    dv_acc[...] += dot_nn(p_cat[...], jnp.concatenate(do_heads, axis=0))
    dk_acc[...] += dot_nn(ds_cat[...], jnp.concatenate(q_heads, axis=0))
    return (jnp.concatenate(dqs, axis=0).T * SCALE).astype(BF16)


def last_kernel(qkv_ref, dc_ref, lse_ref, dmid_ref, x_ref, emb_ref, wqkv_ref, u_ref, gqkv2_ref,
                r2_ref, mid2_ref, keep2_ref, away1_ref, mid1_ref, keep1_ref, awayo_ref, mido_ref, keepo_ref,
                dx_ref, g1_ref, g2_ref, go_ref, gq_ref, gk_ref, gv_ref,
                dch, k_t, dk_acc, dv_acc, p_cat, ds_cat, d_heads, d_qkv, buf, buf_o, second, second_o, tmp, tmp_o,
                third, third_o, sum_1, sum_2, sum_o, qa, qb, q1, q2, q3, q4, d_1, w_s, u_s, g_s,
                local_sem, load_sem, send_sem, recv_sem, dc_send, dc_recv, dq_send, dq_recv, z_send, z_recv, x_send, x_recv,
                p_send, p_recv):
    seq = qkv_ref.shape[0]
    blk = seq // 4
    head_cols = 2 * PAIR
    here = Place()
    z, core, role, owner = here.z, here.c, here.role, here.owner
    here.meet()
    copies = Copies(send_sem, recv_sem)
    waits = []

    def span(index, count):
        return pl.ds(pl.multiple_of(index * count, count), count)

    def load(src, dst, n):
        copy = pltpu.make_async_copy(src, dst, load_sem.at[n])
        copy.start()
        return copy

    no = jnp.logical_not
    to_a, to_b = here.device(y=here.ya, x=here.xa), here.device(y=here.yb, x=here.xb)
    partner = here.device(c=1 - core)
    member = [here.device(z=z // 2 * 2 + i // 2, c=i % 2) for i in range(4)]
    piece = tmp.shape[1]

    def dc_copy(i):
        return pltpu.make_async_remote_copy(
            src_ref=dc_ref.at[:, i * head_cols:(i + 1) * head_cols], dst_ref=dch.at[span(role, blk), :],
            send_sem=dc_send.at[i], recv_sem=dc_recv.at[role], device_id=member[i], device_id_type=MESH)

    for i in range(4):
        pl.when(role != i)(dc_copy(i).start)

        @pl.when(role == i)
        def _():
            dch[i * blk:(i + 1) * blk, :] = dc_ref[:, i * head_cols:(i + 1) * head_cols]

    firsts = {('1', q): copies.start(away1_ref.at[q], buf.at[4 + q], to_a) for q in range(4)}
    firsts['o'] = copies.start(awayo_ref, buf_o, to_a)
    w2_loads = [load(r2_ref.at[q], buf.at[q], q) for q in range(4)]
    seconds = {(w, q): copies.make(buf.at[u + q, piece:, :], second.at[u + q], to_b) for w, u in (('2', 0), ('1', 4)) for q in range(4)}
    seconds['o'] = copies.make(buf_o.at[:, piece:, :], second_o, to_b)

    def add_mid(unit):
        if unit == 'o':
            mid, keep, t, n = mido_ref, keepo_ref, tmp_o, 4
            bottom, top = buf_o.at[:, piece:, :], buf_o.at[:, :piece, :]
        else:
            w, q = unit
            mid, keep = (mid2_ref.at[q], keep2_ref.at[q]) if w == '2' else (mid1_ref.at[q], keep1_ref.at[q])
            u = q if w == '2' else 4 + q
            t, n, bottom, top = tmp, 6, buf.at[u, piece:, :], buf.at[u, :piece, :]
        loads = [load(mid, t.at[0], n), load(keep, t.at[1], n + 1)]
        if unit == 'o' or unit[0] == '1':
            firsts[unit].wait_recv()
        else:
            w2_loads[unit[1]].wait()
        for copy in loads:
            copy.wait()
        bottom[...] += t[0]
        top[...] += t[1]
        seconds[unit].start()

    def z_copy(unit, q):
        if unit == 'o':
            src, dst, n = buf_o.at[q, :piece, :], third_o.at[z], 8
        else:
            w = 0 if unit == '2' else 1
            src, dst, n = buf.at[4 * w + q, :piece, :], third.at[w, z], 4 * w
        return pltpu.make_async_remote_copy(
            src_ref=src, dst_ref=dst, send_sem=z_send.at[n + q], recv_sem=z_recv.at[n + z],
            device_id=here.device(z=q), device_id_type=MESH)

    def finish(unit):
        seconds[unit].wait_recv()
        if unit == 'o':
            buf_o[:, :piece, :] += second_o[...]
            for q in range(4):
                pl.when(z != q)(z_copy('o', q).start)
        else:
            w, q = unit
            u = q if w == '2' else 4 + q
            buf[u, :piece, :] += second[u]
            pl.when(z != q)(z_copy(w, q).start)

    mine, by_a = here.piece(here.y, here.x), here.piece(here.ya, here.xa)
    by_b, by_ab = here.piece(here.yb, here.xb), here.piece(1 - here.y, 1 - here.x)
    gathers = {}

    def total(unit):
        out, got, n = {'2': (sum_2, third.at[0], 0), '1': (sum_1, third.at[1], 4), 'o': (sum_o, third_o, 8)}[unit]
        if unit == 'o':
            out[...] = buf_o[z, :piece, :]
        else:
            out[...] = buf[n + z, :piece, :]
        for zz in range(4):
            @pl.when(z != zz)
            def _():
                pltpu.make_async_copy(out, got.at[zz], z_recv.at[n + zz]).wait()
                out[...] += got[zz]

    def gather_start(name, src, out, n):
        rows = lambda e: out.at[span(e, piece), :]
        keep = pltpu.make_async_copy(src, rows(mine), local_sem.at[n])
        keep.start()
        waits.append(keep)
        gathers[name] = dict(src=src, rows=rows, a=copies.start(src, rows(mine), to_a), b1=copies.start(src, rows(mine), to_b))

    def gather_second(name):
        g = gathers[name]
        g['a'].wait_recv()
        g['b2'] = copies.start(g['rows'](by_a), g['rows'](by_a), to_b)

    def gather_core(name):
        g = gathers[name]
        g['c'] = [copies.start(g['src'], g['rows'](mine), partner), copies.start(g['rows'](by_a), g['rows'](by_a), partner)]
        g['b1'].wait_recv()
        g['c'].append(copies.start(g['rows'](by_b), g['rows'](by_b), partner))
        g['b2'].wait_recv()
        g['c'].append(copies.start(g['rows'](by_ab), g['rows'](by_ab), partner))

    def dq_copy(j, i, t):
        col = t * head_cols + j * PAIR
        return pltpu.make_async_remote_copy(
            src_ref=d_heads.at[i * blk:(i + 1) * blk, col:col + PAIR],
            dst_ref=d_qkv.at[:, pl.ds(pl.multiple_of(role * 3 * head_cols + col, PAIR), PAIR)],
            send_sem=dq_send.at[(j * 4 + i) * 3 + t], recv_sem=dq_recv.at[(j * 4 + role) * 3 + t],
            device_id=member[i], device_id_type=MESH)

    def send_d_heads(j):
        for i in range(4):
            @pl.when(role != i)
            def _():
                for t in range(3):
                    dq_copy(j, i, t).start()

    for i in range(4):
        @pl.when(role != i)
        def _():
            pltpu.make_async_copy(dc_ref.at[:, :head_cols], dch.at[:blk, :], dc_recv.at[i]).wait()

    moves = {(0, 0): [(add_mid, ('2', 0))], (0, 1): [(add_mid, ('2', 1))], (0, 2): [(add_mid, ('2', 2))],
             (0, 3): [(add_mid, ('2', 3))], (0, 5): [(add_mid, ('1', 0))], (0, 6): [(finish, ('2', 0))],
             (1, 0): [(send_d_heads, 0), (finish, ('2', 1))], (1, 1): [(add_mid, ('1', 1))], (1, 3): [(finish, ('2', 2))],
             (1, 4): [(add_mid, ('1', 2))], (1, 6): [(finish, ('2', 3))]}
    steps = seq // BWD_ROWS
    for j in range(2):
        k_view, v_view = qkv_ref.at[:, (2 + j) * PAIR:(3 + j) * PAIR], qkv_ref.at[:, (4 + j) * PAIR:(5 + j) * PAIR]
        k_t[...] = k_view[...].T
        dk_acc[...] = jnp.zeros_like(dk_acc)
        dv_acc[...] = jnp.zeros_like(dv_acc)

        def block(i, _):
            for n in range(8):
                if (j, n) in moves:
                    @pl.when(i == min(n, steps - 1))
                    def _():
                        for move, what in moves[(j, n)]:
                            move(what)
            rows = span(i, BWD_ROWS)
            cols = slice(j * PAIR, (j + 1) * PAIR)
            d_heads[rows, cols] = backward_rows(
                qkv_ref[rows, cols], dch[rows, cols], lse_ref[2 * j:2 * j + 2, rows], k_view, v_view,
                k_t, p_cat, ds_cat, dk_acc, dv_acc)
            return 0

        lax.fori_loop(0, steps, block, 0)
        d_heads[:, head_cols + j * PAIR:head_cols + (j + 1) * PAIR] = (dk_acc[...] * SCALE).astype(BF16)
        d_heads[:, 2 * head_cols + j * PAIR:2 * head_cols + (j + 1) * PAIR] = dv_acc[...].astype(BF16)

    quarter = 2 * piece
    index = [here.ya * 2 + here.xa, (1 - here.y) * 2 + 1 - here.x, here.yb * 2 + here.xb, here.y * 2 + here.x]

    def quarter_loads(n):
        return [load(u_ref.at[:, span(index[n], quarter)], u_s.at[n % 2], 8 + n % 2),
                load(gqkv2_ref.at[span(index[n], quarter), :], g_s.at[n % 2], 10 + n % 2)]

    pending = quarter_loads(0)
    for i in range(4):
        @pl.when(role == i)
        def _():
            d_qkv[:, i * 3 * head_cols:(i + 1) * 3 * head_cols] = d_heads[i * blk:(i + 1) * blk, :]
    send_d_heads(1)
    targets = [qa.at[0], qa.at[1], qb.at[0], qb.at[1]]
    first_q = None
    for n in range(4):
        ahead = quarter_loads(n + 1) if n < 3 else []
        for copy in pending:
            copy.wait()
        targets[n][...] = dot_tn(u_s[n % 2], d_heads[...]) + g_s[n % 2]
        pending = ahead
        if n == 2:
            first_q = copies.start(qa, q1, to_a)

    add_mid(('1', 3))
    finish(('1', 0))
    w_rows = w_s.shape[1]
    chunks = wqkv_ref.shape[0] // w_rows
    w_load = load(wqkv_ref.at[:w_rows, :], w_s.at[0], 12)
    for j in range(2):
        for i in range(4):
            @pl.when(role != i)
            def _():
                for t in range(3):
                    pltpu.make_async_copy(d_heads.at[:blk, :PAIR], d_qkv.at[:, :PAIR], dq_recv.at[(j * 4 + i) * 3 + t]).wait()
    for n in range(chunks):
        ahead = load(wqkv_ref.at[(n + 1) * w_rows:(n + 2) * w_rows, :], w_s.at[(n + 1) % 2], 12 + (n + 1) % 2) if n + 1 < chunks else None
        w_load.wait()
        d_1[:, n * w_rows:(n + 1) * w_rows] = dot_nt(d_qkv[...], w_s[n % 2]).astype(BF16)
        w_load = ahead

    count = min(128, blk)
    for n in range(blk // count):
        rows = slice(n * count, (n + 1) * count)
        values = x_ref[rows, :].astype(F32) + emb_ref[...]
        up = d_1[rows, :].astype(F32)
        inverse = lax.rsqrt(jnp.mean(values * values, axis=-1, keepdims=True) + EPS_NORM)
        inner = jnp.mean(values * up, axis=-1, keepdims=True)
        d_1[rows, :] = (dmid_ref[rows, :].astype(F32) + inverse * up - values * (inverse * inverse * inverse * inner)).astype(BF16)

    own_seq = z // 2
    rows_dx = span(role, blk)

    def dx_copy(n, device):
        slot = [0, 1 + core, 3 + core][n]
        return pltpu.make_async_remote_copy(
            src_ref=d_1, dst_ref=dx_ref.at[rows_dx, :], send_sem=x_send.at[n], recv_sem=x_recv.at[slot],
            device_id=device, device_id_type=MESH)

    dx_side = dx_copy(0, partner)
    dx_next = dx_copy(1, here.device(z=here.z_by[1], c=own_seq))
    dx_cross = dx_copy(2, here.device(z=here.z_by[2], c=own_seq))
    dx_keep = pltpu.make_async_copy(d_1, dx_ref.at[rows_dx, :], local_sem.at[8])

    def dx_pass(cc):
        rows = span(z % 2 * 2 + cc, blk)
        return pltpu.make_async_remote_copy(
            src_ref=dx_ref.at[rows, :], dst_ref=dx_ref.at[rows, :], send_sem=x_send.at[3 + cc], recv_sem=x_recv.at[5 + cc],
            device_id=here.device(z=here.z_by[1]), device_id_type=MESH)

    add_mid('o')
    dx_cross.start()
    dx_next.start()
    pl.when(owner)(dx_keep.start)
    pl.when(no(owner))(dx_side.start)

    def dx_got(slot):
        pltpu.make_async_copy(d_1, dx_ref.at[:blk, :], x_recv.at[slot]).wait()

    first_q.wait_recv()
    qb[0] += q1[1]
    qb[1] += q1[0]
    second_q = copies.start(qb.at[0], q2, to_b)
    finish(('1', 1))
    total('2')
    finish(('1', 2))
    gather_start('2', sum_2, g2_ref, 0)
    finish(('1', 3))
    finish('o')
    second_q.wait_recv()
    qb[1] += q2[...]
    plane_stays = jnp.logical_and(2 * (z % 2) + core == z, z // 2 == core)
    plane_q = pltpu.make_async_remote_copy(
        src_ref=qb.at[1], dst_ref=q3, send_sem=p_send.at[0], recv_sem=p_recv.at[0],
        device_id=here.device(z=2 * (z % 2) + core, c=z // 2), device_id_type=MESH)

    @pl.when(plane_stays)
    def _():
        q3[...] = qb[1]

    pl.when(no(plane_stays))(plane_q.start)
    gather_second('2')

    @pl.when(no(owner))
    def _():
        for cc in range(2):
            dx_got(3 + cc)
            dx_pass(cc).start()

    total('1')
    total('o')
    gather_start('1', sum_1, g1_ref, 1)
    gather_start('o', sum_o, go_ref, 2)
    gather_core('2')
    pl.when(no(plane_stays))(plane_q.wait_recv)
    give_q = copies.start(q3.at[span(1 - core, piece), :], q4.at[0], partner)
    gather_second('1')
    gather_second('o')
    give_q.wait_recv()
    q4[1] = q4[0] + q3[span(core, piece), :]
    for t, (name, out) in enumerate((('q', gq_ref), ('k', gk_ref), ('v', gv_ref))):
        gather_start(name, q4.at[1, :, t * head_cols:(t + 1) * head_cols], out, 3 + t)
    gather_core('1')
    gather_core('o')
    for name in 'qkv':
        gather_second(name)
    for name in 'qkv':
        gather_core(name)

    @pl.when(owner)
    def _():
        for slot in (0, 1, 2):
            dx_got(slot)
        dx_keep.wait()

    @pl.when(no(owner))
    def _():
        dx_side.wait_send()
        for cc in range(2):
            dx_got(5 + cc)
            dx_pass(cc).wait_send()

    for g in gathers.values():
        for copy in g['c']:
            copy.wait_recv()
    for copy in waits:
        copy.wait()
    for copy in copies.sent:
        copy.wait_send()
    dx_cross.wait_send()
    dx_next.wait_send()
    pl.when(no(plane_stays))(plane_q.wait_send)
    for i in range(4):
        @pl.when(role != i)
        def _():
            dc_copy(i).wait_send()
            for j in range(2):
                for t in range(3):
                    dq_copy(j, i, t).wait_send()

        for unit in '21o':
            pl.when(z != i)(z_copy(unit, i).wait_send)


def last_call(qkv, d_c, lse, d_mid, x, emb, w_qkv, u_seq, g_qkv, w2_parts, w1_parts, wo_parts):
    seq, d_model = u_seq.shape
    blk, piece = seq // 4, d_model // 8
    n1, no = w1_parts[0].shape[2], wo_parts[0].shape[2]
    assert w2_parts[0].shape[1:] == (2 * piece, n1)
    heads3 = qkv.shape[1]
    anywhere = pl.BlockSpec(memory_space=pl.ANY)
    in_vmem = pl.BlockSpec(memory_space=pltpu.VMEM)
    copies = 5 + 9 + 6 * 7 + 3
    dma = pltpu.SemaphoreType.DMA
    w_rows = min(256, d_model)
    return pl.pallas_call(
        last_kernel,
        in_specs=[in_vmem] * 6 + [anywhere] * 12,
        out_specs=[anywhere] * 7,
        out_shape=[
            jax.ShapeDtypeStruct((seq, d_model), BF16),
            jax.ShapeDtypeStruct((d_model, n1), F32),
            jax.ShapeDtypeStruct((8 * piece, n1), F32),
            jax.ShapeDtypeStruct((d_model, no), F32),
        ] + [jax.ShapeDtypeStruct((d_model, heads3 // 3), F32)] * 3,
        scratch_shapes=[
            pltpu.VMEM((seq, heads3 // 3), BF16),
            pltpu.VMEM((PAIR, seq), BF16),
            pltpu.VMEM((seq, PAIR), F32),
            pltpu.VMEM((seq, PAIR), F32),
            pltpu.VMEM((seq, 2 * BWD_ROWS), BF16),
            pltpu.VMEM((seq, 2 * BWD_ROWS), BF16),
            pltpu.VMEM((seq, heads3), BF16),
            pltpu.VMEM((blk, 4 * heads3), BF16),
            pltpu.VMEM((8, 2 * piece, n1), F32),
            pltpu.VMEM((4, 2 * piece, no), F32),
            pltpu.VMEM((8, piece, n1), F32),
            pltpu.VMEM((4, piece, no), F32),
            pltpu.VMEM((2, piece, n1), F32),
            pltpu.VMEM((2, 4, piece, no), F32),
            pltpu.VMEM((2, 4, piece, n1), F32),
            pltpu.VMEM((4, piece, no), F32),
            pltpu.VMEM((piece, n1), F32),
            pltpu.VMEM((piece, n1), F32),
            pltpu.VMEM((piece, no), F32),
            pltpu.VMEM((2, 2 * piece, heads3), F32),
            pltpu.VMEM((2, 2 * piece, heads3), F32),
            pltpu.VMEM((2, 2 * piece, heads3), F32),
            pltpu.VMEM((2 * piece, heads3), F32),
            pltpu.VMEM((2 * piece, heads3), F32),
            pltpu.VMEM((2, piece, heads3), F32),
            pltpu.VMEM((blk, d_model), BF16),
            pltpu.VMEM((2, w_rows, 4 * heads3), BF16),
            pltpu.VMEM((2, seq, 2 * piece), BF16),
            pltpu.VMEM((2, 2 * piece, heads3), F32),
            dma((9,)), dma((14,)), dma((copies,)), dma((copies,)),
            dma((4,)), dma((4,)), dma((24,)), dma((24,)), dma((12,)), dma((12,)), dma((5,)), dma((7,)), dma((1,)), dma((1,)),
        ],
        compiler_params=pltpu.CompilerParams(vmem_limit_bytes=63 << 20, collective_id=1, has_side_effects=True),
        cost_estimate=pl.CostEstimate(
            flops=160 * seq * seq * PAIR, bytes_accessed=128 * seq * d_model, transcendentals=seq * seq * 4),
        name="last",
    )(qkv, d_c, lse, d_mid, x, emb, w_qkv, u_seq, g_qkv, *w2_parts, *w1_parts, *wo_parts)


def lin(z, y, x, c):
    return z * 8 + y * 4 + x * 2 + c


def send(value, to):
    pairs = []
    for z in range(4):
        for y in range(2):
            for x in range(2):
                for c in range(2):
                    dst = to(z, y, x, c)
                    if dst is not None:
                        pairs.append((lin(z, y, x, c), lin(*dst)))
    return lax.ppermute(value, AXES, pairs)


def role_of(z, c):
    return (z % 2) * 2 + c


def in_group(k):
    def to(z, y, x, c):
        role = role_of(z, c) ^ k
        return (z // 2 * 2 + role // 2, y, x, role % 2)

    return to


def other_core(z, y, x, c):
    return (z, y, x, 1 - c)


def swap_first(z, y, x, c):
    return (z, y, 1 - x, c) if c == 0 else (z, 1 - y, x, c)


def unscramble(parts, role):
    odd, high = role % 2 == 1, role // 2 == 1
    a = [jnp.where(odd, parts[i ^ 1], parts[i]) for i in range(4)]
    return [jnp.where(high, a[i ^ 2], a[i]) for i in range(4)]


def rows_of(value, index, count):
    return lax.dynamic_slice_in_dim(value, index * count, count, axis=0)


def solution(mesh):
    spec_col = P(None, 'model')
    spec_row = P('model', None)
    spec_act = P('data', None, None)
    spec_rep = P(None, None)

    def device_step(x_in, cot_out, step_emb, w_q, w_k, w_v, w_o, w_1, w_2):
        seq, d_model = x_in.shape[1:]
        head_cols = w_q.shape[1]
        blk = seq // 4
        z = lax.axis_index('model')
        d = lax.axis_index('data')
        y, x, core = d // 4, d // 2 % 2, d % 2
        role = z % 2 * 2 + core
        owner = core == z // 2
        emb = step_emb.astype(F32)

        c_1, lse_1, x_seq, cot, wo, w1, w2, w_qkv = first_call(
            x_in[0], cot_out[0], emb[:1], w_q, w_k, w_v, w_o, w_1, w_2)
        wo, w2 = wo.reshape(-1, d_model), w2.reshape(-1, d_model)
        w_qkv_role = lax.dynamic_slice_in_dim(w_qkv, role * 3 * head_cols, 3 * head_cols, axis=1)
        x_1 = rows_of(x_seq, role, blk)

        def exchange(parts):
            swapped = unscramble(parts, role)
            got = [swapped[0]] + [send(swapped[k], in_group(k)) for k in (1, 2, 3)]
            return unscramble(got, role)

        def mlp_forward(x_f, context):
            h = (x_f + dot_nn(context, wo)).astype(BF16)
            m = rms_norm(h.astype(F32)).astype(BF16)
            up = dot_nn(m, w1).astype(BF16)
            act = jax.nn.gelu(up.astype(F32)).astype(BF16)
            return h, m, up, act

        def interleave(pairs):
            return jnp.concatenate([pairs[j][i] for i in range(4) for j in range(2)], axis=1)

        s_1 = x_1.astype(F32) + emb[0]
        h_1, m_1, up_1, act_1 = mlp_forward(s_1, c_1)
        x_2 = (h_1.astype(F32) + dot_nn(act_1, w2)).astype(BF16)

        side = send(x_2, other_core)
        over = send(x_2, in_group(2))
        x_2_seq = jnp.concatenate(unscramble([x_2, side, over, send(over, other_core)], role), axis=0)
        u_2_seq = rms_norm(x_2_seq.astype(F32) + emb[1]).astype(BF16)
        qkv_2 = dot_nn(u_2_seq, w_qkv_role).astype(BF16)
        got, lse_2 = [], []
        for j in range(2):
            c_heads, lse = attn_fwd(qkv_2, j)
            got.append(exchange([c_heads[i * blk:(i + 1) * blk] for i in range(4)]))
            lse_2.append(lse)
        c_2 = interleave(got)
        lse_2 = jnp.concatenate(lse_2, axis=0)
        s_2 = x_2.astype(F32) + emb[1]
        h_2, m_2, up_2, act_2 = mlp_forward(s_2, c_2)

        def mlp_backward(d_next, h, up):
            d_act = dot_nt(d_next, w2).astype(BF16)
            d_up = jax.vjp(jax.nn.gelu, up.astype(F32))[1](d_act.astype(F32))[0].astype(BF16)
            d_m = dot_nt(d_up, w1).astype(BF16)
            d_h = jax.vjp(rms_norm, h.astype(F32))[1](d_m.astype(F32))[0]
            return d_up, (d_next.astype(F32) + d_h).astype(BF16)

        d_up_2, d_mid_2 = mlp_backward(cot, h_2, up_2)
        d_c = dot_nt(d_mid_2, wo).astype(BF16)
        pairs, grads = [], []
        for j in range(2):
            heads = exchange([d_c[:, i * head_cols + j * PAIR:i * head_cols + (j + 1) * PAIR] for i in range(4)])
            d_heads = attn_bwd(qkv_2, jnp.concatenate(heads, axis=0), lse_2[2 * j:2 * j + 2], j)
            grads.append(dot_tn(u_2_seq, d_heads))
            pairs.append(exchange([d_heads[i * blk:(i + 1) * blk] for i in range(4)]))
        d_qkv = jnp.concatenate(
            [pairs[j][i][:, t * PAIR:(t + 1) * PAIR] for i in range(4) for t in range(3) for j in range(2)], axis=1)
        g_qkv_2 = jnp.concatenate([grads[j][:, t * PAIR:(t + 1) * PAIR] for t in range(3) for j in range(2)], axis=1)
        d_u = dot_nt(d_qkv, w_qkv).astype(BF16)
        d_s = jax.vjp(rms_norm, s_2)[1](d_u.astype(F32))[0]
        d_2 = (d_mid_2.astype(F32) + d_s).astype(BF16)

        u_1_seq = rms_norm(x_seq.astype(F32) + emb[0]).astype(BF16)
        qkv_1 = dot_nn(u_1_seq, w_qkv_role).astype(BF16)

        first, second = jnp.where(core == 0, x, y), jnp.where(core == 0, y, x)

        def at(i, j):
            return jnp.where(core == 0, j * 2 + i, i * 2 + j)

        order = [at(1 - first, second), at(1 - first, 1 - second), at(first, 1 - second), at(first, second)]
        column = jnp.stack(order) * 2 + core

        def products(sides, by_left=False):
            lefts, rights = [], []
            for left, right in sides:
                lefts += [left, send(left, other_core)]
                rights += [right, send(right, other_core)]
            return grad_products(column, lefts, rights, by_left)

        away, mid, keep = products([(act_2, cot), (act_1, d_2)], True)
        d_2, away = lax.optimization_barrier((d_2, away))
        w2_parts = (send(away, swap_first), mid, keep)
        d_up_1, d_mid_1 = mlp_backward(d_2, h_1, up_1)
        w1_parts = products([(m_2, d_up_2), (m_1, d_up_1)])
        wo_parts = products([(d_mid_2, c_2), (d_mid_1, c_1)])
        d_c = dot_nt(d_mid_1, wo).astype(BF16)
        d_x, g_w1, g_w2, g_wo, g_q, g_k, g_v = last_call(
            qkv_1, d_c, lse_1, d_mid_1, x_1, emb[:1], w_qkv, u_1_seq, g_qkv_2, w2_parts, w1_parts, wo_parts)
        return g_q, g_k, g_v, g_wo.T, g_w1, g_w2, d_x[None]

    return jax.shard_map(device_step, mesh=mesh,
                         in_specs=(spec_act, spec_act, spec_rep, spec_col, spec_col, spec_col, spec_row, spec_col, spec_row),
                         out_specs=(spec_col, spec_col, spec_col, spec_row, spec_col, spec_row, spec_act),
                         check_vma=False)
```

profile of v0, /device:TPU:17, one launch (start us, length us, event | category | flops | bytes accessed | tf_op | source)
XLA Modules:
  0.0 779.4 jit_solution(371875045414154825)
XLA Ops:
  2.0 119.1 %first.1 = (bf16[512,1024]{1,0:T(8,128)(2,1)}, f32[4,2048]{1,0:T(4,128)}, bf16[2048,1024]{1,0:T(8,128)(2,1)}, bf16[512,1024]{1,0:T(8,128)(2,1)}, bf16[4,256,1024...) custom-call(bf16[2048,1024]{1,0:T(8,128)(2,1)} %bitcast.51, ...), custom_call_target="tpu_custom_call" | custom-call | flops 34359738368 | bytes 134217728 | tf_op jit(solution)/shard_map/first/pallas_call | solution.py:412
  122.6 3.9 fusion.32
  126.9 7.7 fusion.13
  134.7 5.4 fusion.34
  140.9 23.9 %collective-permute-done = bf16[512,1024]{1,0:T(8,128)(2,1)S(1)} collective-permute-done((bf16[512,1024]{1,0:T(8,128)(2,1)S(1)}, bf16[512,1024]{1,0:T(8,128)(2,1)S(1)}, u32[]{:S(2)}, u32[]{:S(2)}) %collective-permute-start) | collective-permute-done | bytes 1048608 | tf_op jit(solution)/shard_map/ppermute | solution.py:935
  167.7 4.1 multiply_convert_fusion.1.u_ref
  174.9 11.4 %multiply_convert_fusion = bf16[2048,1024]{1,0:T(8,128)(2,1)S(1)} fusion(f32[2048]{0:T(1024)S(1)} %add_rsqrt_fusion, f32[1024]{0:T(1024)S(1)} %bitcast.44, bf16[512,1024]{1,0:T(8,128)(2,1)S(1)} %get-tuple-element.97, bf16[512,1024]{1,0:T(8,128)(2,1)S(1)} %get-tuple-element.96, bf16[512,1024]{1,0:T(8,128)(2,1)S(1)} %get-tuple-element.95, ...), kind=kLoop, calls=%fused_computation.34 | loop fusion | flops 23068672 | bytes 8400896 | tf_op jit(solution)/shard_map/convert_element_type | solution.py:1013
  188.4 6.1 convolution_convert_fusion.4.q_ref.k_ref.v_ref
  194.5 15.2 %attn_fwd.3 = (bf16[2048,128]{1,0:T(8,128)(2,1)}, f32[2,2048]{1,0:T(2,128)}) custom-call(bf16[2048,768]{1,0:T(8,128)(2,1)} %convolution_convert_fusion.4.q_ref.k_ref.v_ref, bf16[2048,768]{1,0:T(8,128)(2,1)} %convolution_convert_fusion.4.q_ref.k_ref.v_ref, bf16[2048,768]{1,0:T(8,128)(2,1)} %convolution_convert_fusion.4.q_ref.k_ref.v_ref), custom_call_target="tpu_custom_call" | custom-call | flops 8589934592 | bytes 2097152 | tf_op jit(solution)/shard_map/attn_fwd/pallas_call | solution.py:57
  209.7 15.7 %attn_fwd.2 = (bf16[2048,128]{1,0:T(8,128)(2,1)}, f32[2,2048]{1,0:T(2,128)}) custom-call(bf16[2048,768]{1,0:T(8,128)(2,1)} %convolution_convert_fusion.4.q_ref.k_ref.v_ref, bf16[2048,768]{1,0:T(8,128)(2,1)} %convolution_convert_fusion.4.q_ref.k_ref.v_ref, bf16[2048,768]{1,0:T(8,128)(2,1)} %convolution_convert_fusion.4.q_ref.k_ref.v_ref), custom_call_target="tpu_custom_call" | custom-call | flops 8589934592 | bytes 2097152 | tf_op jit(solution)/shard_map/attn_fwd/pallas_call | solution.py:57
  228.9 3.6 collective-permute-done.3
  241.9 11.6 %fusion.21 = (bf16[512,4096]{1,0:T(8,128)(2,1)}, bf16[512,4096]{1,0:T(8,128)(2,1)S(1)}) fusion(bf16[512,1024]{1,0:T(8,128)(2,1)S(1)} %fusion.30.refs_0_.refs_1_.refs_2_.refs_3_, bf16[1024,4096]{1,0:T(8,128)(2,1)} %get-tuple-element.43), kind=kOutput, calls=%fused_computation.33 | convolution fusion | flops 4318035968 | bytes 17825792 | tf_op jit(solution)/shard_map/dot_general | solution.py:36
  253.6 12.6 %fusion.4.refs_16_ = bf16[512,4096]{1,0:T(8,128)(2,1)} fusion(bf16[512,4096]{1,0:T(8,128)(2,1)S(1)} %get-tuple-element.147, bf16[512,1024]{1,0:T(8,128)(2,1)} %get-tuple-element.39.refs_16_, bf16[4096,1024]{1,0:T(8,128)(2,1)S(1)} %bitcast.59), kind=kOutput, calls=%fused_computation.16 | convolution fusion | flops 4343201792 | bytes 17825792 | tf_op jit(solution)/shard_map/dot_general | solution.py:32
  266.2 9.3 %fusion.31 = (f32[512]{0:T(512)S(1)}, bf16[512,1024]{1,0:T(8,128)(2,1)S(1)}) fusion(bf16[512,1024]{1,0:T(8,128)(2,1)S(1)} %get-tuple-element.142, bf16[512,4096]{1,0:T(8,128)(2,1)} %fusion.4.refs_16_, bf16[1024,4096]{1,0:T(8,128)(2,1)} %get-tuple-element.43), kind=kOutput, calls=%fused_computation.72 | convolution fusion | flops 4297588224 | bytes 14682112 | tf_op jit(solution)/shard_map/dot_general | solution.py:32
  282.9 3.3 collective-permute-start.15
  289.2 30.5 %attn_bwd.2 = bf16[2048,384]{1,0:T(8,128)(2,1)} custom-call(bf16[2048,768]{1,0:T(8,128)(2,1)} %convolution_convert_fusion.4.q_ref.k_ref.v_ref, bf16[2048,768]{1,0:T(8,128)(2,1)} %convolution_convert_fusion.4.q_ref.k_ref.v_ref, bf16[2048,768]{1,0:T(8,128)(2,1)} %convolution_convert_fusion.4.q_ref.k_ref.v_ref, bf16[2048,128]{1,0:T(8,128)(2,1)} %pad_maximum_fusion.1.do_ref, ...), custom_call_target="tpu_custom_call" | custom-call | flops 21474836480 | bytes 3670016 | tf_op jit(solution)/shard_map/attn_bwd/pallas_call | solution.py:102
  319.7 2.5 broadcast_select_fusion.38
  326.9 30.7 %attn_bwd.3 = bf16[2048,384]{1,0:T(8,128)(2,1)} custom-call(bf16[2048,768]{1,0:T(8,128)(2,1)} %convolution_convert_fusion.4.q_ref.k_ref.v_ref, bf16[2048,768]{1,0:T(8,128)(2,1)} %convolution_convert_fusion.4.q_ref.k_ref.v_ref, bf16[2048,768]{1,0:T(8,128)(2,1)} %convolution_convert_fusion.4.q_ref.k_ref.v_ref, bf16[2048,128]{1,0:T(8,128)(2,1)} %pad_maximum_fusion.2.do_ref, ...), custom_call_target="tpu_custom_call" | custom-call | flops 21474836480 | bytes 3670016 | tf_op jit(solution)/shard_map/attn_bwd/pallas_call | solution.py:102
  363.0 7.9 %collective-permute-done.18 = bf16[512,384]{1,0:T(8,128)(2,1)S(1)} collective-permute-done((bf16[512,384]{1,0:T(8,128)(2,1)S(1)}, bf16[512,384]{1,0:T(8,128)(2,1)S(1)}, u32[]{:S(2)}, u32[]{:S(2)}) %collective-permute-start.18) | collective-permute-done | bytes 393248 | tf_op jit(solution)/shard_map/ppermute | solution.py:935
  370.8 7.8 collective-permute-done.19
  381.1 3.6 multiply_reduce_fusion.2
  387.2 5.1 convolution_convert_fusion.5.qkv_ref
  392.4 3.5 fusion.47
  398.4 17.8 %grad.3 = (f32[4,256,1024]{2,1,0:T(8,128)}, f32[4,128,1024]{2,1,0:T(8,128)}, f32[4,128,1024]{2,1,0:T(8,128)}) custom-call(s32[4]{0:T(128)} %fusion.41._, bf16[512,4096]{1,0:T(8,128)(2,1)} %get-tuple-element.146.refs_0_.refs_1_.refs_2_.refs_3_, bf16[512,4096]{1,0:T(8,128)(2,1)} %get-tuple-element.146.refs_0_.refs_1_.refs_2_.refs_3_, ...), custom_call_target="tpu_custom_call" | custom-call | flops 8589934592 | bytes 27262976 | tf_op jit(solution)/shard_map/grad/pallas_call | solution.py:480
  416.2 13.8 %fusion.7.refs_18_ = bf16[512,4096]{1,0:T(8,128)(2,1)} fusion(bf16[512,4096]{1,0:T(8,128)(2,1)} %copy-done.39, bf16[512,1024]{1,0:T(8,128)(2,1)} %fusion.26.refs_18_, bf16[4096,1024]{1,0:T(8,128)(2,1)} %bitcast.53), kind=kOutput, calls=%fused_computation.19 | convolution fusion | flops 4343201792 | bytes 17825792 | tf_op jit(solution)/shard_map/dot_general | solution.py:32
  431.0 9.4 %fusion.35 = (f32[512]{0:T(512)S(1)}, bf16[512,1024]{1,0:T(8,128)(2,1)S(1)}) fusion(bf16[512,1024]{1,0:T(8,128)(2,1)S(1)} %copy-done.12, bf16[512,4096]{1,0:T(8,128)(2,1)} %fusion.7.refs_18_, bf16[1024,4096]{1,0:T(8,128)(2,1)} %get-tuple-element.43), kind=kOutput, calls=%fused_computation.76 | convolution fusion | flops 4297588224 | bytes 14682112 | tf_op jit(solution)/shard_map/dot_general | solution.py:32
  443.8 2.4 fusion.46
  455.3 8.0 %grad.5 = (f32[4,256,256]{2,1,0:T(8,128)}, f32[4,128,256]{2,1,0:T(8,128)}, f32[4,128,256]{2,1,0:T(8,128)}) custom-call(s32[4]{0:T(128)} %fusion.41._, bf16[512,1024]{1,0:T(8,128)(2,1)} %copy-done.2, bf16[512,1024]{1,0:T(8,128)(2,1)} %copy-done.2, bf16[512,1024]{1,0:T(8,128)(2,1)} %copy-done.2, bf16[512,1024]{1,0:T(8,128)(2,1)} %copy-done.2, ...), custom_call_target="tpu_custom_call" | custom-call | flops 2147483648 | bytes 8388608 | tf_op jit(solution)/shard_map/grad/pallas_call | solution.py:480
  464.3 16.8 %grad.4 = (f32[4,256,1024]{2,1,0:T(8,128)}, f32[4,128,1024]{2,1,0:T(8,128)}, f32[4,128,1024]{2,1,0:T(8,128)}) custom-call(s32[4]{0:T(128)} %fusion.41._, bf16[512,1024]{1,0:T(8,128)(2,1)} %copy-done.5, bf16[512,1024]{1,0:T(8,128)(2,1)} %copy-done.5, bf16[512,1024]{1,0:T(8,128)(2,1)} %copy-done.5, bf16[512,1024]{1,0:T(8,128)(2,1)} %copy-done.5, ...), custom_call_target="tpu_custom_call" | custom-call | flops 8589934592 | bytes 27262976 | tf_op jit(solution)/shard_map/grad/pallas_call | solution.py:480
  481.1 281.4 %last.1 = (bf16[2048,1024]{1,0:T(8,128)(2,1)}, f32[1024,1024]{1,0:T(8,128)}, f32[1024,1024]{1,0:T(8,128)}, f32[1024,256]{1,0:T(8,128)}, f32[1024,256]{1,0:T(8,12...) custom-call(bf16[2048,768]{1,0:T(8,128)(2,1)} %convolution_convert_fusion.5.qkv_ref, ...), custom_call_target="tpu_custom_call" | custom-call | flops 85899345920 | bytes 268435456 | tf_op jit(solution)/shard_map/last/pallas_call | solution.py:872
  762.5 2.7 copy.22
  765.2 2.4 copy.66
  (238 shorter events, 78.0 us)
Async XLA Ops:
  140.1 24.7 %collective-permute-start = (bf16[512,1024]{1,0:T(8,128)(2,1)S(1)}, bf16[512,1024]{1,0:T(8,128)(2,1)S(1)}, u32[]{:S(2)}, u32[]{:S(2)}) collective-permute-start(bf16[512,1024]{1,0:T(8,128)(2,1)S(1)} %fusion.34), channel_id=1, source_target_pairs={{0,8},{1,9},{2,10},{3,11},{4,12},{5,13},{6,14},{7,15},{8,0},{9,1},... | collective-permute-start | bytes 3145736 | tf_op jit(solution)/shard_map/ppermute | solution.py:935
  140.2 31.6 %collective-permute-start.2 = (bf16[512,1024]{1,0:T(8,128)(2,1)S(1)}, bf16[512,1024]{1,0:T(8,128)(2,1)}, u32[]{:S(2)}, u32[]{:S(2)}) collective-permute-start(bf16[512,1024]{1,0:T(8,128)(2,1)S(1)} %fusion.34), channel_id=1, source_target_pairs={{0,1},{1,0},{2,3},{3,2},{4,5},{5,4},{6,7},{7,6},{8,9},{9,8},{10,11... | collective-permute-start | bytes 3145736 | tf_op jit(solution)/shard_map/ppermute | solution.py:935
  140.4 302.2 %collective-permute-start.33 = (bf16[512,1024]{1,0:T(8,128)(2,1)}, bf16[512,1024]{1,0:T(8,128)(2,1)}, u32[]{:S(2)}, u32[]{:S(2)}) collective-permute-start(bf16[512,1024]{1,0:T(8,128)(2,1)} %get-tuple-element.41.refs_18_), channel_id=1, source_target_pairs={{0,1},{1,0},{2,3},{3,2},{4,5},{5,4},{6,7},{7,6},{8,9},{9,8},{10,11... | collective-permute-start | bytes 3145736 | tf_op jit(solution)/shard_map/ppermute | solution.py:935
  140.8 255.1 %collective-permute-start.23 = (bf16[512,1024]{1,0:T(8,128)(2,1)}, bf16[512,1024]{1,0:T(8,128)(2,1)}, u32[]{:S(2)}, u32[]{:S(2)}) collective-permute-start(bf16[512,1024]{1,0:T(8,128)(2,1)} %get-tuple-element.39.refs_16_), channel_id=1, source_target_pairs={{0,1},{1,0},{2,3},{3,2},{4,5},{5,4},{6,7},{7,6},{8,9},{9,8},{10,11... | collective-permute-start | bytes 3145736 | tf_op jit(solution)/shard_map/ppermute | solution.py:935
  164.8 7.0 collective-permute-start.1
  226.7 5.9 collective-permute-start.3
  226.7 7.6 collective-permute-start.4
  228.1 6.4 collective-permute-start.5
  232.5 5.7 collective-permute-start.6
  234.3 5.0 collective-permute-start.7
  279.8 6.4 collective-permute-start.11
  281.1 7.2 collective-permute-start.9
  282.9 39.2 %collective-permute-start.15 = (bf16[512,128]{1,0:T(8,128)(2,1)S(1)}, bf16[512,128]{1,0:T(8,128)(2,1)S(1)}, u32[]{:S(2)}, u32[]{:S(2)}) collective-permute-start(bf16[512,128]{1,0:T(8,128)(2,1)S(1)} %get-tuple-element.119), channel_id=1, source_target_pairs={{0,9},{1,8},{2,11},{3,10},{4,13},{5,12},{6,15},{7,14},{8,1},{9,0},... | collective-permute-start | bytes 393224 | tf_op jit(solution)/shard_map/ppermute | solution.py:935
  286.2 37.1 %collective-permute-start.16 = (bf16[512,128]{1,0:T(8,128)(2,1)}, bf16[512,128]{1,0:T(8,128)(2,1)}, u32[]{:S(2)}, u32[]{:S(2)}) collective-permute-start(bf16[512,128]{1,0:T(8,128)(2,1)} %get-tuple-element.79), channel_id=1, source_target_pairs={{0,8},{1,9},{2,10},{3,11},{4,12},{5,13},{6,14},{7,15},{8,0},{9,1},... | collective-permute-start | bytes 393224 | tf_op jit(solution)/shard_map/ppermute | solution.py:935
  288.3 36.4 %collective-permute-start.17 = (bf16[512,128]{1,0:T(8,128)(2,1)S(1)}, bf16[512,128]{1,0:T(8,128)(2,1)}, u32[]{:S(2)}, u32[]{:S(2)}) collective-permute-start(bf16[512,128]{1,0:T(8,128)(2,1)S(1)} %get-tuple-element.113), channel_id=1, source_target_pairs={{0,1},{1,0},{2,3},{3,2},{4,5},{5,4},{6,7},{7,6},{8,9},{9,8},{10,11... | collective-permute-start | bytes 393224 | tf_op jit(solution)/shard_map/ppermute | solution.py:935
  322.8 36.5 %collective-permute-start.12 = (bf16[512,384]{1,0:T(8,128)(2,1)}, bf16[512,384]{1,0:T(8,128)(2,1)S(1)}, u32[]{:S(2)}, u32[]{:S(2)}) collective-permute-start(bf16[512,384]{1,0:T(8,128)(2,1)} %get-tuple-element.112), channel_id=1, source_target_pairs={{0,9},{1,8},{2,11},{3,10},{4,13},{5,12},{6,15},{7,14},{8,1},{9,0},... | collective-permute-start | bytes 1179656 | tf_op jit(solution)/shard_map/ppermute | solution.py:935
  323.3 36.4 %collective-permute-start.13 = (bf16[512,384]{1,0:T(8,128)(2,1)}, bf16[512,384]{1,0:T(8,128)(2,1)}, u32[]{:S(2)}, u32[]{:S(2)}) collective-permute-start(bf16[512,384]{1,0:T(8,128)(2,1)} %get-tuple-element.82), channel_id=1, source_target_pairs={{0,8},{1,9},{2,10},{3,11},{4,12},{5,13},{6,14},{7,15},{8,0},{9,1},... | collective-permute-start | bytes 1179656 | tf_op jit(solution)/shard_map/ppermute | solution.py:935
  324.7 36.3 %collective-permute-start.14 = (bf16[512,384]{1,0:T(8,128)(2,1)S(1)}, bf16[512,384]{1,0:T(8,128)(2,1)}, u32[]{:S(2)}, u32[]{:S(2)}) collective-permute-start(bf16[512,384]{1,0:T(8,128)(2,1)S(1)} %get-tuple-element.111), channel_id=1, source_target_pairs={{0,1},{1,0},{2,3},{3,2},{4,5},{5,4},{6,7},{7,6},{8,9},{9,8},{10,11... | collective-permute-start | bytes 1179656 | tf_op jit(solution)/shard_map/ppermute | solution.py:935
  359.4 11.5 %collective-permute-start.18 = (bf16[512,384]{1,0:T(8,128)(2,1)S(1)}, bf16[512,384]{1,0:T(8,128)(2,1)S(1)}, u32[]{:S(2)}, u32[]{:S(2)}) collective-permute-start(bf16[512,384]{1,0:T(8,128)(2,1)S(1)} %get-tuple-element.107), channel_id=1, source_target_pairs={{0,9},{1,8},{2,11},{3,10},{4,13},{5,12},{6,15},{7,14},{8,1},{9,0},... | collective-permute-start | bytes 1179656 | tf_op jit(solution)/shard_map/ppermute | solution.py:935
  359.7 18.9 %collective-permute-start.19 = (bf16[512,384]{1,0:T(8,128)(2,1)S(1)}, bf16[512,384]{1,0:T(8,128)(2,1)S(1)}, u32[]{:S(2)}, u32[]{:S(2)}) collective-permute-start(bf16[512,384]{1,0:T(8,128)(2,1)S(1)} %get-tuple-element.108), channel_id=1, source_target_pairs={{0,8},{1,9},{2,10},{3,11},{4,12},{5,13},{6,14},{7,15},{8,0},{9,1},... | collective-permute-start | bytes 1179656 | tf_op jit(solution)/shard_map/ppermute | solution.py:935
  361.0 18.5 %collective-permute-start.20 = (bf16[512,384]{1,0:T(8,128)(2,1)S(1)}, bf16[512,384]{1,0:T(8,128)(2,1)S(1)}, u32[]{:S(2)}, u32[]{:S(2)}) collective-permute-start(bf16[512,384]{1,0:T(8,128)(2,1)S(1)} %get-tuple-element.106), channel_id=1, source_target_pairs={{0,1},{1,0},{2,3},{3,2},{4,5},{5,4},{6,7},{7,6},{8,9},{9,8},{10,11... | collective-permute-start | bytes 1179656 | tf_op jit(solution)/shard_map/ppermute | solution.py:935
  370.8 25.6 %collective-permute-start.22 = (bf16[512,4096]{1,0:T(8,128)(2,1)S(1)}, bf16[512,4096]{1,0:T(8,128)(2,1)S(1)}, u32[]{:S(2)}, u32[]{:S(2)}) collective-permute-start(bf16[512,4096]{1,0:T(8,128)(2,1)S(1)} %copy-done), channel_id=1, source_target_pairs={{0,1},{1,0},{2,3},{3,2},{4,5},{5,4},{6,7},{7,6},{8,9},{9,8},{10,11... | collective-permute-start | bytes 12582920 | tf_op jit(solution)/shard_map/ppermute | solution.py:935
  378.6 19.7 %collective-permute-start.21 = (bf16[512,4096]{1,0:T(8,128)(2,1)}, bf16[512,4096]{1,0:T(8,128)(2,1)}, u32[]{:S(2)}, u32[]{:S(2)}) collective-permute-start(bf16[512,4096]{1,0:T(8,128)(2,1)} %get-tuple-element.146.refs_0_.refs_1_.refs_2_.refs_3_), channel_id=1, source_target_pairs={{0,1},{1,0},{2,3},{3,2},{4,5},{5,4},{6,7},{7,6},{8,9},{9,8},{10,11... | collective-permute-start | bytes 12582920 | tf_op jit(solution)/shard_map/ppermute | solution.py:935
  386.4 9.6 %collective-permute-start.24 = (bf16[512,1024]{1,0:T(8,128)(2,1)}, bf16[512,1024]{1,0:T(8,128)(2,1)S(1)}, u32[]{:S(2)}, u32[]{:S(2)}) collective-permute-start(bf16[512,1024]{1,0:T(8,128)(2,1)} %fusion.26.refs_18_), channel_id=1, source_target_pairs={{0,1},{1,0},{2,3},{3,2},{4,5},{5,4},{6,7},{7,6},{8,9},{9,8},{10,11... | collective-permute-start | bytes 3145736 | tf_op jit(solution)/shard_map/ppermute | solution.py:935
  395.9 47.8 %collective-permute-start.30 = (bf16[512,1024]{1,0:T(8,128)(2,1)S(1)}, bf16[512,1024]{1,0:T(8,128)(2,1)}, u32[]{:S(2)}, u32[]{:S(2)}) collective-permute-start(bf16[512,1024]{1,0:T(8,128)(2,1)S(1)} %fusion.24.refs_0_.refs_1_.refs_2_.refs_3_), channel_id=1, source_target_pairs={{0,1},{1,0},{2,3},{3,2},{4,5},{5,4},{6,7},{7,6},{8,9},{9,8},{10,11... | collective-permute-start | bytes 3145736 | tf_op jit(solution)/shard_map/ppermute | solution.py:935
  395.9 67.4 %collective-permute-start.28 = (bf16[512,4096]{1,0:T(8,128)(2,1)}, bf16[512,4096]{1,0:T(8,128)(2,1)}, u32[]{:S(2)}, u32[]{:S(2)}) collective-permute-start(bf16[512,4096]{1,0:T(8,128)(2,1)} %fusion.4.refs_16_), channel_id=1, source_target_pairs={{0,1},{1,0},{2,3},{3,2},{4,5},{5,4},{6,7},{7,6},{8,9},{9,8},{10,11... | collective-permute-start | bytes 12582920 | tf_op jit(solution)/shard_map/ppermute | solution.py:935
  430.1 33.3 %collective-permute-start.29 = (bf16[512,4096]{1,0:T(8,128)(2,1)}, bf16[512,4096]{1,0:T(8,128)(2,1)}, u32[]{:S(2)}, u32[]{:S(2)}) collective-permute-start(bf16[512,4096]{1,0:T(8,128)(2,1)} %fusion.7.refs_18_), channel_id=1, source_target_pairs={{0,1},{1,0},{2,3},{3,2},{4,5},{5,4},{6,7},{7,6},{8,9},{9,8},{10,11... | collective-permute-start | bytes 12582920 | tf_op jit(solution)/shard_map/ppermute | solution.py:935
  430.5 50.5 %collective-permute-start.25 = (f32[4,256,1024]{2,1,0:T(8,128)}, f32[4,256,1024]{2,1,0:T(8,128)}, u32[]{:S(2)}, u32[]{:S(2)}) collective-permute-start(f32[4,256,1024]{2,1,0:T(8,128)} %get-tuple-element.51), channel_id=1, source_target_pairs={{0,2},{1,5},{2,0},{3,7},{4,6},{5,1},{6,4},{7,3},{8,10},{9,13},{10,... | collective-permute-start | bytes 12582920 | tf_op jit(solution)/shard_map/ppermute | solution.py:935
  442.6 7.2 collective-permute-start.32
  443.7 6.5 collective-permute-start.31
  449.8 13.5 %collective-permute-start.27 = (bf16[512,1024]{1,0:T(8,128)(2,1)S(1)}, bf16[512,1024]{1,0:T(8,128)(2,1)S(1)}, u32[]{:S(2)}, u32[]{:S(2)}) collective-permute-start(bf16[512,1024]{1,0:T(8,128)(2,1)S(1)} %copy-done.4), channel_id=1, source_target_pairs={{0,1},{1,0},{2,3},{3,2},{4,5},{5,4},{6,7},{7,6},{8,9},{9,8},{10,11... | collective-permute-start | bytes 3145736 | tf_op jit(solution)/shard_map/ppermute | solution.py:935
  450.3 13.0 %collective-permute-start.26 = (bf16[512,1024]{1,0:T(8,128)(2,1)S(1)}, bf16[512,1024]{1,0:T(8,128)(2,1)}, u32[]{:S(2)}, u32[]{:S(2)}) collective-permute-start(bf16[512,1024]{1,0:T(8,128)(2,1)S(1)} %copy-done.6), channel_id=1, source_target_pairs={{0,1},{1,0},{2,3},{3,2},{4,5},{5,4},{6,7},{7,6},{8,9},{9,8},{10,11... | collective-permute-start | bytes 3145736 | tf_op jit(solution)/shard_map/ppermute | solution.py:935
  (50 other events, 606.6 us)
where the time goes:
time: 790 us; the launch traced here: 779 us
  Pallas kernels  535 us (68%)
  matrix products  99.5 us (13%)
  waiting for transfers between devices  48.5 us (6%)
  other arithmetic  38.2 us (5%)
  local copies, waits for them, and re-layouts  33.2 us (4%)
  starting transfers between devices  22.7 us (3%)
    pallas_call x1, Pallas kernels, last_call(): pl.pallas_call(last_kernel, in_specs=[in_vmem] * 6 + [anywhere] * 12, out...  281 us
    pallas_call x1, Pallas kernels, first_call(): pl.pallas_call(first_kernel, in_specs=[in_vmem, anywhere] + [in_vmem] * 7...  119 us
    pallas_call x2, Pallas kernels, attn_bwd(): pl.pallas_call(attn_bwd_kernel, grid=(seq // BWD_ROWS,), in_specs=[rows(p...  61.3 us
    dot_general x7, matrix products, dot_nt(): lax.dot_general(a, b, (((1,), (1,)), ((), ())), preferred_element_type=F32)  52.3 us
    ppermute x34, waiting for transfers between devices, send(): return lax.ppermute(value, AXES, pairs)  48.5 us
    pallas_call x3, Pallas kernels, grad_products(): pl.pallas_call(functools.partial(grad_kernel, by_left), grid_spec=pltpu.P...  42.5 us
    dot_general x7, matrix products, dot_nn(): lax.dot_general(a, b, (((1,), (0,)), ((), ())), preferred_element_type=F32)  41.3 us
    pallas_call x2, Pallas kernels, attn_fwd(): pl.pallas_call(attn_fwd_kernel, grid=(seq // rows,), in_specs=[pl.BlockSp...  30.9 us
  transfers between devices with their start and end apart: 34, of which 7 were waited for; matrix products, arithmetic and copies ran while one was open for 16% of the time, Pallas kernels for 17%

commit v1 on v0

--- a/solution.py
+++ b/solution.py
@@ -520,12 +520,15 @@
 
 
 def last_kernel(qkv_ref, dc_ref, lse_ref, dmid_ref, x_ref, emb_ref, wqkv_ref, u_ref, gqkv2_ref,
-                r2_ref, mid2_ref, keep2_ref, away1_ref, mid1_ref, keep1_ref, awayo_ref, mido_ref, keepo_ref,
-                dx_ref, g1_ref, g2_ref, go_ref, gq_ref, gk_ref, gv_ref,
-                dch, k_t, dk_acc, dv_acc, p_cat, ds_cat, d_heads, d_qkv, buf, buf_o, second, second_o, tmp, tmp_o,
-                third, third_o, sum_1, sum_2, sum_o, qa, qb, q1, q2, q3, q4, d_1, w_s, u_s, g_s,
-                local_sem, load_sem, send_sem, recv_sem, dc_send, dc_recv, dq_send, dq_recv, z_send, z_recv, x_send, x_recv,
-                p_send, p_recv):
+                r2_ref, mid2_ref, keep2_ref, *refs):
+    lefts = {'1': refs[:4], 'o': refs[8:12]}
+    rights = {'1': refs[4:8], 'o': refs[12:16]}
+    (dx_ref, g1_ref, g2_ref, go_ref, gq_ref, gk_ref, gv_ref, away1_ref, mid1_ref, keep1_ref, awayo_ref, mido_ref, keepo_ref,
+     dch, k_t, dk_acc, dv_acc, p_cat, ds_cat, d_heads, d_qkv, buf, buf_o, second, second_o, tmp, tmp_o,
+     third, third_o, sum_1, sum_2, sum_o, qa, qb, q1, q2, q3, q4, d_1, w_s, u_s, g_s,
+     left_t, stage,
+     local_sem, load_sem, send_sem, recv_sem, dc_send, dc_recv, dq_send, dq_recv, z_send, z_recv, x_send, x_recv,
+     p_send, p_recv) = refs[16:]
     seq = qkv_ref.shape[0]
     blk = seq // 4
     head_cols = 2 * PAIR
@@ -561,8 +564,10 @@
         def _():
             dch[i * blk:(i + 1) * blk, :] = dc_ref[:, i * head_cols:(i + 1) * head_cols]
 
-    firsts = {('1', q): copies.start(away1_ref.at[q], buf.at[4 + q], to_a) for q in range(4)}
-    firsts['o'] = copies.start(awayo_ref, buf_o, to_a)
+    half = rights['1'][0].shape[1] // 8
+    firsts = {('1', q): [copies.make(away1_ref.at[q, :, h * half:(h + 1) * half], buf.at[4 + q, :, h * half:(h + 1) * half], to_a)
+                         for h in range(2)] for q in range(4)}
+    firsts['o'] = [copies.make(awayo_ref.at[2 * h:2 * h + 2], buf_o.at[2 * h:2 * h + 2], to_a) for h in range(2)]
     w2_loads = [load(r2_ref.at[q], buf.at[q], q) for q in range(4)]
     seconds = {(w, q): copies.make(buf.at[u + q, piece:, :], second.at[u + q], to_b) for w, u in (('2', 0), ('1', 4)) for q in range(4)}
     seconds['o'] = copies.make(buf_o.at[:, piece:, :], second_o, to_b)
@@ -578,7 +583,8 @@
             t, n, bottom, top = tmp, 6, buf.at[u, piece:, :], buf.at[u, :piece, :]
         loads = [load(mid, t.at[0], n), load(keep, t.at[1], n + 1)]
         if unit == 'o' or unit[0] == '1':
-            firsts[unit].wait_recv()
+            for copy in firsts[unit]:
+                copy.wait_recv()
         else:
             w2_loads[unit[1]].wait()
         for copy in loads:
@@ -660,15 +666,74 @@
                 for t in range(3):
                     dq_copy(j, i, t).start()
 
+    index = [here.ya * 2 + here.xa, (1 - here.y) * 2 + 1 - here.x, here.yb * 2 + here.xb, here.y * 2 + here.x]
+    spaces = (p_cat, ds_cat)
+    parts = [('1', n) for n in range(8)] + [('o', n) for n in range(2)]
+
+    def load_lefts(name):
+        for n in range(16):
+            pltpu.make_async_copy(
+                lefts[name][n // 4].at[:, span(index[n % 4] * 2 + core, piece)],
+                d_heads.at[n // 4 * blk:(n // 4 + 1) * blk, n % 4 * piece:(n % 4 + 1) * piece], load_sem.at[14]).start()
+
+    def load_rights(s):
+        name, n = parts[s]
+        for i in range(4):
+            pltpu.make_async_copy(
+                rights[name][i].at[:, n * half:(n + 1) * half], spaces[s % 2].at[i * blk:(i + 1) * blk, :],
+                load_sem.at[15 + s % 2]).start()
+
+    def stored(s):
+        pltpu.make_async_copy(stage.at[s % 2], stage.at[s % 2], load_sem.at[17 + s % 2]).wait()
+
+    def send_part(s):
+        name, n = parts[s]
+        if name == '1':
+            firsts[('1', n // 2)][n % 2].start()
+        else:
+            firsts['o'][n].start()
+
+    load_lefts('1')
+    load_rights(0)
+    for s in range(len(parts)):
+        name, n = parts[s]
+        if n == 0:
+            every = d_heads.at[:, :4 * piece]
+            pltpu.make_async_copy(every, every, load_sem.at[14]).wait()
+            left_t[...] = every[...].T
+            if name == '1':
+                load_lefts('o')
+        if s + 1 < len(parts):
+            load_rights(s + 1)
+        space = spaces[s % 2]
+        pltpu.make_async_copy(space, space, load_sem.at[15 + s % 2]).wait()
+        if s >= 1:
+            stored(s - 1)
+            send_part(s - 1)
+        stage[s % 2] = dot_nn(left_t[...], space[...])
+        if s < 8 and s % 2 == 1:
+            add_mid(('2', s // 2))
+        for row, ref in ((0, (away1_ref, awayo_ref)), (2 * piece, (mid1_ref, mido_ref)), (3 * piece, (keep1_ref, keepo_ref))):
+            count = 2 * piece if row == 0 else piece
+            rows = slice(row, row + count)
+            if name == '1':
+                pltpu.make_async_copy(stage.at[s % 2, rows, :], ref[0].at[n // 2, :, n % 2 * half:(n % 2 + 1) * half],
+                                      load_sem.at[17 + s % 2]).start()
+            else:
+                for k in range(2):
+                    pltpu.make_async_copy(stage.at[s % 2, rows, k * (half // 2):(k + 1) * (half // 2)], ref[1].at[2 * n + k],
+                                          load_sem.at[17 + s % 2]).start()
+    stored(len(parts) - 1)
+    send_part(len(parts) - 1)
+
     for i in range(4):
         @pl.when(role != i)
         def _():
             pltpu.make_async_copy(dc_ref.at[:, :head_cols], dch.at[:blk, :], dc_recv.at[i]).wait()
 
-    moves = {(0, 0): [(add_mid, ('2', 0))], (0, 1): [(add_mid, ('2', 1))], (0, 2): [(add_mid, ('2', 2))],
-             (0, 3): [(add_mid, ('2', 3))], (0, 5): [(add_mid, ('1', 0))], (0, 6): [(finish, ('2', 0))],
-             (1, 0): [(send_d_heads, 0), (finish, ('2', 1))], (1, 1): [(add_mid, ('1', 1))], (1, 3): [(finish, ('2', 2))],
-             (1, 4): [(add_mid, ('1', 2))], (1, 6): [(finish, ('2', 3))]}
+    moves = {(0, 1): [(finish, ('2', 0))], (0, 4): [(finish, ('2', 1)), (add_mid, ('1', 0))], (0, 7): [(finish, ('2', 2))],
+             (1, 0): [(send_d_heads, 0)], (1, 2): [(finish, ('2', 3)), (add_mid, ('1', 1))], (1, 4): [(finish, ('1', 0))],
+             (1, 6): [(add_mid, ('1', 2))]}
     steps = seq // BWD_ROWS
     for j in range(2):
         k_view, v_view = qkv_ref.at[:, (2 + j) * PAIR:(3 + j) * PAIR], qkv_ref.at[:, (4 + j) * PAIR:(5 + j) * PAIR]
@@ -695,7 +760,6 @@
         d_heads[:, 2 * head_cols + j * PAIR:2 * head_cols + (j + 1) * PAIR] = dv_acc[...].astype(BF16)
 
     quarter = 2 * piece
-    index = [here.ya * 2 + here.xa, (1 - here.y) * 2 + 1 - here.x, here.yb * 2 + here.xb, here.y * 2 + here.x]
 
     def quarter_loads(n):
         return [load(u_ref.at[:, span(index[n], quarter)], u_s.at[n % 2], 8 + n % 2),
@@ -719,7 +783,6 @@
             first_q = copies.start(qa, q1, to_a)
 
     add_mid(('1', 3))
-    finish(('1', 0))
     w_rows = w_s.shape[1]
     chunks = wqkv_ref.shape[0] // w_rows
     w_load = load(wqkv_ref.at[:w_rows, :], w_s.at[0], 12)
@@ -858,27 +921,29 @@
             pl.when(z != i)(z_copy(unit, i).wait_send)
 
 
-def last_call(qkv, d_c, lse, d_mid, x, emb, w_qkv, u_seq, g_qkv, w2_parts, w1_parts, wo_parts):
+def last_call(qkv, d_c, lse, d_mid, x, emb, w_qkv, u_seq, g_qkv, w2_parts, w1_sides, wo_sides):
     seq, d_model = u_seq.shape
     blk, piece = seq // 4, d_model // 8
-    n1, no = w1_parts[0].shape[2], wo_parts[0].shape[2]
+    n1, no = w1_sides[4].shape[1] // 4, wo_sides[4].shape[1] // 4
+    assert n1 == 2 * 2 * BWD_ROWS and no * 2 == 2 * BWD_ROWS
     assert w2_parts[0].shape[1:] == (2 * piece, n1)
     heads3 = qkv.shape[1]
     anywhere = pl.BlockSpec(memory_space=pl.ANY)
     in_vmem = pl.BlockSpec(memory_space=pltpu.VMEM)
-    copies = 5 + 9 + 6 * 7 + 3
+    copies = 10 + 9 + 6 * 7 + 3
     dma = pltpu.SemaphoreType.DMA
-    w_rows = min(256, d_model)
+    w_rows = min(128, d_model)
     return pl.pallas_call(
         last_kernel,
-        in_specs=[in_vmem] * 6 + [anywhere] * 12,
-        out_specs=[anywhere] * 7,
+        in_specs=[in_vmem] * 6 + [anywhere] * 22,
+        out_specs=[anywhere] * 13,
         out_shape=[
             jax.ShapeDtypeStruct((seq, d_model), BF16),
             jax.ShapeDtypeStruct((d_model, n1), F32),
             jax.ShapeDtypeStruct((8 * piece, n1), F32),
             jax.ShapeDtypeStruct((d_model, no), F32),
-        ] + [jax.ShapeDtypeStruct((d_model, heads3 // 3), F32)] * 3,
+        ] + [jax.ShapeDtypeStruct((d_model, heads3 // 3), F32)] * 3
+        + [jax.ShapeDtypeStruct((4, k * piece, n), F32) for n in (n1, no) for k in (2, 1, 1)],
         scratch_shapes=[
             pltpu.VMEM((seq, heads3 // 3), BF16),
             pltpu.VMEM((PAIR, seq), BF16),
@@ -909,14 +974,16 @@
             pltpu.VMEM((2, w_rows, 4 * heads3), BF16),
             pltpu.VMEM((2, seq, 2 * piece), BF16),
             pltpu.VMEM((2, 2 * piece, heads3), F32),
-            dma((9,)), dma((14,)), dma((copies,)), dma((copies,)),
+            pltpu.VMEM((4 * piece, seq), BF16),
+            pltpu.VMEM((2, 4 * piece, 2 * BWD_ROWS), F32),
+            dma((9,)), dma((19,)), dma((copies,)), dma((copies,)),
             dma((4,)), dma((4,)), dma((24,)), dma((24,)), dma((12,)), dma((12,)), dma((5,)), dma((7,)), dma((1,)), dma((1,)),
         ],
         compiler_params=pltpu.CompilerParams(vmem_limit_bytes=63 << 20, collective_id=1, has_side_effects=True),
         cost_estimate=pl.CostEstimate(
             flops=160 * seq * seq * PAIR, bytes_accessed=128 * seq * d_model, transcendentals=seq * seq * 4),
         name="last",
-    )(qkv, d_c, lse, d_mid, x, emb, w_qkv, u_seq, g_qkv, *w2_parts, *w1_parts, *wo_parts)
+    )(qkv, d_c, lse, d_mid, x, emb, w_qkv, u_seq, g_qkv, *w2_parts, *w1_sides, *wo_sides)[:7]
 
 
 def lin(z, y, x, c):
@@ -1055,22 +1122,23 @@
         order = [at(1 - first, second), at(1 - first, 1 - second), at(first, 1 - second), at(first, second)]
         column = jnp.stack(order) * 2 + core
 
-        def products(sides, by_left=False):
+        def both_cores(sides):
             lefts, rights = [], []
             for left, right in sides:
                 lefts += [left, send(left, other_core)]
                 rights += [right, send(right, other_core)]
-            return grad_products(column, lefts, rights, by_left)
-
-        away, mid, keep = products([(act_2, cot), (act_1, d_2)], True)
+            return lefts, rights
+
+        lefts, rights = both_cores([(act_2, cot), (act_1, d_2)])
+        away, mid, keep = grad_products(column, lefts, rights, True)
         d_2, away = lax.optimization_barrier((d_2, away))
         w2_parts = (send(away, swap_first), mid, keep)
         d_up_1, d_mid_1 = mlp_backward(d_2, h_1, up_1)
-        w1_parts = products([(m_2, d_up_2), (m_1, d_up_1)])
-        wo_parts = products([(d_mid_2, c_2), (d_mid_1, c_1)])
+        w1_sides = sum(both_cores([(m_2, d_up_2), (m_1, d_up_1)]), [])
+        wo_sides = sum(both_cores([(d_mid_2, c_2), (d_mid_1, c_1)]), [])
         d_c = dot_nt(d_mid_1, wo).astype(BF16)
         d_x, g_w1, g_w2, g_wo, g_q, g_k, g_v = last_call(
-            qkv_1, d_c, lse_1, d_mid_1, x_1, emb[:1], w_qkv, u_1_seq, g_qkv_2, w2_parts, w1_parts, wo_parts)
+            qkv_1, d_c, lse_1, d_mid_1, x_1, emb[:1], w_qkv, u_1_seq, g_qkv_2, w2_parts, w1_sides, wo_sides)
         return g_q, g_k, g_v, g_wo.T, g_w1, g_w2, d_x[None]
 
     return jax.shard_map(device_step, mesh=mesh,

time: 790 us -> 788 us (level)
  waiting for transfers between devices: 48.5 us -> 78.8 us
  Pallas kernels: 535 us -> 509 us
    ppermute x34, waiting for transfers between devices: 48.5 us -> 78.8 us  [send(): return lax.ppermute(value, AXES, pairs)]
    pallas_call x3 -> x1, Pallas kernels: 42.5 us -> 17.8 us  [grad_products(): pl.pallas_call(functools.partial(grad_kernel, by_left), grid_spec=pltpu.P...]
    unnamed x131 -> x125, local copies, waits for them, and re-layouts: 29.4 us -> 22.8 us
  transfers between devices with their start and end apart: 34 -> 34, of which waited for: 7 -> 9; matrix products, arithmetic and copies ran while one was open for 16% -> 16% of each run, Pallas kernels for 17% -> 14%
where the time goes in v1:
time: 788 us; the launch traced here: 778 us
  Pallas kernels  509 us (65%)
  matrix products  101 us (13%)
  waiting for transfers between devices  78.8 us (10%)
  other arithmetic  38.8 us (5%)
  local copies, waits for them, and re-layouts  25.7 us (3%)
  starting transfers between devices  22.8 us (3%)
    pallas_call x1, Pallas kernels, last_call(): pl.pallas_call(last_kernel, in_specs=[in_vmem] * 6 + [anywhere] * 22, out...  280 us
    pallas_call x1, Pallas kernels, first_call(): pl.pallas_call(first_kernel, in_specs=[in_vmem, anywhere] + [in_vmem] * 7...  119 us
    ppermute x34, waiting for transfers between devices, send(): return lax.ppermute(value, AXES, pairs)  78.8 us
    pallas_call x2, Pallas kernels, attn_bwd(): pl.pallas_call(attn_bwd_kernel, grid=(seq // BWD_ROWS,), in_specs=[rows(p...  61.2 us
    dot_general x7, matrix products, dot_nt(): lax.dot_general(a, b, (((1,), (1,)), ((), ())), preferred_element_type=F32)  50 us
    dot_general x7, matrix products, dot_nn(): lax.dot_general(a, b, (((1,), (0,)), ((), ())), preferred_element_type=F32)  43.4 us
    pallas_call x2, Pallas kernels, attn_fwd(): pl.pallas_call(attn_fwd_kernel, grid=(seq // rows,), in_specs=[pl.BlockSp...  30.7 us
    unnamed x125, local copies, waits for them, and re-layouts  22.8 us
  transfers between devices with their start and end apart: 34, of which 9 were waited for; matrix products, arithmetic and copies ran while one was open for 16% of the time, Pallas kernels for 14%

profile of v1, /device:TPU:17, one launch (start us, length us, event | category | flops | bytes accessed | tf_op | source)
XLA Modules:
  0.0 777.7 jit_solution(6189070790241729629)
XLA Ops:
  2.0 119.1 %first.1 = (bf16[512,1024]{1,0:T(8,128)(2,1)}, f32[4,2048]{1,0:T(4,128)}, bf16[2048,1024]{1,0:T(8,128)(2,1)}, bf16[512,1024]{1,0:T(8,128)(2,1)}, bf16[4,256,1024...) custom-call(bf16[2048,1024]{1,0:T(8,128)(2,1)} %bitcast.51, ...), custom_call_target="tpu_custom_call" | custom-call | flops 34359738368 | bytes 134217728 | tf_op jit(solution)/shard_map/first/pallas_call | solution.py:412
  122.7 4.2 fusion.32
  128.1 9.7 %fusion.13 = (bf16[512,4096]{1,0:T(8,128)(2,1)}, bf16[512,4096]{1,0:T(8,128)(2,1)S(1)}) fusion(bf16[512,1024]{1,0:T(8,128)(2,1)} %fusion.33.refs_2_, bf16[1024,4096]{1,0:T(8,128)(2,1)S(1)} %bitcast.67), kind=kOutput, calls=%fused_computation.25 | convolution fusion | flops 4318035968 | bytes 17825792 | tf_op jit(solution)/shard_map/dot_general | solution.py:36
  137.9 5.4 fusion.34
  144.1 23.9 %collective-permute-done = bf16[512,1024]{1,0:T(8,128)(2,1)S(1)} collective-permute-done((bf16[512,1024]{1,0:T(8,128)(2,1)S(1)}, bf16[512,1024]{1,0:T(8,128)(2,1)S(1)}, u32[]{:S(2)}, u32[]{:S(2)}) %collective-permute-start) | collective-permute-done | bytes 1048608 | tf_op jit(solution)/shard_map/ppermute | solution.py:1002
  170.2 4.1 multiply_convert_fusion.1.u_ref
  177.1 11.4 %multiply_convert_fusion = bf16[2048,1024]{1,0:T(8,128)(2,1)S(1)} fusion(f32[2048]{0:T(1024)S(1)} %add_rsqrt_fusion, f32[1024]{0:T(1024)S(1)} %bitcast.44, bf16[512,1024]{1,0:T(8,128)(2,1)S(1)} %get-tuple-element.85, bf16[512,1024]{1,0:T(8,128)(2,1)S(1)} %get-tuple-element.84, bf16[512,1024]{1,0:T(8,128)(2,1)S(1)} %get-tuple-element.83, ...), kind=kLoop, calls=%fused_computation.34 | loop fusion | flops 23068672 | bytes 8400896 | tf_op jit(solution)/shard_map/convert_element_type | solution.py:1080
  190.5 6.2 convolution_convert_fusion.4.q_ref.k_ref.v_ref
  196.7 15.2 %attn_fwd.3 = (bf16[2048,128]{1,0:T(8,128)(2,1)}, f32[2,2048]{1,0:T(2,128)}) custom-call(bf16[2048,768]{1,0:T(8,128)(2,1)} %convolution_convert_fusion.4.q_ref.k_ref.v_ref, bf16[2048,768]{1,0:T(8,128)(2,1)} %convolution_convert_fusion.4.q_ref.k_ref.v_ref, bf16[2048,768]{1,0:T(8,128)(2,1)} %convolution_convert_fusion.4.q_ref.k_ref.v_ref), custom_call_target="tpu_custom_call" | custom-call | flops 8589934592 | bytes 2097152 | tf_op jit(solution)/shard_map/attn_fwd/pallas_call | solution.py:57
  211.9 15.5 %attn_fwd.2 = (bf16[2048,128]{1,0:T(8,128)(2,1)}, f32[2,2048]{1,0:T(2,128)}) custom-call(bf16[2048,768]{1,0:T(8,128)(2,1)} %convolution_convert_fusion.4.q_ref.k_ref.v_ref, bf16[2048,768]{1,0:T(8,128)(2,1)} %convolution_convert_fusion.4.q_ref.k_ref.v_ref, bf16[2048,768]{1,0:T(8,128)(2,1)} %convolution_convert_fusion.4.q_ref.k_ref.v_ref), custom_call_target="tpu_custom_call" | custom-call | flops 8589934592 | bytes 2097152 | tf_op jit(solution)/shard_map/attn_fwd/pallas_call | solution.py:57
  231.0 3.6 collective-permute-done.3
  238.0 2.3 collective-permute-done.6
  243.9 11.7 %fusion.21 = (bf16[512,4096]{1,0:T(8,128)(2,1)}, bf16[512,4096]{1,0:T(8,128)(2,1)S(1)}) fusion(bf16[512,1024]{1,0:T(8,128)(2,1)S(1)} %fusion.30.refs_0_, bf16[1024,4096]{1,0:T(8,128)(2,1)} %get-tuple-element.37), kind=kOutput, calls=%fused_computation.33 | convolution fusion | flops 4318035968 | bytes 17825792 | tf_op jit(solution)/shard_map/dot_general | solution.py:36
  255.6 12.9 %fusion.4.refs_4_ = bf16[512,4096]{1,0:T(8,128)(2,1)} fusion(bf16[512,4096]{1,0:T(8,128)(2,1)S(1)} %get-tuple-element.135, bf16[512,1024]{1,0:T(8,128)(2,1)} %get-tuple-element.33.refs_16_, bf16[4096,1024]{1,0:T(8,128)(2,1)S(1)} %bitcast.59), kind=kOutput, calls=%fused_computation.16 | convolution fusion | flops 4343201792 | bytes 17825792 | tf_op jit(solution)/shard_map/dot_general | solution.py:32
  268.5 9.3 %fusion.31 = (f32[512]{0:T(512)S(1)}, bf16[512,1024]{1,0:T(8,128)(2,1)S(1)}) fusion(bf16[512,1024]{1,0:T(8,128)(2,1)S(1)} %get-tuple-element.130, bf16[512,4096]{1,0:T(8,128)(2,1)} %fusion.4.refs_4_, bf16[1024,4096]{1,0:T(8,128)(2,1)} %get-tuple-element.37), kind=kOutput, calls=%fused_computation.72 | convolution fusion | flops 4297588224 | bytes 14682112 | tf_op jit(solution)/shard_map/dot_general | solution.py:32
  285.2 3.3 collective-permute-start.15
  291.5 30.5 %attn_bwd.2 = bf16[2048,384]{1,0:T(8,128)(2,1)} custom-call(bf16[2048,768]{1,0:T(8,128)(2,1)} %convolution_convert_fusion.4.q_ref.k_ref.v_ref, bf16[2048,768]{1,0:T(8,128)(2,1)} %convolution_convert_fusion.4.q_ref.k_ref.v_ref, bf16[2048,768]{1,0:T(8,128)(2,1)} %convolution_convert_fusion.4.q_ref.k_ref.v_ref, bf16[2048,128]{1,0:T(8,128)(2,1)} %pad_maximum_fusion.1.do_ref, ...), custom_call_target="tpu_custom_call" | custom-call | flops 21474836480 | bytes 3670016 | tf_op jit(solution)/shard_map/attn_bwd/pallas_call | solution.py:102
  322.0 2.4 broadcast_select_fusion.38
  329.1 30.7 %attn_bwd.3 = bf16[2048,384]{1,0:T(8,128)(2,1)} custom-call(bf16[2048,768]{1,0:T(8,128)(2,1)} %convolution_convert_fusion.4.q_ref.k_ref.v_ref, bf16[2048,768]{1,0:T(8,128)(2,1)} %convolution_convert_fusion.4.q_ref.k_ref.v_ref, bf16[2048,768]{1,0:T(8,128)(2,1)} %convolution_convert_fusion.4.q_ref.k_ref.v_ref, bf16[2048,128]{1,0:T(8,128)(2,1)} %pad_maximum_fusion.2.do_ref, ...), custom_call_target="tpu_custom_call" | custom-call | flops 21474836480 | bytes 3670016 | tf_op jit(solution)/shard_map/attn_bwd/pallas_call | solution.py:102
  365.2 7.9 %collective-permute-done.18 = bf16[512,384]{1,0:T(8,128)(2,1)S(1)} collective-permute-done((bf16[512,384]{1,0:T(8,128)(2,1)S(1)}, bf16[512,384]{1,0:T(8,128)(2,1)S(1)}, u32[]{:S(2)}, u32[]{:S(2)}) %collective-permute-start.18) | collective-permute-done | bytes 393248 | tf_op jit(solution)/shard_map/ppermute | solution.py:1002
  373.1 7.8 %collective-permute-done.19 = bf16[512,384]{1,0:T(8,128)(2,1)S(1)} collective-permute-done((bf16[512,384]{1,0:T(8,128)(2,1)S(1)}, bf16[512,384]{1,0:T(8,128)(2,1)S(1)}, u32[]{:S(2)}, u32[]{:S(2)}) %collective-permute-start.19) | collective-permute-done | bytes 393248 | tf_op jit(solution)/shard_map/ppermute | solution.py:1002
  383.3 3.6 multiply_reduce_fusion.2
  389.4 4.9 convolution_convert_fusion.5.qkv_ref
  395.0 5.0 fusion.46
  402.0 17.8 %grad.1 = (f32[4,256,1024]{2,1,0:T(8,128)}, f32[4,128,1024]{2,1,0:T(8,128)}, f32[4,128,1024]{2,1,0:T(8,128)}) custom-call(s32[4]{0:T(128)} %fusion.41._, bf16[512,4096]{1,0:T(8,128)(2,1)} %get-tuple-element.134.refs_0_.refs_1_.refs_2_.refs_3_, bf16[512,4096]{1,0:T(8,128)(2,1)} %get-tuple-element.134.refs_0_.refs_1_.refs_2_.refs_3_, ...), custom_call_target="tpu_custom_call" | custom-call | flops 8589934592 | bytes 27262976 | tf_op jit(solution)/shard_map/grad/pallas_call | solution.py:480
  419.9 12.7 %fusion.7.refs_6_ = bf16[512,4096]{1,0:T(8,128)(2,1)S(1)} fusion(bf16[512,4096]{1,0:T(8,128)(2,1)} %copy-done.36, bf16[512,1024]{1,0:T(8,128)(2,1)} %fusion.26.refs_18_, bf16[4096,1024]{1,0:T(8,128)(2,1)} %bitcast.53), kind=kOutput, calls=%fused_computation.19 | convolution fusion | flops 4343201792 | bytes 17825792 | tf_op jit(solution)/shard_map/dot_general | solution.py:32
  433.7 2.4 fusion.47
  437.4 8.0 %fusion.35 = (f32[512]{0:T(512)S(1)}, bf16[512,1024]{1,0:T(8,128)(2,1)S(1)}) fusion(bf16[512,1024]{1,0:T(8,128)(2,1)S(1)} %copy-done.2, bf16[512,4096]{1,0:T(8,128)(2,1)S(1)} %fusion.7.refs_6_, bf16[1024,4096]{1,0:T(8,128)(2,1)} %get-tuple-element.37), kind=kOutput, calls=%fused_computation.76 | convolution fusion | flops 4297588224 | bytes 14682112 | tf_op jit(solution)/shard_map/dot_general | solution.py:32
  451.8 29.3 %collective-permute-done.25.r2_ref = f32[4,256,1024]{2,1,0:T(8,128)} collective-permute-done((f32[4,256,1024]{2,1,0:T(8,128)}, f32[4,256,1024]{2,1,0:T(8,128)}, u32[]{:S(2)}, u32[]{:S(2)}) %collective-permute-start.25) | collective-permute-done | bytes 4194336 | tf_op jit(solution)/shard_map/ppermute | solution.py:1002
  481.1 279.7 %last.1 = (bf16[2048,1024]{1,0:T(8,128)(2,1)}, f32[1024,1024]{1,0:T(8,128)}, f32[1024,1024]{1,0:T(8,128)}, f32[1024,256]{1,0:T(8,128)}, f32[1024,256]{1,0:T(8,12...) custom-call(bf16[2048,768]{1,0:T(8,128)(2,1)} %convolution_convert_f, ...), custom_call_target="tpu_custom_call" | custom-call | flops 85899345920 | bytes 268435456 | tf_op jit(solution)/shard_map/last/pallas_call | solution.py:936
  760.9 2.7 copy.22
  763.6 2.4 copy.66
  (230 shorter events, 70.1 us)
Async XLA Ops:
  143.3 24.7 %collective-permute-start = (bf16[512,1024]{1,0:T(8,128)(2,1)S(1)}, bf16[512,1024]{1,0:T(8,128)(2,1)S(1)}, u32[]{:S(2)}, u32[]{:S(2)}) collective-permute-start(bf16[512,1024]{1,0:T(8,128)(2,1)S(1)} %fusion.34), channel_id=1, source_target_pairs={{0,8},{1,9},{2,10},{3,11},{4,12},{5,13},{6,14},{7,15},{8,0},{9,1},... | collective-permute-start | bytes 3145736 | tf_op jit(solution)/shard_map/ppermute | solution.py:1002
  143.4 30.9 %collective-permute-start.2 = (bf16[512,1024]{1,0:T(8,128)(2,1)S(1)}, bf16[512,1024]{1,0:T(8,128)(2,1)S(1)}, u32[]{:S(2)}, u32[]{:S(2)}) collective-permute-start(bf16[512,1024]{1,0:T(8,128)(2,1)S(1)} %fusion.34), channel_id=1, source_target_pairs={{0,1},{1,0},{2,3},{3,2},{4,5},{5,4},{6,7},{7,6},{8,9},{9,8},{10,11... | collective-permute-start | bytes 3145736 | tf_op jit(solution)/shard_map/ppermute | solution.py:1002
  143.6 292.6 %collective-permute-start.27 = (bf16[512,1024]{1,0:T(8,128)(2,1)}, bf16[512,1024]{1,0:T(8,128)(2,1)}, u32[]{:S(2)}, u32[]{:S(2)}) collective-permute-start(bf16[512,1024]{1,0:T(8,128)(2,1)} %fusion.33.refs_2_), channel_id=1, source_target_pairs={{0,1},{1,0},{2,3},{3,2},{4,5},{5,4},{6,7},{7,6},{8,9},{9,8},{10,11... | collective-permute-start | bytes 3145736 | tf_op jit(solution)/shard_map/ppermute | solution.py:1002
  144.0 257.0 %collective-permute-start.23 = (bf16[512,1024]{1,0:T(8,128)(2,1)}, bf16[512,1024]{1,0:T(8,128)(2,1)}, u32[]{:S(2)}, u32[]{:S(2)}) collective-permute-start(bf16[512,1024]{1,0:T(8,128)(2,1)} %get-tuple-element.33.refs_16_), channel_id=1, source_target_pairs={{0,1},{1,0},{2,3},{3,2},{4,5},{5,4},{6,7},{7,6},{8,9},{9,8},{10,11... | collective-permute-start | bytes 3145736 | tf_op jit(solution)/shard_map/ppermute | solution.py:1002
  168.0 6.3 collective-permute-start.1
  228.7 5.9 collective-permute-start.3
  228.8 7.5 collective-permute-start.4
  230.1 6.4 collective-permute-start.5
  234.6 5.7 collective-permute-start.6
  236.3 5.0 collective-permute-start.7
  236.5 4.8 collective-permute-start.8
  281.1 4.1 collective-permute-start.10
  282.1 6.5 collective-permute-start.11
  283.4 7.1 collective-permute-start.9
  285.2 39.2 %collective-permute-start.15 = (bf16[512,128]{1,0:T(8,128)(2,1)S(1)}, bf16[512,128]{1,0:T(8,128)(2,1)S(1)}, u32[]{:S(2)}, u32[]{:S(2)}) collective-permute-start(bf16[512,128]{1,0:T(8,128)(2,1)S(1)} %get-tuple-element.107), channel_id=1, source_target_pairs={{0,9},{1,8},{2,11},{3,10},{4,13},{5,12},{6,15},{7,14},{8,1},{9,0},... | collective-permute-start | bytes 393224 | tf_op jit(solution)/shard_map/ppermute | solution.py:1002
  288.5 37.0 %collective-permute-start.16 = (bf16[512,128]{1,0:T(8,128)(2,1)}, bf16[512,128]{1,0:T(8,128)(2,1)}, u32[]{:S(2)}, u32[]{:S(2)}) collective-permute-start(bf16[512,128]{1,0:T(8,128)(2,1)} %get-tuple-element.67), channel_id=1, source_target_pairs={{0,8},{1,9},{2,10},{3,11},{4,12},{5,13},{6,14},{7,15},{8,0},{9,1},... | collective-permute-start | bytes 393224 | tf_op jit(solution)/shard_map/ppermute | solution.py:1002
  290.6 36.4 %collective-permute-start.17 = (bf16[512,128]{1,0:T(8,128)(2,1)S(1)}, bf16[512,128]{1,0:T(8,128)(2,1)}, u32[]{:S(2)}, u32[]{:S(2)}) collective-permute-start(bf16[512,128]{1,0:T(8,128)(2,1)S(1)} %get-tuple-element.101), channel_id=1, source_target_pairs={{0,1},{1,0},{2,3},{3,2},{4,5},{5,4},{6,7},{7,6},{8,9},{9,8},{10,11... | collective-permute-start | bytes 393224 | tf_op jit(solution)/shard_map/ppermute | solution.py:1002
  325.1 36.5 %collective-permute-start.12 = (bf16[512,384]{1,0:T(8,128)(2,1)}, bf16[512,384]{1,0:T(8,128)(2,1)S(1)}, u32[]{:S(2)}, u32[]{:S(2)}) collective-permute-start(bf16[512,384]{1,0:T(8,128)(2,1)} %get-tuple-element.100), channel_id=1, source_target_pairs={{0,9},{1,8},{2,11},{3,10},{4,13},{5,12},{6,15},{7,14},{8,1},{9,0},... | collective-permute-start | bytes 1179656 | tf_op jit(solution)/shard_map/ppermute | solution.py:1002
  325.5 36.4 %collective-permute-start.13 = (bf16[512,384]{1,0:T(8,128)(2,1)}, bf16[512,384]{1,0:T(8,128)(2,1)}, u32[]{:S(2)}, u32[]{:S(2)}) collective-permute-start(bf16[512,384]{1,0:T(8,128)(2,1)} %get-tuple-element.70), channel_id=1, source_target_pairs={{0,8},{1,9},{2,10},{3,11},{4,12},{5,13},{6,14},{7,15},{8,0},{9,1},... | collective-permute-start | bytes 1179656 | tf_op jit(solution)/shard_map/ppermute | solution.py:1002
  326.9 36.3 %collective-permute-start.14 = (bf16[512,384]{1,0:T(8,128)(2,1)S(1)}, bf16[512,384]{1,0:T(8,128)(2,1)}, u32[]{:S(2)}, u32[]{:S(2)}) collective-permute-start(bf16[512,384]{1,0:T(8,128)(2,1)S(1)} %get-tuple-element.99), channel_id=1, source_target_pairs={{0,1},{1,0},{2,3},{3,2},{4,5},{5,4},{6,7},{7,6},{8,9},{9,8},{10,11... | collective-permute-start | bytes 1179656 | tf_op jit(solution)/shard_map/ppermute | solution.py:1002
  361.6 11.5 %collective-permute-start.18 = (bf16[512,384]{1,0:T(8,128)(2,1)S(1)}, bf16[512,384]{1,0:T(8,128)(2,1)S(1)}, u32[]{:S(2)}, u32[]{:S(2)}) collective-permute-start(bf16[512,384]{1,0:T(8,128)(2,1)S(1)} %get-tuple-element.95), channel_id=1, source_target_pairs={{0,9},{1,8},{2,11},{3,10},{4,13},{5,12},{6,15},{7,14},{8,1},{9,0},... | collective-permute-start | bytes 1179656 | tf_op jit(solution)/shard_map/ppermute | solution.py:1002
  361.9 18.9 %collective-permute-start.19 = (bf16[512,384]{1,0:T(8,128)(2,1)S(1)}, bf16[512,384]{1,0:T(8,128)(2,1)S(1)}, u32[]{:S(2)}, u32[]{:S(2)}) collective-permute-start(bf16[512,384]{1,0:T(8,128)(2,1)S(1)} %get-tuple-element.96), channel_id=1, source_target_pairs={{0,8},{1,9},{2,10},{3,11},{4,12},{5,13},{6,14},{7,15},{8,0},{9,1},... | collective-permute-start | bytes 1179656 | tf_op jit(solution)/shard_map/ppermute | solution.py:1002
  363.2 18.5 %collective-permute-start.20 = (bf16[512,384]{1,0:T(8,128)(2,1)S(1)}, bf16[512,384]{1,0:T(8,128)(2,1)S(1)}, u32[]{:S(2)}, u32[]{:S(2)}) collective-permute-start(bf16[512,384]{1,0:T(8,128)(2,1)S(1)} %get-tuple-element.94), channel_id=1, source_target_pairs={{0,1},{1,0},{2,3},{3,2},{4,5},{5,4},{6,7},{7,6},{8,9},{9,8},{10,11... | collective-permute-start | bytes 1179656 | tf_op jit(solution)/shard_map/ppermute | solution.py:1002
  373.1 28.4 %collective-permute-start.22 = (bf16[512,4096]{1,0:T(8,128)(2,1)}, bf16[512,4096]{1,0:T(8,128)(2,1)}, u32[]{:S(2)}, u32[]{:S(2)}) collective-permute-start(bf16[512,4096]{1,0:T(8,128)(2,1)} %get-tuple-element.136.refs_8_.refs_9_.refs_10_.refs_11_), channel_id=1, source_target_pairs={{0,1},{1,0},{2,3},{3,2},{4,5},{5,4},{6,7},{7,6},{8,9},{9,8},{10,11... | collective-permute-start | bytes 12582920 | tf_op jit(solution)/shard_map/ppermute | solution.py:1002
  380.8 20.6 %collective-permute-start.21 = (bf16[512,4096]{1,0:T(8,128)(2,1)}, bf16[512,4096]{1,0:T(8,128)(2,1)}, u32[]{:S(2)}, u32[]{:S(2)}) collective-permute-start(bf16[512,4096]{1,0:T(8,128)(2,1)} %get-tuple-element.134.refs_0_.refs_1_.refs_2_.refs_3_), channel_id=1, source_target_pairs={{0,1},{1,0},{2,3},{3,2},{4,5},{5,4},{6,7},{7,6},{8,9},{9,8},{10,11... | collective-permute-start | bytes 12582920 | tf_op jit(solution)/shard_map/ppermute | solution.py:1002
  388.6 12.5 %collective-permute-start.24 = (bf16[512,1024]{1,0:T(8,128)(2,1)}, bf16[512,1024]{1,0:T(8,128)(2,1)S(1)}, u32[]{:S(2)}, u32[]{:S(2)}) collective-permute-start(bf16[512,1024]{1,0:T(8,128)(2,1)} %fusion.26.refs_18_), channel_id=1, source_target_pairs={{0,1},{1,0},{2,3},{3,2},{4,5},{5,4},{6,7},{7,6},{8,9},{9,8},{10,11... | collective-permute-start | bytes 3145736 | tf_op jit(solution)/shard_map/ppermute | solution.py:1002
  401.0 36.3 %collective-permute-start.33 = (bf16[512,1024]{1,0:T(8,128)(2,1)}, bf16[512,1024]{1,0:T(8,128)(2,1)}, u32[]{:S(2)}, u32[]{:S(2)}) collective-permute-start(bf16[512,1024]{1,0:T(8,128)(2,1)} %get-tuple-element.35.refs_14_), channel_id=1, source_target_pairs={{0,1},{1,0},{2,3},{3,2},{4,5},{5,4},{6,7},{7,6},{8,9},{9,8},{10,11... | collective-permute-start | bytes 3145736 | tf_op jit(solution)/shard_map/ppermute | solution.py:1002
  401.0 49.6 %collective-permute-start.28 = (bf16[512,4096]{1,0:T(8,128)(2,1)}, bf16[512,4096]{1,0:T(8,128)(2,1)}, u32[]{:S(2)}, u32[]{:S(2)}) collective-permute-start(bf16[512,4096]{1,0:T(8,128)(2,1)} %fusion.4.refs_4_), channel_id=1, source_target_pairs={{0,1},{1,0},{2,3},{3,2},{4,5},{5,4},{6,7},{7,6},{8,9},{9,8},{10,11... | collective-permute-start | bytes 12582920 | tf_op jit(solution)/shard_map/ppermute | solution.py:1002
  432.6 19.2 %collective-permute-start.29 = (bf16[512,4096]{1,0:T(8,128)(2,1)S(1)}, bf16[512,4096]{1,0:T(8,128)(2,1)}, u32[]{:S(2)}, u32[]{:S(2)}) collective-permute-start(bf16[512,4096]{1,0:T(8,128)(2,1)S(1)} %fusion.7.refs_6_), channel_id=1, source_target_pairs={{0,1},{1,0},{2,3},{3,2},{4,5},{5,4},{6,7},{7,6},{8,9},{9,8},{10,11... | collective-permute-start | bytes 12582920 | tf_op jit(solution)/shard_map/ppermute | solution.py:1002
  433.1 48.0 %collective-permute-start.25 = (f32[4,256,1024]{2,1,0:T(8,128)}, f32[4,256,1024]{2,1,0:T(8,128)}, u32[]{:S(2)}, u32[]{:S(2)}) collective-permute-start(f32[4,256,1024]{2,1,0:T(8,128)} %get-tuple-element.45), channel_id=1, source_target_pairs={{0,2},{1,5},{2,0},{3,7},{4,6},{5,1},{6,4},{7,3},{8,10},{9,13},{10,... | collective-permute-start | bytes 12582920 | tf_op jit(solution)/shard_map/ppermute | solution.py:1002
  436.2 11.3 %collective-permute-start.30 = (bf16[512,1024]{1,0:T(8,128)(2,1)S(1)}, bf16[512,1024]{1,0:T(8,128)(2,1)S(1)}, u32[]{:S(2)}, u32[]{:S(2)}) collective-permute-start(bf16[512,1024]{1,0:T(8,128)(2,1)S(1)} %fusion.24.refs_8_), channel_id=1, source_target_pairs={{0,1},{1,0},{2,3},{3,2},{4,5},{5,4},{6,7},{7,6},{8,9},{9,8},{10,11... | collective-permute-start | bytes 3145736 | tf_op jit(solution)/shard_map/ppermute | solution.py:1002
  437.3 10.7 %collective-permute-start.26 = (bf16[512,1024]{1,0:T(8,128)(2,1)S(1)}, bf16[512,1024]{1,0:T(8,128)(2,1)S(1)}, u32[]{:S(2)}, u32[]{:S(2)}) collective-permute-start(bf16[512,1024]{1,0:T(8,128)(2,1)S(1)} %copy-done.15), channel_id=1, source_target_pairs={{0,1},{1,0},{2,3},{3,2},{4,5},{5,4},{6,7},{7,6},{8,9},{9,8},{10,11... | collective-permute-start | bytes 3145736 | tf_op jit(solution)/shard_map/ppermute | solution.py:1002
  (47 other events, 627.1 us)

commit v2 on v1

--- a/solution.py
+++ b/solution.py
@@ -14,7 +14,6 @@
 SCALE = HEAD_DIM ** -0.5
 EXP2_SCALE = SCALE * math.log2(math.e)
 PAIR = 2 * HEAD_DIM
-FWD_ROWS = 512
 BWD_ROWS = 256
 KEYS = 256
 INTERPRET = False
@@ -38,86 +37,6 @@
 
 def dot_tn(a, b):
     return lax.dot_general(a, b, (((0,), (0,)), ((), ())), preferred_element_type=F32)
-
-
-def attn_fwd_kernel(q_ref, k_ref, v_ref, o_ref, lse_ref, vt_ref, *e_refs):
-    @pl.when(pl.program_id(0) == 0)
-    def _():
-        vt_ref[...] = v_ref[...].T
-
-    outs, sums = attend_rows(q_ref[...], k_ref, vt_ref, e_refs)
-    o_ref[...] = jnp.concatenate(outs, axis=0).T.astype(BF16)
-    for head in range(2):
-        lse_ref[head:head + 1, :] = sums[head]
-
-
-def attn_fwd(qkv, pair):
-    seq = qkv.shape[0]
-    rows = min(FWD_ROWS, seq)
-    return pl.pallas_call(
-        attn_fwd_kernel,
-        grid=(seq // rows,),
-        in_specs=[
-            pl.BlockSpec((rows, PAIR), lambda i: (i, pair)),
-            pl.BlockSpec((seq, PAIR), lambda i: (0, 2 + pair)),
-            pl.BlockSpec((seq, PAIR), lambda i: (0, 4 + pair)),
-        ],
-        out_specs=[
-            pl.BlockSpec((rows, PAIR), lambda i: (i, 0)),
-            pl.BlockSpec((2, rows), lambda i: (0, i)),
-        ],
-        out_shape=[jax.ShapeDtypeStruct((seq, PAIR), BF16), jax.ShapeDtypeStruct((2, seq), F32)],
-        scratch_shapes=[pltpu.VMEM((PAIR, seq), BF16)] + [pltpu.VMEM((seq, rows), F32)] * 2,
-        compiler_params=pltpu.CompilerParams(vmem_limit_bytes=60 << 20),
-        cost_estimate=pl.CostEstimate(
-            flops=16 * seq * seq * PAIR, bytes_accessed=8 * seq * PAIR, transcendentals=seq * seq * 2),
-        interpret=INTERPRET,
-        name="attn_fwd",
-    )(qkv, qkv, qkv)
-
-
-def attn_bwd_kernel(q_ref, k_ref, v_ref, do_ref, lse_ref, out_ref, kt_ref, dk_acc, dv_acc, p_cat, ds_cat):
-    step = pl.program_id(0)
-
-    @pl.when(step == 0)
-    def _():
-        kt_ref[...] = k_ref[...].T
-        dk_acc[...] = jnp.zeros_like(dk_acc)
-        dv_acc[...] = jnp.zeros_like(dv_acc)
-
-    block = q_ref.shape[0]
-    out_ref[pl.ds(pl.multiple_of(step * block, block), block), :PAIR] = backward_rows(
-        q_ref[...], do_ref[...], lse_ref[...], k_ref, v_ref, kt_ref, p_cat, ds_cat, dk_acc, dv_acc)
-
-    @pl.when(step == pl.num_programs(0) - 1)
-    def _():
-        out_ref[:, PAIR:2 * PAIR] = (dk_acc[...] * SCALE).astype(BF16)
-        out_ref[:, 2 * PAIR:] = dv_acc[...].astype(BF16)
-
-
-def attn_bwd(qkv, d_context, lse, pair):
-    seq = qkv.shape[0]
-    full = lambda column: pl.BlockSpec((seq, PAIR), lambda i: (0, column))
-    rows = lambda column: pl.BlockSpec((BWD_ROWS, PAIR), lambda i: (i, column))
-    return pl.pallas_call(
-        attn_bwd_kernel,
-        grid=(seq // BWD_ROWS,),
-        in_specs=[rows(pair), full(2 + pair), full(4 + pair), rows(0), pl.BlockSpec((2, BWD_ROWS), lambda i: (0, i))],
-        out_specs=pl.BlockSpec((seq, 3 * PAIR), lambda i: (0, 0)),
-        out_shape=jax.ShapeDtypeStruct((seq, 3 * PAIR), BF16),
-        scratch_shapes=[
-            pltpu.VMEM((PAIR, seq), BF16),
-            pltpu.VMEM((seq, PAIR), F32),
-            pltpu.VMEM((seq, PAIR), F32),
-            pltpu.VMEM((seq, 2 * BWD_ROWS), BF16),
-            pltpu.VMEM((seq, 2 * BWD_ROWS), BF16),
-        ],
-        compiler_params=pltpu.CompilerParams(vmem_limit_bytes=60 << 20),
-        cost_estimate=pl.CostEstimate(
-            flops=40 * seq * seq * PAIR, bytes_accessed=14 * seq * PAIR, transcendentals=seq * seq * 2),
-        interpret=INTERPRET,
-        name="attn_bwd",
-    )(qkv, qkv, qkv, d_context, lse)
 
 
 def attend_rows(q, k_ref, v_t, e_refs):
@@ -446,6 +365,332 @@
     )(x, cot, emb, w_q, w_k, w_v, w_o, w_1, w_2)
 
 
+def unit_rows(values, emb):
+    values = values.astype(F32) + emb
+    return (values * lax.rsqrt(jnp.mean(values * values, axis=-1, keepdims=True) + EPS_NORM)).astype(BF16)
+
+
+def forward_kernel(x_ref, emb_ref, xs1_ref, wqkv_ref,
+                   c_ref, lse_ref, u2_ref, qkv2_ref, u1_ref, qkv1_ref,
+                   w_s, blocks, u_s, qkv_s, x1_s, u1_s, qkv1_s, v_t, e_a, e_b, c_buf, lse_s,
+                   local_sem, first_sem, out_sem, x_send, x_recv, c_send, c_recv):
+    seq = xs1_ref.shape[0]
+    blk = seq // 4
+    head_cols = 2 * PAIR
+    here = Place()
+    z, core, role = here.z, here.c, here.role
+
+    def span(index, count):
+        return pl.ds(pl.multiple_of(index * count, count), count)
+
+    w_load = pltpu.make_async_copy(wqkv_ref.at[:, span(role, 3 * head_cols)], w_s, local_sem.at[0])
+    w_load.start()
+    x1_load = [pltpu.make_async_copy(xs1_ref.at[i * blk:(i + 1) * blk, :], x1_s.at[i % 2], first_sem.at[i % 2]) for i in range(4)]
+    x1_load[0].start()
+    here.meet()
+    partner, across = here.device(c=1 - core), here.device(z=here.z_by[1])
+    role_side, role_over = z % 2 * 2 + 1 - core, (1 - z % 2) * 2 + core
+    role_last = (1 - z % 2) * 2 + 1 - core
+
+    def x_copy(n, src, slot, device):
+        return pltpu.make_async_remote_copy(
+            src_ref=src, dst_ref=blocks.at[slot], send_sem=x_send.at[n], recv_sem=x_recv.at[n],
+            device_id=device, device_id_type=MESH)
+
+    over, side = x_copy(0, x_ref, 0, across), x_copy(1, x_ref, 1, partner)
+    last = x_copy(2, blocks.at[0], 2, partner)
+    over.start()
+    side.start()
+
+    def project(src, at_role):
+        rows = span(at_role, blk)
+        unit = unit_rows(src, emb_ref[1:2, :])
+        u_s[rows, :] = unit
+        qkv_s[rows, :] = dot_nn(unit, w_s[...]).astype(BF16)
+
+    w_load.wait()
+    project(x_ref[...], role)
+    side.wait_recv()
+    project(blocks[1], role_side)
+
+    stores = []
+    for i in range(4):
+        if i < 3:
+            x1_load[i + 1].start()
+        x1_load[i].wait()
+        if i >= 2:
+            for copy in stores[i - 2]:
+                copy.wait()
+        unit = unit_rows(x1_s[i % 2], emb_ref[0:1, :])
+        u1_s[i % 2] = unit
+        qkv1_s[i % 2] = dot_nn(unit, w_s[...]).astype(BF16)
+        stores.append([pltpu.make_async_copy(u1_s.at[i % 2], u1_ref.at[i * blk:(i + 1) * blk, :], out_sem.at[i % 2]),
+                       pltpu.make_async_copy(qkv1_s.at[i % 2], qkv1_ref.at[i * blk:(i + 1) * blk, :], out_sem.at[2 + i % 2])])
+        for copy in stores[i]:
+            copy.start()
+
+    over.wait_recv()
+    last.start()
+    project(blocks[0], role_over)
+    last.wait_recv()
+    project(blocks[2], role_last)
+    keep_u = pltpu.make_async_copy(u_s, u2_ref, local_sem.at[1])
+    keep_qkv = pltpu.make_async_copy(qkv_s, qkv2_ref, local_sem.at[2])
+    keep_u.start()
+    keep_qkv.start()
+
+    member = [here.device(z=z // 2 * 2 + i // 2, c=i % 2) for i in range(4)]
+
+    def c_copy(j, i):
+        src = c_buf.at[j, i * blk:(i + 1) * blk, :]
+        dst = c_ref.at[:, pl.ds(pl.multiple_of((role * 2 + j) * PAIR, PAIR), PAIR)]
+        remote = pltpu.make_async_remote_copy(
+            src_ref=src, dst_ref=dst, send_sem=c_send.at[j * 4 + i], recv_sem=c_recv.at[j * 4 + role],
+            device_id=member[i], device_id_type=MESH)
+        return remote, pltpu.make_async_copy(src, dst, c_recv.at[j * 4 + role])
+
+    def send_context(j, i):
+        remote, local = c_copy(j, i)
+        pl.when(role == i)(local.start)
+        pl.when(role != i)(remote.start)
+
+    for j in range(2):
+        v_t[...] = qkv_s[:, (4 + j) * PAIR:(5 + j) * PAIR].T
+        k_view = qkv_s.at[:, (2 + j) * PAIR:(3 + j) * PAIR]
+        for i in range(4):
+            if i or j:
+                send_context(j if i else 0, i - 1 if i else 3)
+            rows = slice(i * blk, (i + 1) * blk)
+            outs, sums = attend_rows(qkv_s[rows, j * PAIR:(j + 1) * PAIR], k_view, v_t, (e_a, e_b))
+            c_buf[j, rows, :] = jnp.concatenate(outs, axis=0).T.astype(BF16)
+            for head in range(2):
+                lse_s[2 * j + head:2 * j + head + 1, rows] = sums[head]
+    lse_ref[...] = lse_s[...]
+    send_context(1, 3)
+    for j in range(2):
+        for i in range(4):
+            pltpu.make_async_copy(c_buf.at[j, :blk, :], c_ref.at[:, :PAIR], c_recv.at[j * 4 + i]).wait()
+            pl.when(role != i)(c_copy(j, i)[0].wait_send)
+    for copy in (over, side, last):
+        copy.wait_send()
+    for group in stores[2:]:
+        for copy in group:
+            copy.wait()
+    keep_u.wait()
+    keep_qkv.wait()
+
+
+def forward_call(x, emb, xs_1, w_qkv):
+    blk, d_model = x.shape
+    seq, head_cols = 4 * blk, 2 * PAIR
+    anywhere = pl.BlockSpec(memory_space=pl.ANY)
+    in_vmem = pl.BlockSpec(memory_space=pltpu.VMEM)
+    dma = pltpu.SemaphoreType.DMA
+    return pl.pallas_call(
+        forward_kernel,
+        in_specs=[in_vmem, in_vmem, anywhere, anywhere],
+        out_specs=[anywhere, in_vmem] + [anywhere] * 4,
+        out_shape=[
+            jax.ShapeDtypeStruct((blk, d_model), BF16),
+            jax.ShapeDtypeStruct((4, seq), F32),
+        ] + [jax.ShapeDtypeStruct((seq, n), BF16) for n in (d_model, 3 * head_cols)] * 2,
+        scratch_shapes=[
+            pltpu.VMEM((d_model, 3 * head_cols), BF16),
+            pltpu.VMEM((3, blk, d_model), BF16),
+            pltpu.VMEM((seq, d_model), BF16),
+            pltpu.VMEM((seq, 3 * head_cols), BF16),
+            pltpu.VMEM((2, blk, d_model), BF16),
+            pltpu.VMEM((2, blk, d_model), BF16),
+            pltpu.VMEM((2, blk, 3 * head_cols), BF16),
+            pltpu.VMEM((PAIR, seq), BF16),
+            pltpu.VMEM((seq, blk), F32),
+            pltpu.VMEM((seq, blk), F32),
+            pltpu.VMEM((2, seq, PAIR), BF16),
+            pltpu.VMEM((4, seq), F32),
+            dma((3,)), dma((2,)), dma((4,)), dma((3,)), dma((3,)), dma((8,)), dma((8,)),
+        ],
+        compiler_params=pltpu.CompilerParams(vmem_limit_bytes=60 << 20, collective_id=2, has_side_effects=True),
+        cost_estimate=pl.CostEstimate(
+            flops=64 * seq * seq * PAIR, bytes_accessed=32 * seq * d_model, transcendentals=seq * seq * 4),
+        name="forward",
+    )(x, emb, xs_1, w_qkv)
+
+
+def through_norm(values, up, d_mid):
+    inverse = lax.rsqrt(jnp.mean(values * values, axis=-1, keepdims=True) + EPS_NORM)
+    inner = jnp.mean(values * up, axis=-1, keepdims=True)
+    return (d_mid.astype(F32) + inverse * up - values * (inverse * inverse * inverse * inner)).astype(BF16)
+
+
+def backward_kernel(qkv_ref, dc_ref, lse_ref, dmid_ref, x_ref, emb_ref, wqkv_ref, u_ref,
+                    d_ref, other_ref, g_ref,
+                    dch, k_t, dk_acc, dv_acc, p_cat, ds_cat, d_heads, d_qkv, d_u, w_s, u_s, g_s,
+                    load_sem, out_sem, dc_send, dc_recv, dq_send, dq_recv, d_send, d_recv):
+    seq = qkv_ref.shape[0]
+    blk = seq // 4
+    head_cols = 2 * PAIR
+    here = Place()
+    z, core, role = here.z, here.c, here.role
+    here.meet()
+    member = [here.device(z=z // 2 * 2 + i // 2, c=i % 2) for i in range(4)]
+
+    def span(index, count):
+        return pl.ds(pl.multiple_of(index * count, count), count)
+
+    def load(src, dst, n):
+        copy = pltpu.make_async_copy(src, dst, load_sem.at[n])
+        copy.start()
+        return copy
+
+    def dc_copy(j, i):
+        col = i * head_cols + j * PAIR
+        return pltpu.make_async_remote_copy(
+            src_ref=dc_ref.at[:, col:col + PAIR], dst_ref=dch.at[span(role, blk), j * PAIR:(j + 1) * PAIR],
+            send_sem=dc_send.at[j * 4 + i], recv_sem=dc_recv.at[j * 4 + role], device_id=member[i], device_id_type=MESH)
+
+    for j in range(2):
+        for i in range(4):
+            pl.when(role != i)(dc_copy(j, i).start)
+    for i in range(4):
+        @pl.when(role == i)
+        def _():
+            dch[i * blk:(i + 1) * blk, :] = dc_ref[:, i * head_cols:(i + 1) * head_cols]
+
+    def dq_copy(j, i, t):
+        col = t * head_cols + j * PAIR
+        return pltpu.make_async_remote_copy(
+            src_ref=d_heads.at[i * blk:(i + 1) * blk, col:col + PAIR],
+            dst_ref=d_qkv.at[:, pl.ds(pl.multiple_of(role * 3 * head_cols + col, PAIR), PAIR)],
+            send_sem=dq_send.at[(j * 4 + i) * 3 + t], recv_sem=dq_recv.at[(j * 4 + role) * 3 + t],
+            device_id=member[i], device_id_type=MESH)
+
+    def send_d_heads(j):
+        for i in range(4):
+            @pl.when(role != i)
+            def _():
+                for t in range(3):
+                    dq_copy(j, i, t).start()
+
+    steps = seq // BWD_ROWS
+    for j in range(2):
+        for i in range(4):
+            @pl.when(role != i)
+            def _():
+                pltpu.make_async_copy(dc_ref.at[:, :PAIR], dch.at[:blk, :PAIR], dc_recv.at[j * 4 + i]).wait()
+        k_view, v_view = qkv_ref.at[:, (2 + j) * PAIR:(3 + j) * PAIR], qkv_ref.at[:, (4 + j) * PAIR:(5 + j) * PAIR]
+        k_t[...] = k_view[...].T
+        dk_acc[...] = jnp.zeros_like(dk_acc)
+        dv_acc[...] = jnp.zeros_like(dv_acc)
+
+        def block(i, _):
+            if j == 1:
+                @pl.when(i == 1)
+                def _():
+                    send_d_heads(0)
+            rows = span(i, BWD_ROWS)
+            cols = slice(j * PAIR, (j + 1) * PAIR)
+            d_heads[rows, cols] = backward_rows(
+                qkv_ref[rows, cols], dch[rows, cols], lse_ref[2 * j:2 * j + 2, rows], k_view, v_view,
+                k_t, p_cat, ds_cat, dk_acc, dv_acc)
+            return 0
+
+        lax.fori_loop(0, steps, block, 0)
+        d_heads[:, head_cols + j * PAIR:head_cols + (j + 1) * PAIR] = (dk_acc[...] * SCALE).astype(BF16)
+        d_heads[:, 2 * head_cols + j * PAIR:2 * head_cols + (j + 1) * PAIR] = dv_acc[...].astype(BF16)
+
+    quarter = u_s.shape[2]
+    pending = load(u_ref.at[:, :quarter], u_s.at[0], 0)
+    for i in range(4):
+        @pl.when(role == i)
+        def _():
+            d_qkv[:, i * 3 * head_cols:(i + 1) * 3 * head_cols] = d_heads[i * blk:(i + 1) * blk, :]
+    send_d_heads(1)
+    stores = []
+    count = u_ref.shape[1] // quarter
+    for n in range(count):
+        ahead = load(u_ref.at[:, (n + 1) * quarter:(n + 2) * quarter], u_s.at[(n + 1) % 2], (n + 1) % 2) if n + 1 < count else None
+        pending.wait()
+        if n >= 2:
+            stores[n - 2].wait()
+        g_s[n % 2] = dot_tn(u_s[n % 2], d_heads[...])
+        stores.append(pltpu.make_async_copy(g_s.at[n % 2], g_ref.at[n * quarter:(n + 1) * quarter, :], out_sem.at[n % 2]))
+        stores[n].start()
+        pending = ahead
+    w_rows = w_s.shape[1]
+    chunks = wqkv_ref.shape[0] // w_rows
+    w_load = load(wqkv_ref.at[:w_rows, :], w_s.at[0], 2)
+    for j in range(2):
+        for i in range(4):
+            @pl.when(role != i)
+            def _():
+                for t in range(3):
+                    pltpu.make_async_copy(d_heads.at[:blk, :PAIR], d_qkv.at[:, :PAIR], dq_recv.at[(j * 4 + i) * 3 + t]).wait()
+    for n in range(chunks):
+        ahead = load(wqkv_ref.at[(n + 1) * w_rows:(n + 2) * w_rows, :], w_s.at[(n + 1) % 2], 2 + (n + 1) % 2) if n + 1 < chunks else None
+        w_load.wait()
+        d_u[:, n * w_rows:(n + 1) * w_rows] = dot_nt(d_qkv[...], w_s[n % 2]).astype(BF16)
+        w_load = ahead
+    rows_each = min(128, blk)
+    for n in range(blk // rows_each):
+        rows = slice(n * rows_each, (n + 1) * rows_each)
+        d_u[rows, :] = through_norm(x_ref[rows, :].astype(F32) + emb_ref[...], d_u[rows, :].astype(F32), dmid_ref[rows, :])
+    keep = pltpu.make_async_copy(d_u, d_ref, out_sem.at[2])
+    keep.start()
+    stores[count - 2].wait()
+    stores[count - 1].wait()
+    give = pltpu.make_async_remote_copy(
+        src_ref=d_u, dst_ref=other_ref, send_sem=d_send.at[0], recv_sem=d_recv.at[0],
+        device_id=here.device(c=1 - core), device_id_type=MESH)
+    give.start()
+    for i in range(4):
+        @pl.when(role != i)
+        def _():
+            for j in range(2):
+                dc_copy(j, i).wait_send()
+                for t in range(3):
+                    dq_copy(j, i, t).wait_send()
+    keep.wait()
+    give.wait()
+
+
+def backward_call(qkv, d_c, lse, d_mid, x, emb, w_qkv, u_seq):
+    seq, d_model = u_seq.shape
+    blk, heads3 = seq // 4, qkv.shape[1]
+    anywhere = pl.BlockSpec(memory_space=pl.ANY)
+    in_vmem = pl.BlockSpec(memory_space=pltpu.VMEM)
+    dma = pltpu.SemaphoreType.DMA
+    quarter = d_model // 4
+    return pl.pallas_call(
+        backward_kernel,
+        in_specs=[in_vmem] * 6 + [anywhere] * 2,
+        out_specs=[anywhere] * 3,
+        out_shape=[
+            jax.ShapeDtypeStruct((blk, d_model), BF16),
+            jax.ShapeDtypeStruct((blk, d_model), BF16),
+            jax.ShapeDtypeStruct((d_model, heads3), F32),
+        ],
+        scratch_shapes=[
+            pltpu.VMEM((seq, heads3 // 3), BF16),
+            pltpu.VMEM((PAIR, seq), BF16),
+            pltpu.VMEM((seq, PAIR), F32),
+            pltpu.VMEM((seq, PAIR), F32),
+            pltpu.VMEM((seq, 2 * BWD_ROWS), BF16),
+            pltpu.VMEM((seq, 2 * BWD_ROWS), BF16),
+            pltpu.VMEM((seq, heads3), BF16),
+            pltpu.VMEM((blk, 4 * heads3), BF16),
+            pltpu.VMEM((blk, d_model), BF16),
+            pltpu.VMEM((2, quarter, 4 * heads3), BF16),
+            pltpu.VMEM((2, seq, quarter), BF16),
+            pltpu.VMEM((2, quarter, heads3), F32),
+            dma((4,)), dma((3,)), dma((8,)), dma((8,)), dma((24,)), dma((24,)), dma((1,)), dma((1,)),
+        ],
+        compiler_params=pltpu.CompilerParams(vmem_limit_bytes=60 << 20, collective_id=3, has_side_effects=True),
+        cost_estimate=pl.CostEstimate(
+            flops=160 * seq * seq * PAIR, bytes_accessed=64 * seq * d_model, transcendentals=seq * seq * 4),
+        name="backward",
+    )(qkv, d_c, lse, d_mid, x, emb, w_qkv, u_seq)
+
+
 def grad_kernel(by_left, _, *refs):
     lefts, rights, (away_ref, mid_ref, keep_ref, left_t, right_s) = refs[:16], refs[16:20], refs[20:]
     count, piece = lefts[0].shape
@@ -801,11 +1046,7 @@
     count = min(128, blk)
     for n in range(blk // count):
         rows = slice(n * count, (n + 1) * count)
-        values = x_ref[rows, :].astype(F32) + emb_ref[...]
-        up = d_1[rows, :].astype(F32)
-        inverse = lax.rsqrt(jnp.mean(values * values, axis=-1, keepdims=True) + EPS_NORM)
-        inner = jnp.mean(values * up, axis=-1, keepdims=True)
-        d_1[rows, :] = (dmid_ref[rows, :].astype(F32) + inverse * up - values * (inverse * inverse * inverse * inner)).astype(BF16)
+        d_1[rows, :] = through_norm(x_ref[rows, :].astype(F32) + emb_ref[...], d_1[rows, :].astype(F32), dmid_ref[rows, :])
 
     own_seq = z // 2
     rows_dx = span(role, blk)
@@ -1002,30 +1243,12 @@
     return lax.ppermute(value, AXES, pairs)
 
 
-def role_of(z, c):
-    return (z % 2) * 2 + c
-
-
-def in_group(k):
-    def to(z, y, x, c):
-        role = role_of(z, c) ^ k
-        return (z // 2 * 2 + role // 2, y, x, role % 2)
-
-    return to
-
-
 def other_core(z, y, x, c):
     return (z, y, x, 1 - c)
 
 
 def swap_first(z, y, x, c):
     return (z, y, 1 - x, c) if c == 0 else (z, 1 - y, x, c)
-
-
-def unscramble(parts, role):
-    odd, high = role % 2 == 1, role // 2 == 1
-    a = [jnp.where(odd, parts[i ^ 1], parts[i]) for i in range(4)]
-    return [jnp.where(high, a[i ^ 2], a[i]) for i in range(4)]
 
 
 def rows_of(value, index, count):
@@ -1040,7 +1263,6 @@
 
     def device_step(x_in, cot_out, step_emb, w_q, w_k, w_v, w_o, w_1, w_2):
         seq, d_model = x_in.shape[1:]
-        head_cols = w_q.shape[1]
         blk = seq // 4
         z = lax.axis_index('model')
         d = lax.axis_index('data')
@@ -1052,13 +1274,7 @@
         c_1, lse_1, x_seq, cot, wo, w1, w2, w_qkv = first_call(
             x_in[0], cot_out[0], emb[:1], w_q, w_k, w_v, w_o, w_1, w_2)
         wo, w2 = wo.reshape(-1, d_model), w2.reshape(-1, d_model)
-        w_qkv_role = lax.dynamic_slice_in_dim(w_qkv, role * 3 * head_cols, 3 * head_cols, axis=1)
         x_1 = rows_of(x_seq, role, blk)
-
-        def exchange(parts):
-            swapped = unscramble(parts, role)
-            got = [swapped[0]] + [send(swapped[k], in_group(k)) for k in (1, 2, 3)]
-            return unscramble(got, role)
 
         def mlp_forward(x_f, context):
             h = (x_f + dot_nn(context, wo)).astype(BF16)
@@ -1067,25 +1283,11 @@
             act = jax.nn.gelu(up.astype(F32)).astype(BF16)
             return h, m, up, act
 
-        def interleave(pairs):
-            return jnp.concatenate([pairs[j][i] for i in range(4) for j in range(2)], axis=1)
-
         s_1 = x_1.astype(F32) + emb[0]
         h_1, m_1, up_1, act_1 = mlp_forward(s_1, c_1)
         x_2 = (h_1.astype(F32) + dot_nn(act_1, w2)).astype(BF16)
 
-        side = send(x_2, other_core)
-        over = send(x_2, in_group(2))
-        x_2_seq = jnp.concatenate(unscramble([x_2, side, over, send(over, other_core)], role), axis=0)
-        u_2_seq = rms_norm(x_2_seq.astype(F32) + emb[1]).astype(BF16)
-        qkv_2 = dot_nn(u_2_seq, w_qkv_role).astype(BF16)
-        got, lse_2 = [], []
-        for j in range(2):
-            c_heads, lse = attn_fwd(qkv_2, j)
-            got.append(exchange([c_heads[i * blk:(i + 1) * blk] for i in range(4)]))
-            lse_2.append(lse)
-        c_2 = interleave(got)
-        lse_2 = jnp.concatenate(lse_2, axis=0)
+        c_2, lse_2, u_2_seq, qkv_2, u_1_seq, qkv_1 = forward_call(x_2, emb, x_seq, w_qkv)
         s_2 = x_2.astype(F32) + emb[1]
         h_2, m_2, up_2, act_2 = mlp_forward(s_2, c_2)
 
@@ -1097,22 +1299,8 @@
             return d_up, (d_next.astype(F32) + d_h).astype(BF16)
 
         d_up_2, d_mid_2 = mlp_backward(cot, h_2, up_2)
-        d_c = dot_nt(d_mid_2, wo).astype(BF16)
-        pairs, grads = [], []
-        for j in range(2):
-            heads = exchange([d_c[:, i * head_cols + j * PAIR:i * head_cols + (j + 1) * PAIR] for i in range(4)])
-            d_heads = attn_bwd(qkv_2, jnp.concatenate(heads, axis=0), lse_2[2 * j:2 * j + 2], j)
-            grads.append(dot_tn(u_2_seq, d_heads))
-            pairs.append(exchange([d_heads[i * blk:(i + 1) * blk] for i in range(4)]))
-        d_qkv = jnp.concatenate(
-            [pairs[j][i][:, t * PAIR:(t + 1) * PAIR] for i in range(4) for t in range(3) for j in range(2)], axis=1)
-        g_qkv_2 = jnp.concatenate([grads[j][:, t * PAIR:(t + 1) * PAIR] for t in range(3) for j in range(2)], axis=1)
-        d_u = dot_nt(d_qkv, w_qkv).astype(BF16)
-        d_s = jax.vjp(rms_norm, s_2)[1](d_u.astype(F32))[0]
-        d_2 = (d_mid_2.astype(F32) + d_s).astype(BF16)
-
-        u_1_seq = rms_norm(x_seq.astype(F32) + emb[0]).astype(BF16)
-        qkv_1 = dot_nn(u_1_seq, w_qkv_role).astype(BF16)
+        d_2, d_2_other, g_qkv_2 = backward_call(
+            qkv_2, dot_nt(d_mid_2, wo).astype(BF16), lse_2, d_mid_2, x_2, emb[1:], w_qkv, u_2_seq)
 
         first, second = jnp.where(core == 0, x, y), jnp.where(core == 0, y, x)
 
@@ -1129,7 +1317,9 @@
                 rights += [right, send(right, other_core)]
             return lefts, rights
 
-        lefts, rights = both_cores([(act_2, cot), (act_1, d_2)])
+        lefts, rights = both_cores([(act_2, cot)])
+        lefts += [act_1, send(act_1, other_core)]
+        rights += [d_2, d_2_other]
         away, mid, keep = grad_products(column, lefts, rights, True)
         d_2, away = lax.optimization_barrier((d_2, away))
         w2_parts = (send(away, swap_first), mid, keep)

time: 788 us -> 760 us (0.964)
  Pallas kernels: 509 us -> 592 us
  waiting for transfers between devices: 78.8 us -> 30.5 us
  other arithmetic: 38.8 us -> 3.75 us
  starting transfers between devices: 22.8 us -> 4.24 us
  matrix products: 101 us -> 89.4 us
    pallas_call x4 -> x2, Pallas kernels: 91.9 us -> 173 us  [the longest x1 111 us: backward_call(): pl.pallas_call(backward_kernel, in_specs=[in_vmem] * 6 + [anywhere] * 2,...]
    ppermute x34 -> x12, waiting for transfers between devices: 78.8 us -> 30.5 us  [send(): return lax.ppermute(value, AXES, pairs)]
    ppermute x34 -> x12, starting transfers between devices: 22.8 us -> 4.24 us  [send(): return lax.ppermute(value, AXES, pairs)]
    convert_element_type x3 -> x1, other arithmetic: 17.2 us -> 1.29 us  [device_step(): emb = step_emb.astype(F32)]
    select_n x11 -> x0, other arithmetic: 10.6 us -> none  [unscramble(): return [jnp.where(high, a[i ^ 2], a[i]) for i in range(4)]]
    dot_general x7 -> x6, matrix products: 50 us -> 45.9 us  [dot_nt(): lax.dot_general(a, b, (((1,), (1,)), ((), ())), preferred_element_type=F32)]
    unnamed x125 -> x85, local copies, waits for them, and re-layouts: 22.8 us -> 25.2 us
    dot_general x7 -> x5, matrix products: 43.4 us -> 43.5 us  [dot_nn(): lax.dot_general(a, b, (((1,), (0,)), ((), ())), preferred_element_type=F32)]
  transfers between devices with their start and end apart: 34 -> 12, of which waited for: 9 -> 1; matrix products, arithmetic and copies ran while one was open for 16% -> 6% of each run, Pallas kernels for 14% -> 17%
where the time goes in v2:
time: 760 us; the launch traced here: 750 us
  Pallas kernels  592 us (78%)
  matrix products  89.4 us (12%)
  waiting for transfers between devices  30.5 us (4%)
  local copies, waits for them, and re-layouts  28 us (4%)
    pallas_call x1, Pallas kernels, last_call(): pl.pallas_call(last_kernel, in_specs=[in_vmem] * 6 + [anywhere] * 22, out...  281 us
    pallas_call x1, Pallas kernels, first_call(): pl.pallas_call(first_kernel, in_specs=[in_vmem, anywhere] + [in_vmem] * 7...  119 us
    pallas_call x1, Pallas kernels, backward_call(): pl.pallas_call(backward_kernel, in_specs=[in_vmem] * 6 + [anywhere] * 2,...  111 us
    pallas_call x1, Pallas kernels, forward_call(): pl.pallas_call(forward_kernel, in_specs=[in_vmem, in_vmem, anywhere, anyw...  62 us
    dot_general x6, matrix products, dot_nt(): lax.dot_general(a, b, (((1,), (1,)), ((), ())), preferred_element_type=F32)  45.9 us
    dot_general x5, matrix products, dot_nn(): lax.dot_general(a, b, (((1,), (0,)), ((), ())), preferred_element_type=F32)  43.5 us
    ppermute x12, waiting for transfers between devices, send(): return lax.ppermute(value, AXES, pairs)  30.5 us
    unnamed x85, local copies, waits for them, and re-layouts  25.2 us
  transfers between devices with their start and end apart: 12, of which 1 were waited for; matrix products, arithmetic and copies ran while one was open for 6% of the time, Pallas kernels for 17%

profile of v2, /device:TPU:17, one launch (start us, length us, event | category | flops | bytes accessed | tf_op | source)
XLA Modules:
  0.0 749.5 jit_solution(8089476467630583966)
XLA Ops:
  0.6 1.4 fusion.37
  2.0 1.3 convert_element_type.101.emb_ref
  3.3 119.1 %first.1 = (bf16[512,1024]{1,0:T(8,128)(2,1)}, f32[4,2048]{1,0:T(4,128)}, bf16[2048,1024]{1,0:T(8,128)(2,1)}, bf16[512,1024]{1,0:T(8,128)(2,1)}, bf16[4,256,1024...) custom-call(bf16[2048,1024]{1,0:T(8,128)(2,1)} %bitcast.37, ...), custom_call_target="tpu_custom_call" | custom-call | flops 34359738368 | bytes 134217728 | tf_op jit(solution)/shard_map/first/pallas_call | solution.py:331
  122.5 1.5 constant_dynamic-slice_fusion.x_ref
  123.9 1.0 copy-done.9
  124.9 14.1 %fusion.29 = (f32[512]{0:T(512)S(1)}, bf16[512,1024]{1,0:T(8,128)(2,1)S(1)}) fusion(bf16[512,1024]{1,0:T(8,128)(2,1)} %get-tuple-element.37.refs_14_, bf16[1024,1024]{1,0:T(8,128)(2,1)} %bitcast.46, f32[1024]{0:T(1024)S(1)} %bitcast.35, bf16[512,1024]{1,0:T(8,128)(2,1)S(1)} %constant_dynamic-slice_fusion.x_ref), kind=kOutput, calls=%fused_computation.58 | convolution fusion | flops 1077411328 | bytes 5249024 | tf_op jit(solution)/shard_map/dot_general | solution.py:35
  140.0 7.7 %fusion.13 = (bf16[512,4096]{1,0:T(8,128)(2,1)}, bf16[512,4096]{1,0:T(8,128)(2,1)S(1)}) fusion(bf16[512,1024]{1,0:T(8,128)(2,1)S(1)} %fusion.30.refs_2_, bf16[1024,4096]{1,0:T(8,128)(2,1)S(1)} %bitcast.51), kind=kOutput, calls=%fused_computation.25 | convolution fusion | flops 4318035968 | bytes 17825792 | tf_op jit(solution)/shard_map/dot_general | solution.py:35
  147.8 6.3 fusion.31.x_ref
  154.1 62.0 %forward.1 = (bf16[512,1024]{1,0:T(8,128)(2,1)}, f32[4,2048]{1,0:T(4,128)}, bf16[2048,1024]{1,0:T(8,128)(2,1)}, bf16[2048,768]{1,0:T(8,128)(2,1)}, bf16[2048,102...) custom-call(bf16[512,1024]{1,0:T(8,128)(2,1)} %fusion.31.x_ref, f32[2,1024]{1,0:T(2,128)} %convert_element_type.101.emb_ref, ...), custom_call_target="tpu_custom_call" | custom-call | flops 34359738368 | bytes 67108864 | tf_op jit(solution)/shard_map/forward/pallas_call | solution.py:489
  216.1 3.0 fusion.26
  219.4 12.4 %fusion.21 = (bf16[512,4096]{1,0:T(8,128)(2,1)}, bf16[512,4096]{1,0:T(8,128)(2,1)}) fusion(bf16[512,1024]{1,0:T(8,128)(2,1)S(1)} %fusion.27.refs_0_, bf16[1024,4096]{1,0:T(8,128)(2,1)} %get-tuple-element.39), kind=kOutput, calls=%fused_computation.33 | convolution fusion | flops 4318035968 | bytes 17825792 | tf_op jit(solution)/shard_map/dot_general | solution.py:35
  232.4 12.3 %fusion.4.refs_4_ = bf16[512,4096]{1,0:T(8,128)(2,1)} fusion(bf16[512,4096]{1,0:T(8,128)(2,1)} %get-tuple-element.81, bf16[512,1024]{1,0:T(8,128)(2,1)S(1)} %copy-done, bf16[4096,1024]{1,0:T(8,128)(2,1)S(1)} %bitcast.45), kind=kOutput, calls=%fused_computation.16 | convolution fusion | flops 4343201792 | bytes 17825792 | tf_op jit(solution)/shard_map/dot_general | solution.py:31
  245.1 7.0 fusion.28
  252.9 2.3 convolution_convert_fusion.7.dc_ref
  255.2 111.4 %backward.1 = (bf16[512,1024]{1,0:T(8,128)(2,1)}, bf16[512,1024]{1,0:T(8,128)(2,1)}, f32[1024,768]{1,0:T(8,128)}) custom-call(bf16[2048,768]{1,0:T(8,128)(2,1)} %get-tuple-element.43.qkv_ref, bf16[512,1024]{1,0:T(8,128)(2,1)} %convolution_convert_fusion.7.dc_ref, f32[4,2048]{1,0:T(4,128)} %get-tuple-element.46.lse_ref, bf16[512,1024]{1,0:T(8,128)(2,1)} %copy-done.7, ...), custom_call_target="tpu_custom_call" | custom-call | flops 85899345920 | bytes 134217728 | tf_op jit(solution)/shard_map/backward/pallas_call | solution.py:663
  368.2 18.2 %grad.1 = (f32[4,256,1024]{2,1,0:T(8,128)}, f32[4,128,1024]{2,1,0:T(8,128)}, f32[4,128,1024]{2,1,0:T(8,128)}) custom-call(s32[4]{0:T(128)} %fusion.35._, bf16[512,4096]{1,0:T(8,128)(2,1)} %get-tuple-element.80.refs_0_.refs_1_.refs_2_.refs_3_, bf16[512,4096]{1,0:T(8,128)(2,1)} %get-tuple-element.80.refs_0_.refs_1_.refs_2_.refs_3_, ...), custom_call_target="tpu_custom_call" | custom-call | flops 8589934592 | bytes 27262976 | tf_op jit(solution)/shard_map/grad/pallas_call | solution.py:725
  386.5 12.5 %fusion.7.refs_6_ = bf16[512,4096]{1,0:T(8,128)(2,1)S(1)} fusion(bf16[512,4096]{1,0:T(8,128)(2,1)} %copy-done.30, bf16[512,1024]{1,0:T(8,128)(2,1)S(1)} %copy-done.1, bf16[4096,1024]{1,0:T(8,128)(2,1)} %bitcast.39), kind=kOutput, calls=%fused_computation.19 | convolution fusion | flops 4343201792 | bytes 17825792 | tf_op jit(solution)/shard_map/dot_general | solution.py:31
  399.5 1.0 collective-permute-start.3
  400.4 0.7 collective-permute-start.10
  401.2 8.0 %fusion.32 = (f32[512]{0:T(512)S(1)}, bf16[512,1024]{1,0:T(8,128)(2,1)S(1)}) fusion(bf16[512,1024]{1,0:T(8,128)(2,1)S(1)} %copy-done.3, bf16[512,4096]{1,0:T(8,128)(2,1)S(1)} %fusion.7.refs_6_, bf16[1024,4096]{1,0:T(8,128)(2,1)} %get-tuple-element.39), kind=kOutput, calls=%fused_computation.61 | convolution fusion | flops 4297588224 | bytes 14682112 | tf_op jit(solution)/shard_map/dot_general | solution.py:31
  410.9 3.8 convolution_convert_fusion.6.dc_ref
  414.8 2.0 copy-done.20
  416.8 30.5 %collective-permute-done.3.r2_ref = f32[4,256,1024]{2,1,0:T(8,128)S(1)} collective-permute-done((f32[4,256,1024]{2,1,0:T(8,128)}, f32[4,256,1024]{2,1,0:T(8,128)S(1)}, u32[]{:S(2)}, u32[]{:S(2)}) %collective-permute-start.3) | collective-permute-done | bytes 4194336 | tf_op jit(solution)/shard_map/ppermute | solution.py:1243
  447.3 2.0 copy-done.21
  449.3 281.4 %last.1 = (bf16[2048,1024]{1,0:T(8,128)(2,1)}, f32[1024,1024]{1,0:T(8,128)}, f32[1024,1024]{1,0:T(8,128)}, f32[1024,256]{1,0:T(8,128)}, f32[1024,256]{1,0:T(8,12...) custom-call(bf16[2048,768]{1,0:T(8,128)(2,1)} %get-tuple-element.42., ...), custom_call_target="tpu_custom_call" | custom-call | flops 85899345920 | bytes 268435456 | tf_op jit(solution)/shard_map/last/pallas_call | solution.py:1177
  730.7 2.5 copy.16
  733.3 2.4 copy.23
  735.7 2.3 copy.24
  737.9 2.3 copy.25
  740.2 4.9 copy.26
  745.1 2.0 copy.27
  747.1 2.0 copy.28
  (109 shorter events, 6.8 us)
Async XLA Ops:
  2.0 214.1 %copy-start.18 = (f32[1,1024]{1,0:T(1,128)}, f32[1,1024]{1,0:T(1,128)S(1)}, u32[]{:S(2)}) copy-start(f32[1,1024]{1,0:T(1,128)S(1)} %get-tuple-element.72.emb_ref) | copy-start | bytes 12292
  3.3 121.6 %copy-start.17 = (f32[1,1024]{1,0:T(1,128)S(1)}, f32[1,1024]{1,0:T(1,128)}, u32[]{:S(2)}) copy-start(f32[1,1024]{1,0:T(1,128)} %get-tuple-element.73.emb_ref) | copy-start | bytes 12292
  122.4 17.5 %slice-start.4 = ((s8[8388608]{0:T(1024)(128)(4,1)}), s8[4194304]{0:T(1024)(128)(4,1)S(1)}, s32[]{:S(2)}) async-start(s8[8388608]{0:T(1024)(128)(4,1)} %bitcast.50), calls=%async_computation.4 | async-start | bytes 8388608
  124.9 15.0 %slice-start.5 = ((s8[8388608]{0:T(1024)(128)(4,1)}), s8[4194304]{0:T(1024)(128)(4,1)S(1)}, s32[]{:S(2)}) async-start(s8[8388608]{0:T(1024)(128)(4,1)} %bitcast.50), calls=%async_computation.5 | async-start | bytes 8388608
  154.1 62.0 %copy-start.27 = (bf16[4,256,1024]{2,1,0:T(8,128)(2,1)S(1)}, bf16[4,256,1024]{2,1,0:T(8,128)(2,1)}, u32[]{:S(2)}) copy-start(bf16[4,256,1024]{2,1,0:T(8,128)(2,1)} %get-tuple-element.38) | copy-start | bytes 6291460
  154.1 62.0 %copy-start.29 = (bf16[512,1024]{1,0:T(8,128)(2,1)S(1)}, bf16[512,1024]{1,0:T(8,128)(2,1)}, u32[]{:S(2)}) copy-start(bf16[512,1024]{1,0:T(8,128)(2,1)} %fusion.31.x_ref) | copy-start | bytes 3145732
  216.1 16.3 %slice-start.2 = ((s8[8388608]{0:T(1024)(128)(4,1)}), s8[4194304]{0:T(1024)(128)(4,1)S(1)}, s32[]{:S(2)}) async-start(s8[8388608]{0:T(1024)(128)(4,1)} %bitcast.43), calls=%async_computation.2 | async-start | bytes 8388608
  219.3 12.4 %copy-start.12 = (bf16[512,1024]{1,0:T(8,128)(2,1)}, bf16[512,1024]{1,0:T(8,128)(2,1)S(1)}, u32[]{:S(2)}) copy-start(bf16[512,1024]{1,0:T(8,128)(2,1)S(1)} %fusion.27.refs_0_) | copy-start | bytes 3145732
  219.4 12.9 %copy-start = (bf16[512,1024]{1,0:T(8,128)(2,1)S(1)}, bf16[512,1024]{1,0:T(8,128)(2,1)}, u32[]{:S(2)}) copy-start(bf16[512,1024]{1,0:T(8,128)(2,1)} %get-tuple-element.44.refs_16_) | copy-start | bytes 3145732
  219.4 13.0 %slice-start.3 = ((s8[8388608]{0:T(1024)(128)(4,1)}), s8[4194304]{0:T(1024)(128)(4,1)S(1)}, s32[]{:S(2)}) async-start(s8[8388608]{0:T(1024)(128)(4,1)} %bitcast.43), calls=%async_computation.3 | async-start | bytes 8388608
  219.4 25.7 %slice-start.6 = ((s8[8388608]{0:T(1024)(128)(4,1)}), s8[4194304]{0:T(1024)(128)(4,1)S(1)}, s32[]{:S(2)}) async-start(s8[8388608]{0:T(1024)(128)(4,1)} %bitcast.52), calls=%async_computation.6 | async-start | bytes 8388608
  231.8 135.9 %collective-permute-start = (bf16[512,4096]{1,0:T(8,128)(2,1)}, bf16[512,4096]{1,0:T(8,128)(2,1)}, u32[]{:S(2)}, u32[]{:S(2)}) collective-permute-start(bf16[512,4096]{1,0:T(8,128)(2,1)} %get-tuple-element.80.refs_0_.refs_1_.refs_2_.refs_3_), channel_id=1, source_target_pairs={{0,1},{1,0},{2,3},{3,2},{4,5},{5,4},{6,7},{7,6},{8,9},{9,8},{10,11... | collective-permute-start | bytes 12582920 | tf_op jit(solution)/shard_map/ppermute | solution.py:1243
  231.9 135.8 %collective-permute-start.1 = (bf16[512,4096]{1,0:T(8,128)(2,1)}, bf16[512,4096]{1,0:T(8,128)(2,1)}, u32[]{:S(2)}, u32[]{:S(2)}) collective-permute-start(bf16[512,4096]{1,0:T(8,128)(2,1)} %get-tuple-element.82.refs_8_.refs_9_.refs_10_.refs_11_), channel_id=1, source_target_pairs={{0,1},{1,0},{2,3},{3,2},{4,5},{5,4},{6,7},{7,6},{8,9},{9,8},{10,11... | collective-permute-start | bytes 12582920 | tf_op jit(solution)/shard_map/ppermute | solution.py:1243
  232.3 135.0 %collective-permute-start.2 = (bf16[512,1024]{1,0:T(8,128)(2,1)S(1)}, bf16[512,1024]{1,0:T(8,128)(2,1)S(1)}, u32[]{:S(2)}, u32[]{:S(2)}) collective-permute-start(bf16[512,1024]{1,0:T(8,128)(2,1)S(1)} %copy-done), channel_id=1, source_target_pairs={{0,1},{1,0},{2,3},{3,2},{4,5},{5,4},{6,7},{7,6},{8,9},{9,8},{10,11... | collective-permute-start | bytes 3145736 | tf_op jit(solution)/shard_map/ppermute | solution.py:1243
  232.4 12.7 %slice-start.7 = ((s8[8388608]{0:T(1024)(128)(4,1)}), s8[4194304]{0:T(1024)(128)(4,1)S(1)}, s32[]{:S(2)}) async-start(s8[8388608]{0:T(1024)(128)(4,1)} %bitcast.52), calls=%async_computation.7 | async-start | bytes 8388608
  244.7 170.0 %collective-permute-start.6 = (bf16[512,4096]{1,0:T(8,128)(2,1)}, bf16[512,4096]{1,0:T(8,128)(2,1)}, u32[]{:S(2)}, u32[]{:S(2)}) collective-permute-start(bf16[512,4096]{1,0:T(8,128)(2,1)} %fusion.4.refs_4_), channel_id=1, source_target_pairs={{0,1},{1,0},{2,3},{3,2},{4,5},{5,4},{6,7},{7,6},{8,9},{9,8},{10,11... | collective-permute-start | bytes 12582920 | tf_op jit(solution)/shard_map/ppermute | solution.py:1243
  252.8 147.6 %collective-permute-start.8 = (bf16[512,1024]{1,0:T(8,128)(2,1)S(1)}, bf16[512,1024]{1,0:T(8,128)(2,1)}, u32[]{:S(2)}, u32[]{:S(2)}) collective-permute-start(bf16[512,1024]{1,0:T(8,128)(2,1)S(1)} %fusion.23.dmid_ref.refs_8_), channel_id=1, source_target_pairs={{0,1},{1,0},{2,3},{3,2},{4,5},{5,4},{6,7},{7,6},{8,9},{9,8},{10,11... | collective-permute-start | bytes 3145736 | tf_op jit(solution)/shard_map/ppermute | solution.py:1243
  367.3 33.8 %collective-permute-start.4 = (bf16[512,1024]{1,0:T(8,128)(2,1)}, bf16[512,1024]{1,0:T(8,128)(2,1)}, u32[]{:S(2)}, u32[]{:S(2)}) collective-permute-start(bf16[512,1024]{1,0:T(8,128)(2,1)} %copy-done.12), channel_id=1, source_target_pairs={{0,1},{1,0},{2,3},{3,2},{4,5},{5,4},{6,7},{7,6},{8,9},{9,8},{10,11... | collective-permute-start | bytes 3145736 | tf_op jit(solution)/shard_map/ppermute | solution.py:1243
  368.2 18.2 %copy-start.1 = (bf16[512,1024]{1,0:T(8,128)(2,1)S(1)}, bf16[512,1024]{1,0:T(8,128)(2,1)}, u32[]{:S(2)}) copy-start(bf16[512,1024]{1,0:T(8,128)(2,1)} %get-tuple-element.51.refs_18_) | copy-start | bytes 3145732
  386.5 13.9 %copy-start.23 = (bf16[512,1024]{1,0:T(8,128)(2,1)S(1)}, bf16[512,1024]{1,0:T(8,128)(2,1)}, u32[]{:S(2)}) copy-start(bf16[512,1024]{1,0:T(8,128)(2,1)} %get-tuple-element.45.refs_12_) | copy-start | bytes 3145732
  386.5 14.6 %copy-start.11 = (bf16[512,1024]{1,0:T(8,128)(2,1)S(1)}, bf16[512,1024]{1,0:T(8,128)(2,1)}, u32[]{:S(2)}) copy-start(bf16[512,1024]{1,0:T(8,128)(2,1)} %copy-done.10) | copy-start | bytes 3145732
  386.5 14.7 %copy-start.3 = (bf16[512,1024]{1,0:T(8,128)(2,1)S(1)}, bf16[512,1024]{1,0:T(8,128)(2,1)}, u32[]{:S(2)}) copy-start(bf16[512,1024]{1,0:T(8,128)(2,1)} %copy-done.2) | copy-start | bytes 3145732
  399.0 15.7 %collective-permute-start.7 = (bf16[512,4096]{1,0:T(8,128)(2,1)S(1)}, bf16[512,4096]{1,0:T(8,128)(2,1)S(1)}, u32[]{:S(2)}, u32[]{:S(2)}) collective-permute-start(bf16[512,4096]{1,0:T(8,128)(2,1)S(1)} %fusion.7.refs_6_), channel_id=1, source_target_pairs={{0,1},{1,0},{2,3},{3,2},{4,5},{5,4},{6,7},{7,6},{8,9},{9,8},{10,11... | collective-permute-start | bytes 12582920 | tf_op jit(solution)/shard_map/ppermute | solution.py:1243
  399.5 47.9 %collective-permute-start.3 = (f32[4,256,1024]{2,1,0:T(8,128)}, f32[4,256,1024]{2,1,0:T(8,128)S(1)}, u32[]{:S(2)}, u32[]{:S(2)}) collective-permute-start(f32[4,256,1024]{2,1,0:T(8,128)} %get-tuple-element.55), channel_id=1, source_target_pairs={{0,2},{1,5},{2,0},{3,7},{4,6},{5,1},{6,4},{7,3},{8,10},{9,13},{10,... | collective-permute-start | bytes 12582920 | tf_op jit(solution)/shard_map/ppermute | solution.py:1243
  400.4 9.5 %collective-permute-start.10 = (bf16[512,1024]{1,0:T(8,128)(2,1)S(1)}, bf16[512,1024]{1,0:T(8,128)(2,1)S(1)}, u32[]{:S(2)}, u32[]{:S(2)}) collective-permute-start(bf16[512,1024]{1,0:T(8,128)(2,1)S(1)} %copy-done.23), channel_id=1, source_target_pairs={{0,1},{1,0},{2,3},{3,2},{4,5},{5,4},{6,7},{7,6},{8,9},{9,8},{10,11... | collective-permute-start | bytes 3145736 | tf_op jit(solution)/shard_map/ppermute | solution.py:1243
  401.1 9.3 %collective-permute-start.5 = (bf16[512,1024]{1,0:T(8,128)(2,1)S(1)}, bf16[512,1024]{1,0:T(8,128)(2,1)}, u32[]{:S(2)}, u32[]{:S(2)}) collective-permute-start(bf16[512,1024]{1,0:T(8,128)(2,1)S(1)} %copy-done.11), channel_id=1, source_target_pairs={{0,1},{1,0},{2,3},{3,2},{4,5},{5,4},{6,7},{7,6},{8,9},{9,8},{10,11... | collective-permute-start | bytes 3145736 | tf_op jit(solution)/shard_map/ppermute | solution.py:1243
  409.9 39.4 %copy-start.24 = (bf16[512,1024]{1,0:T(8,128)(2,1)}, bf16[512,1024]{1,0:T(8,128)(2,1)S(1)}, u32[]{:S(2)}) copy-start(bf16[512,1024]{1,0:T(8,128)(2,1)S(1)} %collective-permute-done.10.refs_13_) | copy-start | bytes 3145732
  409.9 4.8 collective-permute-start.11
  410.4 4.3 collective-permute-start.9
  414.7 34.6 %copy-start.25 = (bf16[512,1024]{1,0:T(8,128)(2,1)}, bf16[512,1024]{1,0:T(8,128)(2,1)S(1)}, u32[]{:S(2)}) copy-start(bf16[512,1024]{1,0:T(8,128)(2,1)S(1)} %collective-permute-done.11.refs_15_) | copy-start | bytes 3145732
  414.7 34.6 %copy-start.26 = (bf16[512,1024]{1,0:T(8,128)(2,1)}, bf16[512,1024]{1,0:T(8,128)(2,1)S(1)}, u32[]{:S(2)}) copy-start(bf16[512,1024]{1,0:T(8,128)(2,1)S(1)} %collective-permute-done.9.refs_11_) | copy-start | bytes 3145732
  733.3 11.9 %copy-start.5 = (f32[1024,1024]{1,0:T(8,128)S(1)}, f32[1024,1024]{1,0:T(8,128)}, u32[]{:S(2)}) copy-start(f32[1024,1024]{1,0:T(8,128)} %get-tuple-element.98) | copy-start | bytes 12582916
  (19 other events, 106.3 us)

commit v3 on v2

--- a/solution.py
+++ b/solution.py
@@ -16,15 +16,12 @@
 PAIR = 2 * HEAD_DIM
 BWD_ROWS = 256
 KEYS = 256
+HIDDEN = 512
 INTERPRET = False
 AXES = ('model', 'data')
 BF16 = jnp.bfloat16
 F32 = jnp.float32
 MESH = pl.DeviceIdType.MESH
-
-
-def rms_norm(values):
-    return values * lax.rsqrt(jnp.mean(values * values, axis=-1, keepdims=True) + EPS_NORM)
 
 
 def dot_nt(a, b):
@@ -689,6 +686,150 @@
             flops=160 * seq * seq * PAIR, bytes_accessed=64 * seq * d_model, transcendentals=seq * seq * 4),
         name="backward",
     )(qkv, d_c, lse, d_mid, x, emb, w_qkv, u_seq)
+
+
+def rms_rows(values):
+    return values * lax.rsqrt(jnp.mean(values * values, axis=-1, keepdims=True) + EPS_NORM)
+
+
+GELU_IN, GELU_CUBE = math.sqrt(2 / math.pi), 0.044715
+
+
+def gelu_parts(z):
+    square = z * z
+    t = jnp.tanh(z * (GELU_IN + (GELU_IN * GELU_CUBE) * square))
+    return 0.5 + 0.5 * t, t, square
+
+
+def hidden_kernel(backward, forward, *refs):
+    refs = list(refs)
+    take = lambda: refs.pop(0)
+    if forward:
+        c_ref, x_ref, emb_ref, wo_ref = take(), take(), take(), take()
+        w1_ref = take()
+    else:
+        h_ref, wo_ref, up_ref = take(), take(), take()
+    w2_ref = take()
+    if backward:
+        d_ref, w1b_ref = take(), take()
+    if forward:
+        h_out, m_out = take(), take()
+        up_out, act_out = take(), take()
+    if backward:
+        dup_out, dmid_out, dc_out = take(), take(), take()
+    else:
+        x_out = take()
+    if forward:
+        h_s, m_s = take(), take()
+    prev_s, acc = take(), take()
+    step, last = pl.program_id(0), pl.num_programs(0) - 1
+
+    if forward:
+        @pl.when(step == 0)
+        def _():
+            h = (x_ref[...].astype(F32) + emb_ref[...] + dot_nn(c_ref[...], wo_ref[...])).astype(BF16)
+            m = rms_rows(h.astype(F32)).astype(BF16)
+            h_s[...], m_s[...] = h, m
+            h_out[...], m_out[...] = h, m
+
+    def first_part():
+        slot = step % 2
+        if backward:
+            d_act = dot_nt(d_ref[...], w2_ref[...]).astype(BF16).astype(F32)
+        if forward:
+            up = dot_nn(m_s[...], w1_ref[...]).astype(BF16)
+            up_out[...] = up
+        else:
+            up = up_ref[...]
+        z = up.astype(F32)
+        factor, t, square = gelu_parts(z)
+        if forward:
+            act = (z * factor).astype(BF16)
+            act_out[...] = act
+        if backward:
+            slope = factor + z * ((1.0 - t * t) * (0.5 * GELU_IN + (1.5 * GELU_IN * GELU_CUBE) * square))
+            d_up = (slope * d_act).astype(BF16)
+            dup_out[...] = d_up
+            prev_s[slot] = d_up
+        else:
+            prev_s[slot] = act
+
+    def second_part():
+        prev = prev_s[1 - step % 2]
+        if backward:
+            return dot_nt(prev, w1b_ref[...])
+        return dot_nn(prev, w2_ref[...])
+
+    pl.when(step == 0)(first_part)
+
+    @pl.when(step == 1)
+    def _():
+        acc[...] = second_part()
+        first_part()
+
+    @pl.when(jnp.logical_and(step > 1, step < last))
+    def _():
+        acc[...] += second_part()
+        first_part()
+
+    @pl.when(step == last)
+    def _():
+        total = acc[...] + second_part()
+        if backward:
+            h = (h_s if forward else h_ref)[...].astype(F32)
+            d_mid = through_norm(h, total.astype(BF16).astype(F32), d_ref[...])
+            dmid_out[...] = d_mid
+            dc_out[...] = dot_nt(d_mid, wo_ref[...]).astype(BF16)
+        else:
+            x_out[...] = (h_s[...].astype(F32) + total).astype(BF16)
+
+
+def hidden_call(forward, backward, w_o, w_1, w_2, context=None, x=None, emb=None, h=None, up=None, d_next=None):
+    blk, d_model = (context if forward else h).shape
+    hidden = w_1.shape[1]
+    tile = HIDDEN
+    steps = hidden // tile
+    now, before = (lambda i: jnp.minimum(i, steps - 1)), (lambda i: jnp.maximum(i - 1, 0))
+    whole = lambda rows, cols: pl.BlockSpec((rows, cols), lambda i: (0, 0))
+    wide = pl.BlockSpec((blk, tile), lambda i: (0, now(i)))
+    args, specs = [], []
+
+    def add(value, spec):
+        args.append(value)
+        specs.append(spec)
+
+    if forward:
+        add(context, whole(blk, d_model))
+        add(x, whole(blk, d_model))
+        add(emb, whole(1, d_model))
+        add(w_o, whole(d_model, d_model))
+        add(w_1, pl.BlockSpec((d_model, tile), lambda i: (0, now(i))))
+    else:
+        add(h, whole(blk, d_model))
+        add(w_o, whole(d_model, d_model))
+        add(up, wide)
+    add(w_2, pl.BlockSpec((tile, d_model), (lambda i: (now(i), 0)) if backward else (lambda i: (before(i), 0))))
+    if backward:
+        add(d_next, whole(blk, d_model))
+        add(w_1, pl.BlockSpec((d_model, tile), lambda i: (0, before(i))))
+    row = (whole(blk, d_model), jax.ShapeDtypeStruct((blk, d_model), BF16))
+    big = (wide, jax.ShapeDtypeStruct((blk, hidden), BF16))
+    outs = ([row, row, big, big] if forward else []) + ([big, row, row] if backward else [row])
+    return pl.pallas_call(
+        functools.partial(hidden_kernel, backward, forward),
+        grid=(steps + 1,),
+        in_specs=specs,
+        out_specs=[spec for spec, _ in outs],
+        out_shape=[shape for _, shape in outs],
+        scratch_shapes=([pltpu.VMEM((blk, d_model), BF16)] * 2 if forward else [])
+        + [pltpu.VMEM((2, blk, tile), BF16), pltpu.VMEM((blk, d_model), F32)],
+        compiler_params=pltpu.CompilerParams(vmem_limit_bytes=60 << 20),
+        cost_estimate=pl.CostEstimate(
+            flops=2 * blk * d_model * (hidden * (3 if forward and backward else 2) + 2 * d_model),
+            bytes_accessed=4 * hidden * d_model + 8 * blk * hidden, transcendentals=blk * hidden),
+        interpret=INTERPRET,
+        name="hidden",
+    )(*args)
 
 
 def grad_kernel(by_left, _, *refs):
@@ -1276,31 +1417,12 @@
         wo, w2 = wo.reshape(-1, d_model), w2.reshape(-1, d_model)
         x_1 = rows_of(x_seq, role, blk)
 
-        def mlp_forward(x_f, context):
-            h = (x_f + dot_nn(context, wo)).astype(BF16)
-            m = rms_norm(h.astype(F32)).astype(BF16)
-            up = dot_nn(m, w1).astype(BF16)
-            act = jax.nn.gelu(up.astype(F32)).astype(BF16)
-            return h, m, up, act
-
-        s_1 = x_1.astype(F32) + emb[0]
-        h_1, m_1, up_1, act_1 = mlp_forward(s_1, c_1)
-        x_2 = (h_1.astype(F32) + dot_nn(act_1, w2)).astype(BF16)
+        h_1, m_1, up_1, act_1, x_2 = hidden_call(True, False, wo, w1, w2, context=c_1, x=x_1, emb=emb[:1])
 
         c_2, lse_2, u_2_seq, qkv_2, u_1_seq, qkv_1 = forward_call(x_2, emb, x_seq, w_qkv)
-        s_2 = x_2.astype(F32) + emb[1]
-        h_2, m_2, up_2, act_2 = mlp_forward(s_2, c_2)
-
-        def mlp_backward(d_next, h, up):
-            d_act = dot_nt(d_next, w2).astype(BF16)
-            d_up = jax.vjp(jax.nn.gelu, up.astype(F32))[1](d_act.astype(F32))[0].astype(BF16)
-            d_m = dot_nt(d_up, w1).astype(BF16)
-            d_h = jax.vjp(rms_norm, h.astype(F32))[1](d_m.astype(F32))[0]
-            return d_up, (d_next.astype(F32) + d_h).astype(BF16)
-
-        d_up_2, d_mid_2 = mlp_backward(cot, h_2, up_2)
+        _, m_2, _, act_2, d_up_2, d_mid_2, d_c = hidden_call(True, True, wo, w1, w2, context=c_2, x=x_2, emb=emb[1:], d_next=cot)
         d_2, d_2_other, g_qkv_2 = backward_call(
-            qkv_2, dot_nt(d_mid_2, wo).astype(BF16), lse_2, d_mid_2, x_2, emb[1:], w_qkv, u_2_seq)
+            qkv_2, d_c, lse_2, d_mid_2, x_2, emb[1:], w_qkv, u_2_seq)
 
         first, second = jnp.where(core == 0, x, y), jnp.where(core == 0, y, x)
 
@@ -1323,10 +1445,9 @@
         away, mid, keep = grad_products(column, lefts, rights, True)
         d_2, away = lax.optimization_barrier((d_2, away))
         w2_parts = (send(away, swap_first), mid, keep)
-        d_up_1, d_mid_1 = mlp_backward(d_2, h_1, up_1)
+        d_up_1, d_mid_1, d_c = hidden_call(False, True, wo, w1, w2, h=h_1, up=up_1, d_next=d_2)
         w1_sides = sum(both_cores([(m_2, d_up_2), (m_1, d_up_1)]), [])
         wo_sides = sum(both_cores([(d_mid_2, c_2), (d_mid_1, c_1)]), [])
-        d_c = dot_nt(d_mid_1, wo).astype(BF16)
         d_x, g_w1, g_w2, g_wo, g_q, g_k, g_v = last_call(
             qkv_1, d_c, lse_1, d_mid_1, x_1, emb[:1], w_qkv, u_1_seq, g_qkv_2, w2_parts, w1_sides, wo_sides)
         return g_q, g_k, g_v, g_wo.T, g_w1, g_w2, d_x[None]

time: 760 us -> 757 us (level)
  matrix products: 89.4 us -> 0 us
  Pallas kernels: 592 us -> 673 us
  waiting for transfers between devices: 30.5 us -> 45 us
  local copies, waits for them, and re-layouts: 28 us -> 20.1 us
    dot_general x11 -> x0, matrix products: 89.4 us -> none  [the longest x6 45.9 us: dot_nt(): lax.dot_general(a, b, (((1,), (1,)), ((), ())), preferred_element_type=F32)]
    pallas_call x0 -> x3, Pallas kernels: none -> 70.5 us  [hidden_call(): pl.pallas_call(functools.partial(hidden_kernel, backward, forward), grid=...]
    ppermute x12, waiting for transfers between devices: 30.5 us -> 45 us  [send(): return lax.ppermute(value, AXES, pairs)]
    pallas_call x1, Pallas kernels: 111 us -> 120 us  [backward_call(): pl.pallas_call(backward_kernel, in_specs=[in_vmem] * 6 + [anywhere] * 2,...]
    unnamed x85 -> x37, local copies, waits for them, and re-layouts: 25.2 us -> 16.5 us
  transfers between devices with their start and end apart: 12 -> 12, of which waited for: 1 -> 7; matrix products, arithmetic and copies ran while one was open for 6% -> 0% of each run, Pallas kernels for 17% -> 37%
where the time goes in v3:
time: 757 us; the launch traced here: 745 us
  Pallas kernels  673 us (89%)
  waiting for transfers between devices  45 us (6%)
  local copies, waits for them, and re-layouts  20.1 us (3%)
    pallas_call x1, Pallas kernels, last_call(): pl.pallas_call(last_kernel, in_specs=[in_vmem] * 6 + [anywhere] * 22, out...  279 us
    pallas_call x1, Pallas kernels, first_call(): pl.pallas_call(first_kernel, in_specs=[in_vmem, anywhere] + [in_vmem] * 7...  122 us
    pallas_call x1, Pallas kernels, backward_call(): pl.pallas_call(backward_kernel, in_specs=[in_vmem] * 6 + [anywhere] * 2,...  120 us
    pallas_call x3, Pallas kernels, hidden_call(): pl.pallas_call(functools.partial(hidden_kernel, backward, forward), grid=...  70.5 us
    pallas_call x1, Pallas kernels, forward_call(): pl.pallas_call(forward_kernel, in_specs=[in_vmem, in_vmem, anywhere, anyw...  63.6 us
    ppermute x12, waiting for transfers between devices, send(): return lax.ppermute(value, AXES, pairs)  45 us
    pallas_call x1, Pallas kernels, grad_products(): pl.pallas_call(functools.partial(grad_kernel, by_left), grid_spec=pltpu.P...  18.1 us
    unnamed x37, local copies, waits for them, and re-layouts  16.5 us
  transfers between devices with their start and end apart: 12, of which 7 were waited for; matrix products, arithmetic and copies ran while one was open for 0% of the time, Pallas kernels for 37%

profile of v3, /device:TPU:17, one launch (start us, length us, event | category | flops | bytes accessed | tf_op | source)
XLA Modules:
  0.0 745.5 jit_solution(4580338233790648790)
XLA Ops:
  0.6 1.4 fusion.1
  2.0 121.5 %first.1 = (bf16[512,1024]{1,0:T(8,128)(2,1)}, f32[4,2048]{1,0:T(4,128)}, bf16[2048,1024]{1,0:T(8,128)(2,1)}, bf16[512,1024]{1,0:T(8,128)(2,1)}, bf16[4,256,1024...) custom-call(bf16[2048,1024]{1,0:T(8,128)(2,1)} %bitcast.12, ...), custom_call_target="tpu_custom_call" | custom-call | flops 34359738368 | bytes 134217728 | tf_op jit(solution)/shard_map/first/pallas_call | solution.py:328
  123.5 0.6 collective-permute-start.2
  124.1 0.6 convert_element_type.3.emb_ref
  124.7 2.3 constant_dynamic-slice_fusion.refs_1_.x_ref
  127.0 20.6 %hidden.3 = (bf16[512,1024]{1,0:T(8,128)(2,1)}, bf16[512,1024]{1,0:T(8,128)(2,1)}, bf16[512,4096]{1,0:T(8,128)(2,1)}, bf16[512,4096]{1,0:T(8,128)(2,1)}, bf16[512,1024]{1,0:T(8,128)(2,1)}) custom-call(bf16[512,1024]{1,0:T(8,128)(2,1)} %get-tuple-element.49.refs_0_.refs_14_, bf16[512,1024]{1,0:T(8,128)(2,1)} %constant_dynamic-slice_fusion.refs_1_.x_ref, ...), custom_call_target="tpu_custom_call" | custom-call | flops 10737418240 | bytes 33554432 | tf_op jit(solution)/shard_map/hidden/pallas_call | solution.py:818
  147.5 63.6 %forward.1 = (bf16[512,1024]{1,0:T(8,128)(2,1)}, f32[4,2048]{1,0:T(4,128)}, bf16[2048,1024]{1,0:T(8,128)(2,1)}, bf16[2048,768]{1,0:T(8,128)(2,1)}, bf16[2048,102...) custom-call(bf16[512,1024]{1,0:T(8,128)(2,1)} %get-tuple-element.54.x_ref.refs_1_, f32[2,1024]{1,0:T(2,128)} %convert_element_type.3.emb_ref, ...), custom_call_target="tpu_custom_call" | custom-call | flops 34359738368 | bytes 67108864 | tf_op jit(solution)/shard_map/forward/pallas_call | solution.py:486
  211.2 29.0 %hidden.4 = (bf16[512,1024]{1,0:T(8,128)(2,1)}, bf16[512,1024]{1,0:T(8,128)(2,1)}, bf16[512,4096]{1,0:T(8,128)(2,1)}, bf16[512,4096]{1,0:T(8,128)(2,1)}, bf16[51...) custom-call(bf16[512,1024]{1,0:T(8,128)(2,1)} %get-tuple-element.60.refs_0_.refs_12_, ...), custom_call_target="tpu_custom_call" | custom-call | flops 15032385536 | bytes 33554432 | tf_op jit(solution)/shard_map/hidden/pallas_call | solution.py:818
  240.3 0.4 collective-permute-start.1
  240.8 120.3 %backward.1 = (bf16[512,1024]{1,0:T(8,128)(2,1)}, bf16[512,1024]{1,0:T(8,128)(2,1)}, f32[1024,768]{1,0:T(8,128)}) custom-call(bf16[2048,768]{1,0:T(8,128)(2,1)} %get-tuple-element.59.qkv_ref, bf16[512,1024]{1,0:T(8,128)(2,1)} %get-tuple-element.62.dc_ref, f32[4,2048]{1,0:T(4,128)} %get-tuple-element.63.lse_ref, ...), custom_call_target="tpu_custom_call" | custom-call | flops 85899345920 | bytes 134217728 | tf_op jit(solution)/shard_map/backward/pallas_call | solution.py:660
  361.2 0.6 fusion._
  361.9 18.1 %grad.1 = (f32[4,256,1024]{2,1,0:T(8,128)}, f32[4,128,1024]{2,1,0:T(8,128)}, f32[4,128,1024]{2,1,0:T(8,128)}) custom-call(s32[4]{0:T(128)} %fusion._, bf16[512,4096]{1,0:T(8,128)(2,1)} %get-tuple-element.67.refs_0_.refs_1_.refs_2_.refs_3_, bf16[512,4096]{1,0:T(8,128)(2,1)} %get-tuple-element.67.refs_0_.refs_1_.refs_2_.refs_3_, ...), custom_call_target="tpu_custom_call" | custom-call | flops 8589934592 | bytes 27262976 | tf_op jit(solution)/shard_map/grad/pallas_call | solution.py:866
  380.1 21.0 %hidden.5 = (bf16[512,4096]{1,0:T(8,128)(2,1)}, bf16[512,1024]{1,0:T(8,128)(2,1)}, bf16[512,1024]{1,0:T(8,128)(2,1)}) custom-call(bf16[512,1024]{1,0:T(8,128)(2,1)} %get-tuple-element.57.refs_0_, bf16[1024,1024]{1,0:T(8,128)(2,1)} %bitcast.19, bf16[512,4096]{1,0:T(8,128)(2,1)} %get-tuple-element.58.refs_2_, bf16[4096,1024]{1,0:T(8,128)(2,1)} %bitcast.16, ...), custom_call_target="tpu_custom_call" | custom-call | flops 10737418240 | bytes 33554432 | tf_op jit(solution)/shard_map/hidden/pallas_call | solution.py:818
  401.4 0.9 collective-permute-start.3
  402.8 7.1 collective-permute-done.4.refs_1_
  410.3 1.1 collective-permute-done.8.refs_9_
  411.8 1.1 collective-permute-done.10.refs_13_
  412.9 0.4 collective-permute-start.11
  413.3 1.1 collective-permute-done.5.refs_3_
  414.8 1.1 collective-permute-done.11.refs_15_
  415.9 1.5 collective-permute-done.9.refs_11_
  417.4 31.9 %collective-permute-done.3.r2_ref = f32[4,256,1024]{2,1,0:T(8,128)} collective-permute-done((f32[4,256,1024]{2,1,0:T(8,128)}, f32[4,256,1024]{2,1,0:T(8,128)}, u32[]{:S(2)}, u32[]{:S(2)}) %collective-permute-start.3) | collective-permute-done | bytes 4194336 | tf_op jit(solution)/shard_map/ppermute | solution.py:1384
  449.4 279.2 %last.1 = (bf16[2048,1024]{1,0:T(8,128)(2,1)}, f32[1024,1024]{1,0:T(8,128)}, f32[1024,1024]{1,0:T(8,128)}, f32[1024,256]{1,0:T(8,128)}, f32[1024,256]{1,0:T(8,12...) custom-call(bf16[2048,768]{1,0:T(8,128)(2,1)} %get-tuple-element.56., ...), custom_call_target="tpu_custom_call" | custom-call | flops 85899345920 | bytes 268435456 | tf_op jit(solution)/shard_map/last/pallas_call | solution.py:1318
  728.6 2.7 copy.16
  731.3 2.4 copy.23
  733.7 1.0 copy.24
  734.7 1.0 copy.25
  735.7 2.1 copy.26
  737.8 1.6 copy-done.1
  739.4 2.1 copy.27
  741.5 1.6 copy-done
  743.1 2.0 copy.28
  (41 shorter events, 2.3 us)
Async XLA Ops:
  2.0 122.1 %copy-start.5 = (bf16[2,1024]{1,0:T(2,128)(2,1)S(1)}, bf16[2,1024]{1,0:T(2,128)(2,1)}, u32[]{:S(2)}) copy-start(bf16[2,1024]{1,0:T(2,128)(2,1)} %param.11) | copy-start | bytes 12292
  123.5 238.3 %collective-permute-start.2 = (bf16[512,1024]{1,0:T(8,128)(2,1)}, bf16[512,1024]{1,0:T(8,128)(2,1)}, u32[]{:S(2)}, u32[]{:S(2)}) collective-permute-start(bf16[512,1024]{1,0:T(8,128)(2,1)} %get-tuple-element.61.refs_6_.refs_16_), channel_id=1, source_target_pairs={{0,1},{1,0},{2,3},{3,2},{4,5},{5,4},{6,7},{7,6},{8,9},{9,8},{10,11... | collective-permute-start | bytes 3145736 | tf_op jit(solution)/shard_map/ppermute | solution.py:1384
  240.1 121.7 %collective-permute-start = (bf16[512,4096]{1,0:T(8,128)(2,1)}, bf16[512,4096]{1,0:T(8,128)(2,1)}, u32[]{:S(2)}, u32[]{:S(2)}) collective-permute-start(bf16[512,4096]{1,0:T(8,128)(2,1)} %get-tuple-element.67.refs_0_.refs_1_.refs_2_.refs_3_), channel_id=1, source_target_pairs={{0,1},{1,0},{2,3},{3,2},{4,5},{5,4},{6,7},{7,6},{8,9},{9,8},{10,11... | collective-permute-start | bytes 12582920 | tf_op jit(solution)/shard_map/ppermute | solution.py:1384
  240.3 121.6 %collective-permute-start.1 = (bf16[512,4096]{1,0:T(8,128)(2,1)}, bf16[512,4096]{1,0:T(8,128)(2,1)}, u32[]{:S(2)}, u32[]{:S(2)}) collective-permute-start(bf16[512,4096]{1,0:T(8,128)(2,1)} %get-tuple-element.68.refs_8_.refs_9_.refs_10_.refs_11_), channel_id=1, source_target_pairs={{0,1},{1,0},{2,3},{3,2},{4,5},{5,4},{6,7},{7,6},{8,9},{9,8},{10,11... | collective-permute-start | bytes 12582920 | tf_op jit(solution)/shard_map/ppermute | solution.py:1384
  240.7 175.2 %collective-permute-start.6 = (bf16[512,4096]{1,0:T(8,128)(2,1)}, bf16[512,4096]{1,0:T(8,128)(2,1)}, u32[]{:S(2)}, u32[]{:S(2)}) collective-permute-start(bf16[512,4096]{1,0:T(8,128)(2,1)} %get-tuple-element.82.refs_4_), channel_id=1, source_target_pairs={{0,1},{1,0},{2,3},{3,2},{4,5},{5,4},{6,7},{7,6},{8,9},{9,8},{10,11... | collective-permute-start | bytes 12582920 | tf_op jit(solution)/shard_map/ppermute | solution.py:1384
  380.0 29.9 %copy-start.8 = (bf16[512,1024]{1,0:T(8,128)(2,1)S(1)}, bf16[512,1024]{1,0:T(8,128)(2,1)}, u32[]{:S(2)}) copy-start(bf16[512,1024]{1,0:T(8,128)(2,1)} %get-tuple-element.60.refs_0_.refs_12_) | copy-start | bytes 3145732
  380.0 31.4 %copy-start.7 = (bf16[512,1024]{1,0:T(8,128)(2,1)S(1)}, bf16[512,1024]{1,0:T(8,128)(2,1)}, u32[]{:S(2)}) copy-start(bf16[512,1024]{1,0:T(8,128)(2,1)} %get-tuple-element.81.refs_2_) | copy-start | bytes 3145732
  380.0 32.9 %copy-start.6 = (bf16[512,1024]{1,0:T(8,128)(2,1)S(1)}, bf16[512,1024]{1,0:T(8,128)(2,1)}, u32[]{:S(2)}) copy-start(bf16[512,1024]{1,0:T(8,128)(2,1)} %get-tuple-element.49.refs_0_.refs_14_) | copy-start | bytes 3145732
  401.0 16.4 %collective-permute-start.7 = (bf16[512,4096]{1,0:T(8,128)(2,1)}, bf16[512,4096]{1,0:T(8,128)(2,1)}, u32[]{:S(2)}, u32[]{:S(2)}) collective-permute-start(bf16[512,4096]{1,0:T(8,128)(2,1)} %get-tuple-element.83.refs_6_), channel_id=1, source_target_pairs={{0,1},{1,0},{2,3},{3,2},{4,5},{5,4},{6,7},{7,6},{8,9},{9,8},{10,11... | collective-permute-start | bytes 12582920 | tf_op jit(solution)/shard_map/ppermute | solution.py:1384
  401.4 48.0 %collective-permute-start.3 = (f32[4,256,1024]{2,1,0:T(8,128)}, f32[4,256,1024]{2,1,0:T(8,128)}, u32[]{:S(2)}, u32[]{:S(2)}) collective-permute-start(f32[4,256,1024]{2,1,0:T(8,128)} %get-tuple-element.77), channel_id=1, source_target_pairs={{0,2},{1,5},{2,0},{3,7},{4,6},{5,1},{6,4},{7,3},{8,10},{9,13},{10,... | collective-permute-start | bytes 12582920 | tf_op jit(solution)/shard_map/ppermute | solution.py:1384
  402.3 7.6 %collective-permute-start.4 = (bf16[512,1024]{1,0:T(8,128)(2,1)}, bf16[512,1024]{1,0:T(8,128)(2,1)S(1)}, u32[]{:S(2)}, u32[]{:S(2)}) collective-permute-start(bf16[512,1024]{1,0:T(8,128)(2,1)} %get-tuple-element.80.refs_0_), channel_id=1, source_target_pairs={{0,1},{1,0},{2,3},{3,2},{4,5},{5,4},{6,7},{7,6},{8,9},{9,8},{10,11... | collective-permute-start | bytes 3145736 | tf_op jit(solution)/shard_map/ppermute | solution.py:1384
  402.6 8.8 %collective-permute-start.8 = (bf16[512,1024]{1,0:T(8,128)(2,1)}, bf16[512,1024]{1,0:T(8,128)(2,1)S(1)}, u32[]{:S(2)}, u32[]{:S(2)}) collective-permute-start(bf16[512,1024]{1,0:T(8,128)(2,1)} %get-tuple-element.64.dmid_ref.refs_8_), channel_id=1, source_target_pairs={{0,1},{1,0},{2,3},{3,2},{4,5},{5,4},{6,7},{7,6},{8,9},{9,8},{10,11... | collective-permute-start | bytes 3145736 | tf_op jit(solution)/shard_map/ppermute | solution.py:1384
  409.9 6.0 copy-start.9
  409.9 3.0 collective-permute-start.10
  411.4 4.5 copy-start.10
  411.4 3.0 collective-permute-start.5
  412.9 4.5 copy-start.11
  412.9 3.0 collective-permute-start.11
  414.4 3.0 copy-start.12
  414.4 3.0 collective-permute-start.9
  415.9 33.5 %copy-start.13 = (bf16[512,1024]{1,0:T(8,128)(2,1)}, bf16[512,1024]{1,0:T(8,128)(2,1)S(1)}, u32[]{:S(2)}) copy-start(bf16[512,1024]{1,0:T(8,128)(2,1)S(1)} %collective-permute-done.11.refs_15_) | copy-start | bytes 3145732
  417.4 32.0 %copy-start.14 = (bf16[512,1024]{1,0:T(8,128)(2,1)}, bf16[512,1024]{1,0:T(8,128)(2,1)S(1)}, u32[]{:S(2)}) copy-start(bf16[512,1024]{1,0:T(8,128)(2,1)S(1)} %collective-permute-done.9.refs_11_) | copy-start | bytes 3145732
  728.6 5.1 copy-start.4
  728.6 6.1 copy-start.3
  731.3 4.4 copy-start.2
  735.7 3.7 copy-start.1
  739.4 3.7 copy-start
